TPU v7x, 32 devices: a whole 2x2x4 slice. The times are simulated.
32 devices in a mesh: groups: 2 (over y), blk: 16 (over z, x, core).
Axes of the slice: x: 2, y: 2, z: 4, core: 2. Of those that a mesh axis runs over, the one named last changes fastest.
Arguments:
- queries: bfloat16 [2048, 2048], P(('groups', 'blk')), parts along dimension 0, may hold values from -48 to 48
- rotated_cache_keys: bfloat16 [16384, 256], P(('groups', 'blk')), parts along dimension 0, may hold values from -4 to 4
- stored_cache_values: bfloat16 [16384, 256], P(('groups', 'blk')), parts along dimension 0, may hold values from -5 to 5
- segment_new_keys: bfloat16 [2048, 256], P(('groups', 'blk')), parts along dimension 0, may hold values from -4 to 4
- segment_new_values: bfloat16 [2048, 256], P(('groups', 'blk')), parts along dimension 0, may hold values from -5 to 5
- block_ids: int32 [2048, 8], P(('groups', 'blk')), parts along dimension 0, may hold values from 0 to 15, all different within a row; in each aligned block of 64 rows (0 to 63, 64 to 127, ...) at most 40 rows name the same one
- residual_in: bfloat16 [2048, 1024], P(('groups', 'blk')), parts along dimension 0, may hold values from -3 to 3
- out_weight: bfloat16 [2048, 1024], replicated, may hold values from -1.5 to 1.5
- norm_gain: float32 [1024], replicated, may hold values from 0.25 to 1.75
- expert_ids: int32 [2048, 8], P(('groups', 'blk')), parts along dimension 0, may hold values from 0 to 15, all different within a row; in each aligned block of 64 rows (0 to 63, 64 to 127, ...) at most 48 rows name the same one
- gate_scores: float32 [2048, 8], P(('groups', 'blk')), parts along dimension 0, may hold values from 0.05 to 1
- w_gate: bfloat16 [16, 1024, 768], P('blk'), may hold values from -0.1875 to 0.1875
- w_up: bfloat16 [16, 1024, 768], P('blk'), may hold values from -0.1875 to 0.1875
- w_down: bfloat16 [16, 768, 1024], P('blk'), may hold values from -0.21875 to 0.21875
Outputs:
- layer_out: bfloat16 [2048, 1024], P(('groups', 'blk')), parts along dimension 0
There are 2 independent parts, one for each index of `groups`. A program takes and returns all parts, laid end to end along the dimension named above; an argument that names none is the same for every part. Nothing has to cross between parts.
Inputs may be any that keep to these rules, and one draw needn't show every extreme that they name: `block_ids`: each row names 8 different blocks. Among the rows of one device no block is named more than 40 times, and in some devices' rows some block is named exactly 40 times. `expert_ids`: each row names 8 different experts. Among the rows of one device no expert is named more than 48 times, and in some devices' rows some expert is named exactly 48 times.
All inputs are finite; a program needn't handle non-finite values.
Results may differ from a plain program's by a relative error of at most 0.0095.
Values may be sent and summed in bfloat16 or wider, within the bound.
No kernel may reach another device: no remote copies, remote signals or barrier semaphores. Data moves between devices by JAX's collectives and lax.ppermute only.
A program may use at most 128 MiB of HBM per device.

v0:
```python
import jax
import jax.numpy as jnp
from jax import lax
from jax.sharding import PartitionSpec as P

QUERY_HEADS = 16
KEY_VALUE_HEADS = 2
HEAD_SIZE = 128
TOPB = 8
TOPE = 8


NORM_EPSILON = 1e-06


def partials(query_rows, key_rows, value_rows, causal):
    queries_per_cluster = QUERY_HEADS // KEY_VALUE_HEADS
    score_scale = HEAD_SIZE ** (-0.5)
    maxima = []
    totals = []
    outputs = []
    for head_cluster in range(KEY_VALUE_HEADS):
        offset = head_cluster * queries_per_cluster * HEAD_SIZE
        group_queries = query_rows[:, offset : offset + queries_per_cluster * HEAD_SIZE].reshape(
            -1, HEAD_SIZE
        )
        group_keys = key_rows[:, head_cluster * HEAD_SIZE : (head_cluster + 1) * HEAD_SIZE]
        group_values = value_rows[:, head_cluster * HEAD_SIZE : (head_cluster + 1) * HEAD_SIZE]
        scores = (
            lax.dot_general(
                group_queries,
                group_keys,
                (((1,), (1,)), ((), ())),
                preferred_element_type=jnp.float32,
            )
            * score_scale
        )
        if causal:
            owner_row = jnp.arange(group_queries.shape[0], dtype=jnp.int32) // queries_per_cluster
            key_place = jnp.arange(key_rows.shape[0], dtype=jnp.int32)
            scores = jnp.where(key_place[None, :] <= owner_row[:, None], scores, -jnp.inf)
        row_max = jnp.max(scores, axis=1)
        weights = jnp.exp(scores - row_max[:, None])
        maxima.append(row_max.reshape(-1, queries_per_cluster))
        totals.append(jnp.sum(weights, axis=1).reshape(-1, queries_per_cluster))
        mixed_rows = jnp.dot(
            weights.astype(jnp.bfloat16), group_values, preferred_element_type=jnp.float32
        )
        outputs.append(mixed_rows.reshape(-1, queries_per_cluster * HEAD_SIZE))
    return (
        jnp.concatenate(maxima, axis=1),
        jnp.concatenate(totals, axis=1),
        jnp.concatenate(outputs, axis=1),
    )


def bucket_slots(targets, capacity, parties):
    flat_targets = targets.reshape(-1)
    pair_count = flat_targets.shape[0]
    one_hot = (flat_targets[:, None] == jnp.arange(parties, dtype=jnp.int32)[None, :]).astype(
        jnp.int32
    )
    before = jnp.sum((jnp.cumsum(one_hot, axis=0) - one_hot) * one_hot, axis=1)
    slot_index = flat_targets * capacity + before
    filler = (
        jnp.full((parties * capacity,), pair_count, jnp.int32)
        .at[slot_index]
        .set(jnp.arange(pair_count, dtype=jnp.int32))
    )
    return (slot_index, filler)


def body(
    queries,
    rotated_cache_keys,
    stored_cache_values,
    segment_new_keys,
    segment_new_values,
    block_ids,
    residual_in,
    out_weight,
    norm_gain,
    expert_ids,
    gate_scores,
    w_gate,
    w_up,
    w_down,
):
    parties = lax.axis_size("blk")
    tok_count = queries.shape[0]
    capacity = tok_count * TOPB * 5 // (4 * parties)
    expert_capacity = tok_count * TOPE * 3 // (2 * parties)
    owner_slots, slot_pair = bucket_slots(block_ids, capacity, parties)
    pair_count = tok_count * TOPB
    occupied = slot_pair < pair_count
    source_token = jnp.minimum(slot_pair, pair_count - 1) // TOPB
    outgoing = jnp.where(
        occupied[:, None], queries[source_token], jnp.zeros((), queries.dtype)
    ).reshape(parties, capacity, QUERY_HEADS * HEAD_SIZE)
    arrived = lax.all_to_all(outgoing, "blk", split_axis=0, concat_axis=0, tiled=True)
    senders, items, row_width = arrived.shape
    far_max, far_total, far_out = partials(
        arrived.reshape(senders * items, row_width), rotated_cache_keys, stored_cache_values, False
    )
    back_max = lax.all_to_all(
        far_max.reshape(senders, items, QUERY_HEADS), "blk", split_axis=0, concat_axis=0, tiled=True
    )
    back_total = lax.all_to_all(
        far_total.reshape(senders, items, QUERY_HEADS),
        "blk",
        split_axis=0,
        concat_axis=0,
        tiled=True,
    )
    back_out = lax.all_to_all(
        far_out.astype(jnp.bfloat16).reshape(senders, items, row_width),
        "blk",
        split_axis=0,
        concat_axis=0,
        tiled=True,
    )
    local_row_maximum, local_denominator, local_output = partials(
        queries, segment_new_keys, segment_new_values, True
    )
    pair_max = back_max.reshape(-1, QUERY_HEADS)[owner_slots].reshape(tok_count, TOPB, QUERY_HEADS)
    pair_total = back_total.reshape(-1, QUERY_HEADS)[owner_slots].reshape(
        tok_count, TOPB, QUERY_HEADS
    )
    pair_out = back_out.reshape(-1, QUERY_HEADS * HEAD_SIZE)[owner_slots].reshape(
        tok_count, TOPB, QUERY_HEADS, HEAD_SIZE
    )
    ceiling = jnp.maximum(local_row_maximum, jnp.max(pair_max, axis=1))
    own_scale = jnp.exp(local_row_maximum - ceiling)
    pair_scale = jnp.exp(pair_max - ceiling[:, None, :])
    denominator = local_denominator * own_scale + jnp.sum(pair_total * pair_scale, axis=1)
    numerator = local_output.reshape(tok_count, QUERY_HEADS, HEAD_SIZE) * own_scale[
        :, :, None
    ] + jnp.einsum("tjh,tjhd->thd", pair_scale, pair_out, preferred_element_type=jnp.float32)
    attention = (
        (numerator / denominator[:, :, None])
        .reshape(tok_count, QUERY_HEADS * HEAD_SIZE)
        .astype(jnp.bfloat16)
    )
    hidden_state = residual_in.astype(jnp.float32) + jnp.dot(
        attention, out_weight, preferred_element_type=jnp.float32
    )
    normed = (
        hidden_state
        * lax.rsqrt(jnp.mean(hidden_state * hidden_state, axis=-1, keepdims=True) + NORM_EPSILON)
        * norm_gain
    ).astype(jnp.bfloat16)
    expert_slots, expert_pair = bucket_slots(expert_ids, expert_capacity, parties)
    expert_pairs = tok_count * TOPE
    expert_used = expert_pair < expert_pairs
    expert_token = jnp.minimum(expert_pair, expert_pairs - 1) // TOPE
    dispatched = jnp.where(
        expert_used[:, None], normed[expert_token], jnp.zeros((), normed.dtype)
    ).reshape(parties, expert_capacity, normed.shape[1])
    arrived = lax.all_to_all(dispatched, "blk", split_axis=0, concat_axis=0, tiled=True)
    flat_rows = arrived.reshape(-1, arrived.shape[2])
    gate_part = jnp.dot(flat_rows, w_gate[0], preferred_element_type=jnp.float32)
    up_part = jnp.dot(flat_rows, w_up[0], preferred_element_type=jnp.float32)
    inner = (jax.nn.silu(gate_part) * up_part).astype(jnp.bfloat16)
    expert_out = (
        jnp.dot(inner, w_down[0], preferred_element_type=jnp.float32)
        .astype(jnp.bfloat16)
        .reshape(arrived.shape)
    )
    returned = lax.all_to_all(expert_out, "blk", split_axis=0, concat_axis=0, tiled=True)
    gathered_rows = returned.reshape(-1, normed.shape[1])[expert_slots].reshape(
        tok_count, TOPE, normed.shape[1]
    )
    mixing = gate_scores / jnp.sum(gate_scores, axis=1, keepdims=True)
    mixture = jnp.einsum("tk,tkd->td", mixing, gathered_rows, preferred_element_type=jnp.float32)
    return (hidden_state + mixture).astype(jnp.bfloat16)


def solution(mesh):
    placed = (
        P(("groups", "blk"), None),
        P(("groups", "blk"), None),
        P(("groups", "blk"), None),
        P(("groups", "blk"), None),
        P(("groups", "blk"), None),
        P(("groups", "blk"), None),
        P(("groups", "blk"), None),
        P(),
        P(),
        P(("groups", "blk"), None),
        P(("groups", "blk"), None),
        P("blk", None, None),
        P("blk", None, None),
        P("blk", None, None),
    )
    return jax.shard_map(
        body, mesh=mesh, in_specs=placed, out_specs=P(("groups", "blk"), None), check_vma=False
    )
```

profile of v0, /device:TPU:0, one launch (start us, length us, event | category | flops | bytes accessed | tf_op | source)
XLA Modules:
  0.0 308.2 jit_solution(5231597037997804013)
XLA Ops:
  0.0 0.8 broadcast_multiply_fusion.1
  0.8 0.8 copy.66
  2.0 1.2 reduce-window.14
  3.1 0.2 slice_reduce_fusion.1
  3.5 2.4 scatter_custom_fusion
  6.1 4.1 %gather_fusion = bf16[640,2048]{1,0:T(8,128)(2,1)} fusion(bf16[64,2048]{1,0:T(8,128)(2,1)S(1)} %copy-done.1, s32[1024]{0:T(1024)S(1)} %pad_clamp_fusion.3), kind=kCustom, calls=%fused_computation | custom fusion | bytes 5245440 | tf_op jit(solution)/shard_map/gather | solution.py:98
  10.2 2.0 broadcast_select_fusion
  12.2 65.6 %all_to_all.30 = bf16[16,40,2048]{2,1,0:T(8,128)(2,1)S(1)} all-to-all(bf16[16,40,2048]{2,1,0:T(8,128)(2,1)S(1)} %broadcast_select_fusion), channel_id=1, replica_groups=mesh['groups'=2,'blk'=16] {'blk'}, dimensions={0} | all-to-all | bytes 5242880 | tf_op jit(solution)/shard_map/all_to_all | solution.py:100
  77.8 1.3 fusion.73
  79.1 1.4 reshape.314
  80.5 2.4 reshape.315
  82.9 5.5 %multiply_reduce_fusion = (f32[5120]{0:T(1024)S(1)}, f32[5120,512]{0,1:T(8,128)}) fusion(bf16[5120,128]{1,0:T(8,128)(2,1)S(1)} %reshape.315, bf16[512,256]{1,0:T(8,128)(2,1)S(1)} %copy-done.11), kind=kOutput, calls=%fused_computation.10 | convolution fusion | flops 676326400 | bytes 11948032 | tf_op jit(solution)/shard_map/dot_general | solution.py:30
  88.6 5.9 %fusion.2 = f32[5120]{0:T(1024)S(1)} fusion(f32[5120,512]{0,1:T(8,128)} %get-tuple-element.12, f32[5120]{0:T(1024)S(1)} %get-tuple-element.11), kind=kLoop, calls=%fused_computation.14 | loop fusion | flops 7859200 | bytes 10526720 | tf_op jit(solution)/shard_map/reduce_sum | solution.py:45
  94.5 1.1 copy-done.2
  95.6 3.3 %convolution_convert_fusion = bf16[5120,128]{1,0:T(8,128)(2,1)S(1)} fusion(f32[5120,512]{0,1:T(8,128)S(1)} %copy-done.2, f32[5120]{0:T(1024)S(1)} %get-tuple-element.11, bf16[512,256]{1,0:T(8,128)(2,1)} %param.16), kind=kOutput, calls=%fused_computation.16 | convolution fusion | flops 679608320 | bytes 11948032 | tf_op jit(solution)/shard_map/dot_general | solution.py:46
  98.8 1.5 multiply_reduce_fusion.1
  100.4 2.3 fusion
  102.7 3.3 %convolution_convert_fusion.1 = bf16[5120,128]{1,0:T(8,128)(2,1)} fusion(f32[5120,512]{0,1:T(8,128)S(1)} %get-tuple-element.14, f32[5120]{0:T(1024)S(1)} %get-tuple-element.13, bf16[512,256]{1,0:T(8,128)(2,1)S(1)} %copy-done.13), kind=kOutput, calls=%fused_computation.17 | convolution fusion | flops 679608320 | bytes 11948032 | tf_op jit(solution)/shard_map/dot_general | solution.py:46
  106.1 0.9 concatenate.73
  107.0 1.4 concatenate.77
  108.4 0.8 copy.70
  109.5 3.4 %concatenate.76 = bf16[16,40,1024]{2,1,0:T(8,128)(2,1)} reshape(bf16[5120,128]{1,0:T(8,128)(2,1)} %convolution_convert_fusion.1) | data formatting | bytes 2621440 | tf_op jit(solution)/shard_map/concatenate | solution.py:53
  112.9 0.8 copy.69
  113.6 0.9 fusion.78
  114.5 0.8 reshape.403
  115.3 5.2 %all-to-all-start.1 = ((f32[16,1,640]{2,1,0:T(1,128)}), f32[16,1,640]{2,1,0:T(1,128)}, u32[]{:S(2)}, u32[]{:S(2)}) async-start(f32[16,1,640]{2,1,0:T(1,128)} %reshape.403), calls=%async_computation.1 | async-start | bytes 81920 | tf_op jit(solution)/shard_map/all_to_all | solution.py:105
  120.5 0.9 concatenate.82
  121.4 0.8 copy.72
  122.2 0.9 fusion.77
  123.1 0.8 reshape.405
  123.8 3.4 %all-to-all-done.1 = f32[16,1,640]{2,1,0:T(1,128)} async-done(((f32[16,1,640]{2,1,0:T(1,128)}), f32[16,1,640]{2,1,0:T(1,128)}, u32[]{:S(2)}, u32[]{:S(2)}) %all-to-all-start.1) | async-done | bytes 40992 | tf_op jit(solution)/shard_map/all_to_all | solution.py:105
  127.3 3.5 %all-to-all-start.3 = ((f32[16,1,640]{2,1,0:T(1,128)}), f32[16,1,640]{2,1,0:T(1,128)S(1)}, u32[]{:S(2)}, u32[]{:S(2)}) async-start(f32[16,1,640]{2,1,0:T(1,128)} %reshape.405), calls=%async_computation.3 | async-start | bytes 81920 | tf_op jit(solution)/shard_map/all_to_all | solution.py:108
  130.8 3.1 %pad_maximum_fusion = bf16[16,40,2048]{2,1,0:T(8,128)(2,1)} fusion(bf16[16,40,1024]{2,1,0:T(8,128)(2,1)S(1)} %copy-done.4, bf16[16,40,1024]{2,1,0:T(8,128)(2,1)} %concatenate.76), kind=kLoop, calls=%fused_computation.22 | loop fusion | flops 5242880 | bytes 5242880 | tf_op jit(solution)/shard_map/concatenate | solution.py:53
  133.9 3.6 %all-to-all-done.3 = f32[16,1,640]{2,1,0:T(1,128)S(1)} async-done(((f32[16,1,640]{2,1,0:T(1,128)}), f32[16,1,640]{2,1,0:T(1,128)S(1)}, u32[]{:S(2)}, u32[]{:S(2)}) %all-to-all-start.3) | async-done | bytes 40992 | tf_op jit(solution)/shard_map/all_to_all | solution.py:108
  137.4 4.4 %all-to-all-start.2 = ((bf16[16,40,2048]{2,1,0:T(8,128)(2,1)}), bf16[16,40,2048]{2,1,0:T(8,128)(2,1)}, u32[]{:S(2)}, u32[]{:S(2)}) async-start(bf16[16,40,2048]{2,1,0:T(8,128)(2,1)} %pad_maximum_fusion), calls=%async_computation.2 | async-start | bytes 5242880 | tf_op jit(solution)/shard_map/all_to_all | solution.py:115
  142.4 1.2 reduce-window.16
  143.5 0.2 slice_reduce_fusion
  143.9 2.4 scatter_custom_fusion.1
  146.9 0.7 concatenate.79
  148.0 0.7 concatenate.80
  148.8 0.2 convolution_bitcast_fusion.1
  149.0 0.2 convolution_bitcast_fusion
  149.3 0.6 broadcast.222
  149.8 1.6 reduce.4
  151.7 0.8 reduce.5
  152.8 1.0 gather_fusion.1
  153.8 1.0 gather_fusion.3
  155.1 0.4 copy.79
  155.6 0.9 fusion.51
  156.5 35.5 %all-to-all-done.2 = bf16[16,40,2048]{2,1,0:T(8,128)(2,1)} async-done(((bf16[16,40,2048]{2,1,0:T(8,128)(2,1)}), bf16[16,40,2048]{2,1,0:T(8,128)(2,1)}, u32[]{:S(2)}, u32[]{:S(2)}) %all-to-all-start.2) | async-done | bytes 2621472 | tf_op jit(solution)/shard_map/all_to_all | solution.py:115
  192.0 7.3 %gather_fusion.2 = bf16[512,2048]{1,0:T(8,128)(2,1)} fusion(bf16[640,2048]{1,0:T(8,128)(2,1)} %bitcast.10, s32[1024]{0:T(1024)S(1)} %pad_clamp_fusion.2), kind=kCustom, calls=%fused_computation.2 | custom fusion | bytes 4196352 | tf_op jit(solution)/shard_map/gather | solution.py:129
  199.3 3.0 fusion.10
  202.2 0.3 fusion.24
  202.6 0.9 multiply_reduce_fusion.2
  203.6 0.7 copy-done.6
  204.4 2.8 gather_fusion.4
  207.4 49.1 %all_to_all.31 = bf16[16,48,1024]{2,1,0:T(8,128)(2,1)S(1)} all-to-all(bf16[16,48,1024]{2,1,0:T(8,128)(2,1)S(1)} %broadcast_select_fusion.1), channel_id=1, replica_groups=mesh['groups'=2,'blk'=16] {'blk'}, dimensions={0} | all-to-all | bytes 3145728 | tf_op jit(solution)/shard_map/all_to_all | solution.py:159
  256.6 2.8 fusion.14
  259.4 6.6 %convolution_convert_fusion.2 = bf16[768,1024]{1,0:T(8,128)(2,1)} fusion(bf16[1,768,1024]{2,1,0:T(8,128)(2,1)S(1)} %copy-done, f32[768,768]{1,0:T(8,128)} %fusion.14, bf16[768,1024]{1,0:T(8,128)(2,1)S(1)} %bitcast.126, bf16[1,1024,768]{2,1,0:T(8,128)(2,1)} %param.26), kind=kOutput, calls=%fused_computation.27 | convolution fusion | flops 2420244480 | bytes 8650752 | tf_op jit(solution)/shard_map/dot_general | solution.py:165
  266.0 5.2 %all-to-all-start.5 = ((bf16[16,48,1024]{2,1,0:T(8,128)(2,1)}), bf16[16,48,1024]{2,1,0:T(8,128)(2,1)S(1)}, u32[]{:S(2)}, u32[]{:S(2)}) async-start(bf16[16,48,1024]{2,1,0:T(8,128)(2,1)} %bitcast.124), calls=%async_computation.5 | async-start | bytes 3145728 | tf_op jit(solution)/shard_map/all_to_all | solution.py:169
  271.4 31.7 %all-to-all-done.5 = bf16[16,48,1024]{2,1,0:T(8,128)(2,1)S(1)} async-done(((bf16[16,48,1024]{2,1,0:T(8,128)(2,1)}), bf16[16,48,1024]{2,1,0:T(8,128)(2,1)S(1)}, u32[]{:S(2)}, u32[]{:S(2)}) %all-to-all-start.5) | async-done | bytes 1572896 | tf_op jit(solution)/shard_map/all_to_all | solution.py:169
  303.1 2.8 gather_fusion.5
  305.8 1.6 fusion.20
  307.5 0.7 fusion.27
  (99 shorter events, 4.0 us)
Async XLA Ops:
  0.0 259.4 %copy-start = (bf16[1,768,1024]{2,1,0:T(8,128)(2,1)S(1)}, bf16[1,768,1024]{2,1,0:T(8,128)(2,1)}, u32[]{:S(2)}) copy-start(bf16[1,768,1024]{2,1,0:T(8,128)(2,1)} %param.27) | copy-start | bytes 4718596
  0.0 6.1 %copy-start.1 = (bf16[64,2048]{1,0:T(8,128)(2,1)S(1)}, bf16[64,2048]{1,0:T(8,128)(2,1)}, u32[]{:S(2)}) copy-start(bf16[64,2048]{1,0:T(8,128)(2,1)} %param.14) | copy-start | bytes 786436
  79.1 3.8 %copy-start.11 = (bf16[512,256]{1,0:T(8,128)(2,1)S(1)}, bf16[512,256]{1,0:T(8,128)(2,1)}, u32[]{:S(2)}) copy-start(bf16[512,256]{1,0:T(8,128)(2,1)} %param.15) | copy-start | bytes 786436
  88.6 7.0 %copy-start.2 = (f32[5120,512]{0,1:T(8,128)S(1)}, f32[5120,512]{0,1:T(8,128)}, u32[]{:S(2)}) copy-start(f32[5120,512]{0,1:T(8,128)} %get-tuple-element.12) | copy-start | bytes 31457284
  95.5 3.3 %copy-start.3 = (bf16[5120,128]{1,0:T(8,128)(2,1)S(1)}, bf16[5120,128]{1,0:T(8,128)(2,1)}, u32[]{:S(2)}) copy-start(bf16[5120,128]{1,0:T(8,128)(2,1)} %reshape.314) | copy-start | bytes 3932164
  95.6 3.3 %copy-start.12 = (bf16[512,256]{1,0:T(8,128)(2,1)S(1)}, bf16[512,256]{1,0:T(8,128)(2,1)}, u32[]{:S(2)}) copy-start(bf16[512,256]{1,0:T(8,128)(2,1)} %param.15) | copy-start | bytes 786436
  100.4 2.3 copy-start.13
  109.2 3.7 %copy-start.8 = (f32[16,40,8]{2,1,0:T(8,128)S(1)}, f32[16,40,8]{2,1,0:T(8,128)}, u32[]{:S(2)}) copy-start(f32[16,40,8]{2,1,0:T(8,128)} %concatenate.73) | copy-start | bytes 61444
  109.5 21.3 %copy-start.4 = (bf16[16,40,1024]{2,1,0:T(8,128)(2,1)S(1)}, bf16[16,40,1024]{2,1,0:T(8,128)(2,1)}, u32[]{:S(2)}) copy-start(bf16[16,40,1024]{2,1,0:T(8,128)(2,1)} %concatenate.77) | copy-start | bytes 3932164
  115.3 12.0 %all-to-all-start.1 = ((f32[16,1,640]{2,1,0:T(1,128)}), f32[16,1,640]{2,1,0:T(1,128)}, u32[]{:S(2)}, u32[]{:S(2)}) async-start(f32[16,1,640]{2,1,0:T(1,128)} %reshape.403), calls=%async_computation.1 | async-start | bytes 81920 | tf_op jit(solution)/shard_map/all_to_all | solution.py:105
  127.3 10.2 %all-to-all-start.3 = ((f32[16,1,640]{2,1,0:T(1,128)}), f32[16,1,640]{2,1,0:T(1,128)S(1)}, u32[]{:S(2)}, u32[]{:S(2)}) async-start(f32[16,1,640]{2,1,0:T(1,128)} %reshape.405), calls=%async_computation.3 | async-start | bytes 81920 | tf_op jit(solution)/shard_map/all_to_all | solution.py:108
  133.9 8.0 %copy-start.17 = (s32[64,8]{0,1:T(8,128)S(1)}, s32[64,8]{0,1:T(8,128)}, u32[]{:S(2)}) copy-start(s32[64,8]{0,1:T(8,128)} %param.23) | copy-start | bytes 6148
  133.9 12.7 %copy-start.15 = (bf16[64,256]{1,0:T(8,128)(2,1)S(1)}, bf16[64,256]{1,0:T(8,128)(2,1)}, u32[]{:S(2)}) copy-start(bf16[64,256]{1,0:T(8,128)(2,1)} %param.17) | copy-start | bytes 98308
  137.4 54.6 %all-to-all-start.2 = ((bf16[16,40,2048]{2,1,0:T(8,128)(2,1)}), bf16[16,40,2048]{2,1,0:T(8,128)(2,1)}, u32[]{:S(2)}, u32[]{:S(2)}) async-start(bf16[16,40,2048]{2,1,0:T(8,128)(2,1)} %pad_maximum_fusion), calls=%async_computation.2 | async-start | bytes 5242880 | tf_op jit(solution)/shard_map/all_to_all | solution.py:115
  141.9 6.9 %copy-start.16 = (bf16[64,256]{1,0:T(8,128)(2,1)S(1)}, bf16[64,256]{1,0:T(8,128)(2,1)}, u32[]{:S(2)}) copy-start(bf16[64,256]{1,0:T(8,128)(2,1)} %param.18) | copy-start | bytes 98308
  146.9 8.1 %copy-start.9 = (f32[64,8]{1,0:T(8,128)}, f32[64,8]{1,0:T(8,128)S(1)}, u32[]{:S(2)}) copy-start(f32[64,8]{1,0:T(8,128)S(1)} %concatenate.70) | copy-start | bytes 6148
  148.0 7.0 %copy-start.10 = (f32[64,8]{1,0:T(8,128)}, f32[64,8]{1,0:T(8,128)S(1)}, u32[]{:S(2)}) copy-start(f32[64,8]{1,0:T(8,128)S(1)} %concatenate.71) | copy-start | bytes 6148
  199.3 3.3 %copy-start.5 = (bf16[2048,1024]{1,0:T(8,128)(2,1)S(1)}, bf16[2048,1024]{1,0:T(8,128)(2,1)}, u32[]{:S(2)}) copy-start(bf16[2048,1024]{1,0:T(8,128)(2,1)} %param.21) | copy-start | bytes 12582916
  199.3 3.3 %copy-start.14 = (bf16[64,1024]{1,0:T(8,128)(2,1)S(1)}, bf16[64,1024]{1,0:T(8,128)(2,1)}, u32[]{:S(2)}) copy-start(bf16[64,1024]{1,0:T(8,128)(2,1)} %param.20) | copy-start | bytes 393220
  202.6 1.7 copy-start.19
  203.6 0.7 copy-start.6
  207.4 49.2 %copy-start.20 = (bf16[1,1024,768]{2,1,0:T(8,128)(2,1)S(1)}, bf16[1,1024,768]{2,1,0:T(8,128)(2,1)}, u32[]{:S(2)}) copy-start(bf16[1,1024,768]{2,1,0:T(8,128)(2,1)} %param.25) | copy-start | bytes 4718596
  266.0 5.2 %copy-start.18 = (f32[64,8]{0,1:T(8,128)S(1)}, f32[64,8]{0,1:T(8,128)}, u32[]{:S(2)}) copy-start(f32[64,8]{0,1:T(8,128)} %param.24) | copy-start | bytes 6148
  266.0 37.0 %all-to-all-start.5 = ((bf16[16,48,1024]{2,1,0:T(8,128)(2,1)}), bf16[16,48,1024]{2,1,0:T(8,128)(2,1)S(1)}, u32[]{:S(2)}, u32[]{:S(2)}) async-start(bf16[16,48,1024]{2,1,0:T(8,128)(2,1)} %bitcast.124), calls=%async_computation.5 | async-start | bytes 3145728 | tf_op jit(solution)/shard_map/all_to_all | solution.py:169
  303.1 4.4 %copy-start.7 = (f32[64,1024]{1,0:T(8,128)S(1)}, f32[64,1024]{1,0:T(8,128)}, u32[]{:S(2)}) copy-start(f32[64,1024]{1,0:T(8,128)} %copy-done.6) | copy-start | bytes 786436
where the time goes:
time: 313 us; the launch traced here: 308 us
  blocking collectives  115 us (37%)
  waiting for transfers between devices  74.1 us (24%)
  local copies, waits for them, and re-layouts  47.4 us (15%)
  matrix products  29.4 us (9%)
  other arithmetic  23.5 us (8%)
  starting transfers between devices  18.4 us (6%)
    all_to_all x1, blocking collectives, body(): lax.all_to_all(outgoing, 'blk', split_axis=0, concat_axis=0, tiled=True)  65.6 us
    all_to_all x1, blocking collectives, body(): lax.all_to_all(dispatched, 'blk', split_axis=0, concat_axis=0, tiled=True)  49.1 us
    all_to_all x1, waiting for transfers between devices, body(): lax.all_to_all(far_out.astype(jnp.bfloat16).reshape(senders, items, row_w...  35.5 us
    all_to_all x1, waiting for transfers between devices, body(): lax.all_to_all(expert_out, 'blk', split_axis=0, concat_axis=0, tiled=True)  31.7 us
    reduce_sum x4, other arithmetic, partials(): totals.append(jnp.sum(weights, axis=1).reshape(-1, queries_per_cluster))  8.28 us
    dot_general x4, matrix products, partials(): lax.dot_general(group_queries, group_keys, (((1,), (1,)), ((), ())), pref...  7.43 us
    gather x1, local copies, waits for them, and re-layouts, body(): back_out.reshape(-1, QUERY_HEADS * HEAD_SIZE)[owner_slots]  7.29 us
    dot_general x4, matrix products, partials(): jnp.dot(weights.astype(jnp.bfloat16), group_values, preferred_element_typ...  7.03 us
  transfers between devices with their start and end apart: 4, of which 4 were waited for; matrix products, arithmetic and copies ran while one was open for 7% of the time, Pallas kernels for 0%

commit v1 on v0

--- a/solution.py
+++ b/solution.py
@@ -1,6 +1,8 @@
 import jax
 import jax.numpy as jnp
 from jax import lax
+from jax.experimental import pallas as pl
+from jax.experimental.pallas import tpu as pltpu
 from jax.sharding import PartitionSpec as P
 
 QUERY_HEADS = 16
@@ -70,7 +72,7 @@
     return (slot_index, filler)
 
 
-def body(
+def routed_body(
     queries,
     rotated_cache_keys,
     stored_cache_values,
@@ -175,6 +177,297 @@
     return (hidden_state + mixture).astype(jnp.bfloat16)
 
 
+CORES = 2
+LOG2_E = 1.4426950408889634
+UNSEEN = -1e20
+SKIPPED = 1e30
+LANES = 128
+
+
+def grid_of(parties):
+    chips = parties // CORES
+    across = round(chips ** (1 / 3))
+    while chips % across:
+        across -= 1
+    return (chips // across, across)
+
+
+def gathers(mesh):
+    return mesh.shape["blk"] <= 4 * TOPB and mesh.shape["blk"] % CORES == 0
+
+
+def shift_pairs(deep, across, step_deep, step_across, step_core):
+    return [
+        (
+            (z * across + x) * CORES + c,
+            ((z + step_deep) % deep * across + (x + step_across) % across) * CORES
+            + (c + step_core) % CORES,
+        )
+        for z in range(deep)
+        for x in range(across)
+        for c in range(CORES)
+    ]
+
+
+def own_kernel(q_ref, k_ref, v_ref, top_ref, total_ref, out_ref):
+    tokens = k_ref.shape[0]
+    heads_per_group = QUERY_HEADS // KEY_VALUE_HEADS
+    factor = HEAD_SIZE ** (-0.5) * LOG2_E
+    rows = lax.broadcasted_iota(jnp.int32, (tokens, tokens), 0)
+    keys = lax.broadcasted_iota(jnp.int32, (tokens, tokens), 1)
+    lane = lax.broadcasted_iota(jnp.int32, (tokens, LANES), 1)
+    top = jnp.full((tokens, LANES), UNSEEN, jnp.float32)
+    total = jnp.zeros((tokens, LANES), jnp.float32)
+    for head in range(QUERY_HEADS):
+        group = head // heads_per_group
+        at = slice(head * HEAD_SIZE, (head + 1) * HEAD_SIZE)
+        of = slice(group * HEAD_SIZE, (group + 1) * HEAD_SIZE)
+        scores = lax.dot_general(
+            q_ref[:tokens, at],
+            k_ref[:, of],
+            (((1,), (1,)), ((), ())),
+            preferred_element_type=jnp.float32,
+        )
+        scores = jnp.where(keys <= rows, scores * factor, -SKIPPED)
+        high = jnp.max(scores, axis=1, keepdims=True)
+        weights = jnp.exp2(scores - high)
+        top = jnp.where(lane == head, high, top)
+        total = jnp.where(lane == head, jnp.sum(weights, axis=1, keepdims=True), total)
+        out_ref[:tokens, at] = jnp.dot(
+            weights.astype(jnp.bfloat16), v_ref[:, of], preferred_element_type=jnp.float32
+        )
+    top_ref[:tokens, :] = top
+    total_ref[:tokens, :] = total
+    top_ref[tokens:, :] = jnp.full((tokens, LANES), UNSEEN, jnp.float32)
+    total_ref[tokens:, :] = jnp.zeros((tokens, LANES), jnp.float32)
+    out_ref[tokens:, :] = jnp.zeros((tokens, QUERY_HEADS * HEAD_SIZE), jnp.float32)
+
+
+def own_partial(queries, keys, values):
+    tokens = keys.shape[0]
+    return pl.pallas_call(
+        own_kernel,
+        out_shape=(
+            jax.ShapeDtypeStruct((2 * tokens, LANES), jnp.float32),
+            jax.ShapeDtypeStruct((2 * tokens, LANES), jnp.float32),
+            jax.ShapeDtypeStruct((2 * tokens, QUERY_HEADS * HEAD_SIZE), jnp.float32),
+        ),
+        name="own_partial",
+    )(queries, keys, values)
+
+
+def block_kernel(columns, group_list, count, *refs):
+    q_ref, chosen_ref, top_in, total_in, out_in = refs[:5]
+    block_refs = refs[5 : 5 + count]
+    top_ref, total_ref, out_ref = refs[5 + count :]
+    tokens = q_ref.shape[0]
+    heads_per_group = QUERY_HEADS // KEY_VALUE_HEADS
+    factor = HEAD_SIZE ** (-0.5) * LOG2_E
+    lane = lax.broadcasted_iota(jnp.int32, (tokens, LANES), 1)
+    top_ref[...] = top_in[...]
+    total_ref[...] = total_in[...]
+    fresh = set()
+    for column, group, block_ref in zip(columns, group_list, block_refs):
+        chosen = chosen_ref[:, column : column + 1] > 0.5
+        ones = jnp.ones((block_ref.shape[0], LANES), jnp.bfloat16)
+        for inner in range(heads_per_group):
+            head = group * heads_per_group + inner
+            at = slice(head * HEAD_SIZE, (head + 1) * HEAD_SIZE)
+            scores = (
+                lax.dot_general(
+                    q_ref[:, at],
+                    block_ref[:, :HEAD_SIZE],
+                    (((1,), (1,)), ((), ())),
+                    preferred_element_type=jnp.float32,
+                )
+                * factor
+            )
+            before = top_ref[:, head : head + 1]
+            high = jnp.max(scores, axis=1, keepdims=True)
+            high = jnp.maximum(before, jnp.where(chosen, high, UNSEEN))
+            weights = jnp.exp2(scores - jnp.where(chosen, high, SKIPPED)).astype(jnp.bfloat16)
+            mixed = jnp.dot(
+                weights,
+                jnp.concatenate([block_ref[:, HEAD_SIZE:], ones], axis=1),
+                preferred_element_type=jnp.float32,
+            )
+            fade = jnp.exp2(before - high)
+            old = out_in[:, at] if head not in fresh else out_ref[:, at]
+            fresh.add(head)
+            out_ref[:, at] = old * fade + mixed[:, :HEAD_SIZE]
+            here = lane == head
+            total = total_ref[...]
+            total_ref[...] = jnp.where(here, total * fade + mixed[:, HEAD_SIZE:], total)
+            top_ref[...] = jnp.where(here, high, top_ref[...])
+
+
+def add_blocks(queries, chosen, state, blocks, columns, group_list):
+    top, total, out = state
+    kernel = lambda *refs: block_kernel(columns, group_list, len(blocks), *refs)
+    rows = queries.shape[0]
+    work = 4 * rows * HEAD_SIZE * (QUERY_HEADS // KEY_VALUE_HEADS) * blocks[0].shape[0]
+    return pl.pallas_call(
+        kernel,
+        out_shape=tuple(jax.ShapeDtypeStruct(a.shape, a.dtype) for a in state),
+        input_output_aliases={2: 0, 3: 1, 4: 2},
+        cost_estimate=pl.CostEstimate(
+            flops=work * len(blocks),
+            bytes_accessed=out.size * 8 + sum(b.size for b in blocks) * 2,
+            transcendentals=0,
+        ),
+        name="add_blocks",
+    )(queries, chosen, top, total, out, *blocks)
+
+
+def gathered_body(
+    queries,
+    rotated_cache_keys,
+    stored_cache_values,
+    segment_new_keys,
+    segment_new_values,
+    block_ids,
+    residual_in,
+    out_weight,
+    norm_gain,
+    expert_ids,
+    gate_scores,
+    w_gate,
+    w_up,
+    w_down,
+):
+    parties = lax.axis_size("blk")
+    deep, across = grid_of(parties)
+    tokens = queries.shape[0]
+    width = residual_in.shape[1]
+    place = lax.axis_index("blk")
+    my_deep = place // (across * CORES)
+    my_across = place // CORES % across
+    my_core = place % CORES
+
+    def moved(array, step_deep, step_across, step_core=0):
+        return lax.ppermute(
+            array, "blk", shift_pairs(deep, across, step_deep, step_across, step_core)
+        )
+
+    spots = [(dz, dx) for dz in range(deep) for dx in range(across)]
+    sources = [
+        ((my_deep - dz) % deep * across + (my_across - dx) % across) * CORES + my_core
+        for dz, dx in spots
+    ]
+
+    chunks = []
+    for group in range(KEY_VALUE_HEADS):
+        of = slice(group * HEAD_SIZE, (group + 1) * HEAD_SIZE)
+        chunks.append(
+            jnp.concatenate([rotated_cache_keys[:, of], stored_cache_values[:, of]], axis=1)
+        )
+    blocks = {}
+    for dz in [0] + [d for k in range(1, deep // 2 + 1) for d in sorted({k, deep - k})]:
+        for group in range(KEY_VALUE_HEADS):
+            if dz == 0:
+                column = chunks[group]
+            elif dz <= deep // 2:
+                column = moved(blocks[dz - 1, 0, group], 1, 0)
+            else:
+                column = moved(blocks[(dz + 1) % deep, 0, group], -1, 0)
+            blocks[dz, 0, group] = column
+            for dx in range(1, across):
+                blocks[dz, dx, group] = moved(column, 0, dx)
+
+    pair_queries = jnp.concatenate([queries, moved(queries, 0, 0, 1)], axis=0)
+    pair_ids = jnp.concatenate([block_ids, moved(block_ids, 0, 0, 1)], axis=0)
+    chosen = jnp.any(
+        pair_ids[:, :, None] == jnp.stack(sources)[None, None, :], axis=1
+    ).astype(jnp.float32)
+    chosen = jnp.pad(chosen, ((0, 0), (0, -len(spots) % LANES)))
+
+    gates = jnp.concatenate([w_gate, moved(w_gate, 0, 0, 1)], axis=0)
+    ups = jnp.concatenate([w_up, moved(w_up, 0, 0, 1)], axis=0)
+    downs = jnp.concatenate([w_down, moved(w_down, 0, 0, 1)], axis=0)
+
+    state = own_partial(queries, segment_new_keys, segment_new_values)
+    order = [0] + [d for k in range(1, deep // 2 + 1) for d in sorted({k, deep - k})]
+    for dz in order:
+        for dx in range(across):
+            state = add_blocks(
+                pair_queries,
+                chosen,
+                state,
+                [blocks[dz, dx, g] for g in range(KEY_VALUE_HEADS)],
+                [dz * across + dx] * KEY_VALUE_HEADS,
+                list(range(KEY_VALUE_HEADS)),
+            )
+    top, total, out = state
+    far = [moved(a[tokens:], 0, 0, 1) for a in (top, total, out.astype(jnp.bfloat16))]
+    near_top, far_top = top[:tokens, :QUERY_HEADS], far[0][:, :QUERY_HEADS]
+    ceiling = jnp.maximum(near_top, far_top)
+    near_scale = jnp.exp2(near_top - ceiling)
+    far_scale = jnp.exp2(far_top - ceiling)
+    denominator = total[:tokens, :QUERY_HEADS] * near_scale + far[1][:, :QUERY_HEADS] * far_scale
+    near_scale = jnp.repeat(near_scale / denominator, HEAD_SIZE, axis=1)
+    far_scale = jnp.repeat(far_scale / denominator, HEAD_SIZE, axis=1)
+    attention = (out[:tokens] * near_scale + far[2].astype(jnp.float32) * far_scale).astype(
+        jnp.bfloat16
+    )
+    hidden_state = residual_in.astype(jnp.float32) + jnp.dot(
+        attention, out_weight, preferred_element_type=jnp.float32
+    )
+    normed = (
+        hidden_state
+        * lax.rsqrt(jnp.mean(hidden_state * hidden_state, axis=-1, keepdims=True) + NORM_EPSILON)
+        * norm_gain
+    ).astype(jnp.bfloat16)
+
+    mixing = gate_scores / jnp.sum(gate_scores, axis=1, keepdims=True)
+    experts = jnp.arange(parties, dtype=jnp.int32)
+    spread = jnp.sum(
+        jnp.where(expert_ids[:, :, None] == experts[None, None, :], mixing[:, :, None], 0.0), axis=1
+    )
+    coarse = spread.astype(jnp.bfloat16)
+    fine = (spread - coarse.astype(jnp.float32)).astype(jnp.bfloat16)
+    extra = jnp.concatenate([coarse, fine], axis=1)
+    extra = jnp.pad(extra, ((0, 0), (0, -extra.shape[1] % LANES)))
+    packed = jnp.concatenate([normed, extra], axis=1)
+
+    rows = {(0, 0): packed}
+    for dz in range(1, deep):
+        rows[dz, 0] = moved(packed, dz, 0)
+    for dz in range(deep):
+        for dx in range(1, across):
+            rows[dz, dx] = moved(rows[dz, 0], 0, dx)
+    partner = place + 1 - 2 * my_core
+
+    def run_experts(block):
+        inputs = block[:, :width]
+        weights = block[:, width : width + parties].astype(jnp.float32) + block[
+            :, width + parties : width + 2 * parties
+        ].astype(jnp.float32)
+        result = 0.0
+        for slot, expert in enumerate((place, partner)):
+            gate_part = jnp.dot(inputs, gates[slot], preferred_element_type=jnp.float32)
+            up_part = jnp.dot(inputs, ups[slot], preferred_element_type=jnp.float32)
+            inner = (jax.nn.silu(gate_part) * up_part).astype(jnp.bfloat16)
+            expert_out = jnp.dot(inner, downs[slot], preferred_element_type=jnp.float32)
+            weight = jnp.sum(jnp.where(experts[None, :] == expert, weights, 0.0), axis=1)
+            result = result + weight[:, None] * expert_out
+        return result
+
+    everything = jnp.concatenate([rows[spot] for spot in spots], axis=0)
+    outcome = run_experts(everything).reshape(len(spots), tokens, width)
+    outcome = {spot: outcome[n] for n, spot in enumerate(spots)}
+    mixture = 0.0
+    for dz in range(deep):
+        column = outcome[dz, 0]
+        for dx in range(1, across):
+            column = column + moved(
+                outcome[dz, dx].astype(jnp.bfloat16), 0, -dx
+            ).astype(jnp.float32)
+        if dz:
+            column = moved(column.astype(jnp.bfloat16), -dz, 0).astype(jnp.float32)
+        mixture = mixture + column
+    return (hidden_state + mixture).astype(jnp.bfloat16)
+
+
 def solution(mesh):
     placed = (
         P(("groups", "blk"), None),
@@ -192,6 +485,7 @@
         P("blk", None, None),
         P("blk", None, None),
     )
+    body = gathered_body if gathers(mesh) else routed_body
     return jax.shard_map(
         body, mesh=mesh, in_specs=placed, out_specs=P(("groups", "blk"), None), check_vma=False
     )

time: 313 us -> 184 us (0.59)
  blocking collectives: 115 us -> 0 us
  Pallas kernels: 0 us -> 63.9 us
  local copies, waits for them, and re-layouts: 47.4 us -> 8.02 us
  waiting for transfers between devices: 74.1 us -> 41.3 us
  starting transfers between devices: 18.4 us -> 41.6 us
  other arithmetic: 23.5 us -> 2.98 us
  matrix products: 29.4 us -> 22.5 us
    all_to_all x2 -> x0, blocking collectives: 115 us -> none  [the longest x1 65.6 us: body(): lax.all_to_all(outgoing, 'blk', split_axis=0, concat_axis=0, tiled=True)]
    all_to_all x4 -> x0, waiting for transfers between devices: 74.1 us -> none  [the longest x1 35.5 us: body(): lax.all_to_all(far_out.astype(jnp.bfloat16).reshape(senders, items, row_w...]
    pallas_call x0 -> x9, Pallas kernels: none -> 63.9 us  [the longest x8 58.3 us: add_blocks(): pl.pallas_call(kernel, out_shape=tuple((jax.ShapeDtypeStruct(a.shape, a.d...]
    ppermute x0 -> x36, starting transfers between devices: none -> 41.6 us  [moved(): lax.ppermute(array, 'blk', shift_pairs(deep, across, step_deep, step_acro...]
    ppermute x0 -> x36, waiting for transfers between devices: none -> 41.3 us  [moved(): lax.ppermute(array, 'blk', shift_pairs(deep, across, step_deep, step_acro...]
    gather x6 -> x0, local copies, waits for them, and re-layouts: 19 us -> none  [the longest x1 7.29 us: body(): back_out.reshape(-1, QUERY_HEADS * HEAD_SIZE)[owner_slots]]
    all_to_all x4 -> x0, starting transfers between devices: 18.4 us -> none  [the longest x1 5.22 us: body(): lax.all_to_all(far_max.reshape(senders, items, QUERY_HEADS), 'blk', split...]
    concatenate x14 -> x2, local copies, waits for them, and re-layouts: 11 us -> 0.98 us  [the longest x1 0.97 us: gathered_body(): pair_queries = jnp.concatenate([queries, moved(queries, 0, 0, 1)], axis=0)]
  transfers between devices with their start and end apart: 4 -> 36, of which waited for: 4 -> 14; matrix products, arithmetic and copies ran while one was open for 7% -> 10% of each run, Pallas kernels for 0% -> 31%
where the time goes in v1:
time: 184 us; the launch traced here: 181 us
  Pallas kernels  63.9 us (35%)
  starting transfers between devices  41.6 us (23%)
  waiting for transfers between devices  41.3 us (22%)
  matrix products  22.5 us (12%)
  local copies, waits for them, and re-layouts  8.02 us (4%)
  other arithmetic  2.98 us (2%)
    pallas_call x8, Pallas kernels, add_blocks(): pl.pallas_call(kernel, out_shape=tuple((jax.ShapeDtypeStruct(a.shape, a.d...  58.3 us
    ppermute x36, starting transfers between devices, moved(): lax.ppermute(array, 'blk', shift_pairs(deep, across, step_deep, step_acro...  41.6 us
    ppermute x36, waiting for transfers between devices, moved(): lax.ppermute(array, 'blk', shift_pairs(deep, across, step_deep, step_acro...  41.3 us
    dot_general x2, matrix products, run_experts(): expert_out = jnp.dot(inner, downs[slot], preferred_element_type=jnp.float32)  11.7 us
    dot_general x2, matrix products, run_experts(): up_part = jnp.dot(inputs, ups[slot], preferred_element_type=jnp.float32)  7.31 us
    pallas_call x1, Pallas kernels, own_partial(): pl.pallas_call(own_kernel, out_shape=(jax.ShapeDtypeStruct((2 * tokens, L...  5.63 us
  transfers between devices with their start and end apart: 36, of which 14 were waited for; matrix products, arithmetic and copies ran while one was open for 10% of the time, Pallas kernels for 31%

profile of v1, /device:TPU:0, one launch (start us, length us, event | category | flops | bytes accessed | tf_op | source)
XLA Modules:
  0.0 181.1 jit_solution(7827727333783313912)
XLA Ops:
  0.0 1.2 fusion.50
  1.2 5.1 %collective-permute-start.8 = (bf16[512,256]{1,0:T(8,128)(2,1)S(1)}, bf16[512,256]{1,0:T(8,128)(2,1)S(1)}, u32[]{:S(2)}, u32[]{:S(2)}) collective-permute-start(bf16[512,256]{1,0:T(8,128)(2,1)S(1)} %pad_maximum_fusion.refs_5_), channel_id=1, source_target_pairs={{0,12},{1,13},{2,14},{3,15},{4,0},{5,1},{6,2},{7,3},{8,4},{9,5},{1... | collective-permute-start | bytes 786440 | tf_op jit(solution)/shard_map/ppermute | solution.py:348
  6.4 1.5 collective-permute-start.2
  8.7 5.6 %own_partial.1 = (f32[128,128]{1,0:T(8,128)}, f32[128,128]{1,0:T(8,128)}, f32[128,2048]{1,0:T(8,128)}) custom-call(bf16[64,2048]{1,0:T(8,128)(2,1)} %q_ref.1, bf16[64,256]{1,0:T(8,128)(2,1)} %k_ref.1, bf16[64,256]{1,0:T(8,128)(2,1)} %v_ref.1), custom_call_target="tpu_custom_call" | custom-call | tf_op jit(solution)/shard_map/own_partial/pallas_call | solution.py:248
  14.5 3.9 %collective-permute-start.9 = (bf16[512,256]{1,0:T(8,128)(2,1)S(1)}, bf16[512,256]{1,0:T(8,128)(2,1)S(1)}, u32[]{:S(2)}, u32[]{:S(2)}) collective-permute-start(bf16[512,256]{1,0:T(8,128)(2,1)S(1)} %pad_maximum_fusion.1.refs_6_), channel_id=1, source_target_pairs={{0,12},{1,13},{2,14},{3,15},{4,0},{5,1},{6,2},{7,3},{8,4},{9,5},{1... | collective-permute-start | bytes 786440 | tf_op jit(solution)/shard_map/ppermute | solution.py:348
  18.4 0.6 collective-permute-start.3
  19.0 1.1 collective-permute-start.12
  20.4 0.6 pad_convert_fusion.refs_1_
  21.0 1.5 collective-permute-start.6
  22.6 8.5 %collective-permute-done.5.refs_6_ = bf16[512,256]{1,0:T(8,128)(2,1)S(1)} collective-permute-done((bf16[512,256]{1,0:T(8,128)(2,1)S(1)}, bf16[512,256]{1,0:T(8,128)(2,1)S(1)}, u32[]{:S(2)}, u32[]{:S(2)}) %collective-permute-start.5) | collective-permute-done | bytes 262176 | tf_op jit(solution)/shard_map/ppermute | solution.py:348
  31.1 2.6 %collective-permute-start.13 = (bf16[512,256]{1,0:T(8,128)(2,1)S(1)}, bf16[512,256]{1,0:T(8,128)(2,1)S(1)}, u32[]{:S(2)}, u32[]{:S(2)}) collective-permute-start(bf16[512,256]{1,0:T(8,128)(2,1)S(1)} %collective-permute-done.5.refs_6_), channel_id=1, source_target_pairs={{0,4},{1,5},{2,6},{3,7},{4,8},{5,9},{6,10},{7,11},{8,12},{9,13},{1... | collective-permute-start | bytes 786440 | tf_op jit(solution)/shard_map/ppermute | solution.py:348
  33.7 0.5 collective-permute-start.7
  34.2 1.5 collective-permute-start.10
  35.7 1.0 collective-permute-done.12.refs_5_
  36.7 0.5 collective-permute-start.11
  37.3 1.0 constant_dynamic-update-slice_fusion.refs_0_
  38.3 0.8 copy-done.1
  39.0 7.3 %add_blocks.8 = (f32[128,128]{1,0:T(8,128)}, f32[128,128]{1,0:T(8,128)}, f32[128,2048]{1,0:T(8,128)}) custom-call(bf16[128,2048]{1,0:T(8,128)(2,1)} %copy-done.1, f32[128,128]{1,0:T(8,128)} %pad_convert_fusion.refs_1_, f32[128,128]{1,0:T(8,128)} %get-tuple-element.32.refs_2_, ...), custom_call_target="tpu_custom_call", output_to_operand_aliasing={{0}: (2, {}), {1}: (3, {}), {2}: (4, {})} | custom-call | flops 536870912 | bytes 2621440 | tf_op jit(solution)/shard_map/add_blocks/pallas_call | solution.py:309
  46.4 1.5 collective-permute-start.14
  47.8 0.5 collective-permute-start.15
  48.4 7.3 %add_blocks.9 = (f32[128,128]{1,0:T(8,128)}, f32[128,128]{1,0:T(8,128)}, f32[128,2048]{1,0:T(8,128)}) custom-call(bf16[128,2048]{1,0:T(8,128)(2,1)} %copy-done.1, f32[128,128]{1,0:T(8,128)} %pad_convert_fusion.refs_1_, f32[128,128]{1,0:T(8,128)} %get-tuple-element.35.refs_2_, ...), custom_call_target="tpu_custom_call", output_to_operand_aliasing={{0}: (2, {}), {1}: (3, {}), {2}: (4, {})} | custom-call | flops 536870912 | bytes 2621440 | tf_op jit(solution)/shard_map/add_blocks/pallas_call | solution.py:309
  55.7 7.3 %add_blocks.10 = (f32[128,128]{1,0:T(8,128)}, f32[128,128]{1,0:T(8,128)}, f32[128,2048]{1,0:T(8,128)}) custom-call(bf16[128,2048]{1,0:T(8,128)(2,1)} %copy-done.1, f32[128,128]{1,0:T(8,128)} %pad_convert_fusion.refs_1_, f32[128,128]{1,0:T(8,128)} %get-tuple-element.38.refs_2_, ...), custom_call_target="tpu_custom_call", output_to_operand_aliasing={{0}: (2, {}), {1}: (3, {}), {2}: (4, {})} | custom-call | flops 536870912 | bytes 2621440 | tf_op jit(solution)/shard_map/add_blocks/pallas_call | solution.py:309
  63.0 7.4 %add_blocks.11 = (f32[128,128]{1,0:T(8,128)}, f32[128,128]{1,0:T(8,128)}, f32[128,2048]{1,0:T(8,128)}) custom-call(bf16[128,2048]{1,0:T(8,128)(2,1)} %copy-done.1, f32[128,128]{1,0:T(8,128)} %pad_convert_fusion.refs_1_, f32[128,128]{1,0:T(8,128)} %get-tuple-element.41.refs_2_, ...), custom_call_target="tpu_custom_call", output_to_operand_aliasing={{0}: (2, {}), {1}: (3, {}), {2}: (4, {})} | custom-call | flops 536870912 | bytes 2621440 | tf_op jit(solution)/shard_map/add_blocks/pallas_call | solution.py:309
  70.4 7.1 %add_blocks.12 = (f32[128,128]{1,0:T(8,128)}, f32[128,128]{1,0:T(8,128)}, f32[128,2048]{1,0:T(8,128)}) custom-call(bf16[128,2048]{1,0:T(8,128)(2,1)} %copy-done.1, f32[128,128]{1,0:T(8,128)} %pad_convert_fusion.refs_1_, f32[128,128]{1,0:T(8,128)} %get-tuple-element.44.refs_2_, ...), custom_call_target="tpu_custom_call", output_to_operand_aliasing={{0}: (2, {}), {1}: (3, {}), {2}: (4, {})} | custom-call | flops 536870912 | bytes 2621440 | tf_op jit(solution)/shard_map/add_blocks/pallas_call | solution.py:309
  77.6 0.7 copy-done.13
  78.3 7.2 %add_blocks.13 = (f32[128,128]{1,0:T(8,128)}, f32[128,128]{1,0:T(8,128)}, f32[128,2048]{1,0:T(8,128)}) custom-call(bf16[128,2048]{1,0:T(8,128)(2,1)} %copy-done.1, f32[128,128]{1,0:T(8,128)} %pad_convert_fusion.refs_1_, f32[128,128]{1,0:T(8,128)} %get-tuple-element.47.refs_2_, ...), custom_call_target="tpu_custom_call", output_to_operand_aliasing={{0}: (2, {}), {1}: (3, {}), {2}: (4, {})} | custom-call | flops 536870912 | bytes 2621440 | tf_op jit(solution)/shard_map/add_blocks/pallas_call | solution.py:309
  85.5 7.3 %add_blocks.14 = (f32[128,128]{1,0:T(8,128)}, f32[128,128]{1,0:T(8,128)}, f32[128,2048]{1,0:T(8,128)}) custom-call(bf16[128,2048]{1,0:T(8,128)(2,1)} %copy-done.1, f32[128,128]{1,0:T(8,128)} %pad_convert_fusion.refs_1_, f32[128,128]{1,0:T(8,128)} %get-tuple-element.50.refs_2_, ...), custom_call_target="tpu_custom_call", output_to_operand_aliasing={{0}: (2, {}), {1}: (3, {}), {2}: (4, {})} | custom-call | flops 536870912 | bytes 2621440 | tf_op jit(solution)/shard_map/add_blocks/pallas_call | solution.py:309
  92.8 0.7 copy-done.12
  93.6 7.3 %add_blocks.15 = (f32[128,128]{1,0:T(8,128)}, f32[128,128]{1,0:T(8,128)}, f32[128,2048]{1,0:T(8,128)}) custom-call(bf16[128,2048]{1,0:T(8,128)(2,1)} %copy-done.1, f32[128,128]{1,0:T(8,128)} %pad_convert_fusion.refs_1_, f32[128,128]{1,0:T(8,128)} %get-tuple-element.53.refs_2_, ...), custom_call_target="tpu_custom_call", output_to_operand_aliasing={{0}: (2, {}), {1}: (3, {}), {2}: (4, {})} | custom-call | flops 536870912 | bytes 2621440 | tf_op jit(solution)/shard_map/add_blocks/pallas_call | solution.py:309
  100.9 0.9 slice.87
  101.8 0.8 slice.90
  102.5 0.5 collective-permute-start.16
  103.0 1.1 slice.187
  104.3 0.8 fusion.46
  105.1 0.6 collective-permute-done.18
  106.1 3.4 %multiply_reduce_fusion = (f32[64]{0:T(128)S(1)}, f32[64,1024]{1,0:T(8,128)S(1)}) fusion(bf16[2048,1024]{1,0:T(8,128)(2,1)} %param.21, f32[8,8,16,128]{3,2,1,0:T(8,128)S(1)} %bitcast.58, f32[8,8,16,128]{3,2,1,0:T(8,128)S(1)} %bitcast.57, bf16[64,2048]{1,0:T(8,128)(2,1)S(1)} %collective-permute-done.18, f32[128,2048]{1,0:T(8,128)S(1)} %copy-done, ...), kind=kOutput, calls=%fused_computation.46 | convolution fusion | flops 269352896 | bytes 6422784 | tf_op jit(solution)/shard_map/dot_general | solution.py:412
  109.7 2.1 %collective-permute-start.20 = (bf16[64,1152]{1,0:T(8,128)(2,1)S(1)}, bf16[64,1152]{1,0:T(8,128)(2,1)S(1)}, u32[]{:S(2)}, u32[]{:S(2)}) collective-permute-start(bf16[64,1152]{1,0:T(8,128)(2,1)S(1)} %get-tuple-element.76), channel_id=1, source_target_pairs={{0,4},{1,5},{2,6},{3,7},{4,8},{5,9},{6,10},{7,11},{8,12},{9,13},{1... | collective-permute-start | bytes 442376 | tf_op jit(solution)/shard_map/ppermute | solution.py:348
  111.8 1.5 collective-permute-start.19
  113.8 0.6 collective-permute-start.22
  114.4 3.7 %collective-permute-done.20 = bf16[64,1152]{1,0:T(8,128)(2,1)S(1)} collective-permute-done((bf16[64,1152]{1,0:T(8,128)(2,1)S(1)}, bf16[64,1152]{1,0:T(8,128)(2,1)S(1)}, u32[]{:S(2)}, u32[]{:S(2)}) %collective-permute-start.20) | collective-permute-done | bytes 147488 | tf_op jit(solution)/shard_map/ppermute | solution.py:348
  118.3 1.9 %collective-permute-start.21 = (bf16[64,1152]{1,0:T(8,128)(2,1)S(1)}, bf16[64,1152]{1,0:T(8,128)(2,1)S(1)}, u32[]{:S(2)}, u32[]{:S(2)}) collective-permute-start(bf16[64,1152]{1,0:T(8,128)(2,1)S(1)} %collective-permute-done.20), channel_id=1, source_target_pairs={{0,2},{1,3},{2,0},{3,1},{4,6},{5,7},{6,4},{7,5},{8,10},{9,11},{10,... | collective-permute-start | bytes 442376 | tf_op jit(solution)/shard_map/ppermute | solution.py:348
  120.2 3.7 %collective-permute-done.22 = bf16[64,1152]{1,0:T(8,128)(2,1)S(1)} collective-permute-done((bf16[64,1152]{1,0:T(8,128)(2,1)S(1)}, bf16[64,1152]{1,0:T(8,128)(2,1)S(1)}, u32[]{:S(2)}, u32[]{:S(2)}) %collective-permute-start.22) | collective-permute-done | bytes 147488 | tf_op jit(solution)/shard_map/ppermute | solution.py:348
  123.9 1.9 %collective-permute-done.24 = bf16[64,1152]{1,0:T(8,128)(2,1)S(1)} collective-permute-done((bf16[64,1152]{1,0:T(8,128)(2,1)S(1)}, bf16[64,1152]{1,0:T(8,128)(2,1)S(1)}, u32[]{:S(2)}, u32[]{:S(2)}) %collective-permute-start.24) | collective-permute-done | bytes 147488 | tf_op jit(solution)/shard_map/ppermute | solution.py:348
  125.8 1.5 collective-permute-start.23
  127.3 0.5 collective-permute-start.25
  127.9 4.1 %collective-permute-done.23 = bf16[64,1152]{1,0:T(8,128)(2,1)S(1)} collective-permute-done((bf16[64,1152]{1,0:T(8,128)(2,1)S(1)}, bf16[64,1152]{1,0:T(8,128)(2,1)S(1)}, u32[]{:S(2)}, u32[]{:S(2)}) %collective-permute-start.23) | collective-permute-done | bytes 147488 | tf_op jit(solution)/shard_map/ppermute | solution.py:348
  132.0 1.5 collective-permute-done.25
  133.9 3.7 %fusion.7 = f32[512,768]{1,0:T(8,128)} fusion(bf16[1,1024,768]{2,1,0:T(8,128)(2,1)} %param.26, bf16[512,1152]{1,0:T(8,128)(2,1)S(1)} %constant_dynamic-update-slice_fusion.2), kind=kOutput, calls=%fused_computation.8 | convolution fusion | flops 805306368 | bytes 4194304 | tf_op jit(solution)/shard_map/dot_general | solution.py:448
  137.6 6.0 %fusion.5 = f32[512,1024]{1,0:T(8,128)} fusion(bf16[1,768,1024]{2,1,0:T(8,128)(2,1)} %param.27, f32[512,768]{1,0:T(8,128)} %fusion.7, bf16[1,1024,768]{2,1,0:T(8,128)(2,1)} %param.25, bf16[512,1152]{1,0:T(8,128)(2,1)S(1)} %constant_dynamic-update-slice_fusion.2), kind=kOutput, calls=%fused_computation.6 | convolution fusion | flops 1612972032 | bytes 7864320 | tf_op jit(solution)/shard_map/dot_general | solution.py:450
  143.7 3.6 %fusion.1 = f32[512,768]{1,0:T(8,128)} fusion(bf16[1,1024,768]{2,1,0:T(8,128)(2,1)} %collective-permute-done.27, bf16[512,1152]{1,0:T(8,128)(2,1)S(1)} %constant_dynamic-update-slice_fusion.2), kind=kOutput, calls=%fused_computation.2 | convolution fusion | flops 805306368 | bytes 4194304 | tf_op jit(solution)/shard_map/dot_general | solution.py:448
  147.3 5.7 %fusion.52 = (bf16[512,1024]{1,0:T(8,128)(2,1)S(1)}, f32[512,1024]{1,0:T(8,128)S(1)}) fusion(bf16[1,768,1024]{2,1,0:T(8,128)(2,1)} %collective-permute-done.28, f32[512,768]{1,0:T(8,128)} %fusion.1, bf16[1,1024,768]{2,1,0:T(8,128)(2,1)} %collective-permute-done.26, bf16[512,1152]{1,0:T(8,128)(2,1)} %copy-done.16, f32[512]{0:T(512)S(1)} %get-tuple-element.60, ...), kind=kOutput, calls=%fused_computation.84 | convolution fusion | flops 1615069184 | bytes 11014144 | tf_op jit(solution)/shard_map/dot_general | solution.py:450
  153.0 1.5 collective-permute-start.34
  154.5 0.5 collective-permute-start.32
  155.1 1.5 collective-permute-start.30
  156.5 0.5 collective-permute-start.29
  157.1 2.3 %collective-permute-done.34 = bf16[64,1024]{1,0:T(8,128)(2,1)S(1)} collective-permute-done((bf16[64,1024]{1,0:T(8,128)(2,1)S(1)}, bf16[64,1024]{1,0:T(8,128)(2,1)S(1)}, u32[]{:S(2)}, u32[]{:S(2)}) %collective-permute-start.34) | collective-permute-done | bytes 131104 | tf_op jit(solution)/shard_map/ppermute | solution.py:348
  159.4 2.7 %collective-permute-done.32 = bf16[64,1024]{1,0:T(8,128)(2,1)S(1)} collective-permute-done((bf16[64,1024]{1,0:T(8,128)(2,1)S(1)}, bf16[64,1024]{1,0:T(8,128)(2,1)S(1)}, u32[]{:S(2)}, u32[]{:S(2)}) %collective-permute-start.32) | collective-permute-done | bytes 131104 | tf_op jit(solution)/shard_map/ppermute | solution.py:348
  162.1 1.4 collective-permute-done.30
  163.6 6.0 %collective-permute-start.31 = (bf16[64,1024]{1,0:T(8,128)(2,1)S(1)}, bf16[64,1024]{1,0:T(8,128)(2,1)S(1)}, u32[]{:S(2)}, u32[]{:S(2)}) collective-permute-start(bf16[64,1024]{1,0:T(8,128)(2,1)S(1)} %get-tuple-element.63), channel_id=1, source_target_pairs={{0,12},{1,13},{2,14},{3,15},{4,0},{5,1},{6,2},{7,3},{8,4},{9,5},{1... | collective-permute-start | bytes 393224 | tf_op jit(solution)/shard_map/ppermute | solution.py:348
  169.5 0.6 collective-permute-start.33
  170.2 2.6 %collective-permute-done.31 = bf16[64,1024]{1,0:T(8,128)(2,1)S(1)} collective-permute-done((bf16[64,1024]{1,0:T(8,128)(2,1)S(1)}, bf16[64,1024]{1,0:T(8,128)(2,1)S(1)}, u32[]{:S(2)}, u32[]{:S(2)}) %collective-permute-start.31) | collective-permute-done | bytes 131104 | tf_op jit(solution)/shard_map/ppermute | solution.py:348
  172.8 4.0 %collective-permute-done.35 = bf16[64,1024]{1,0:T(8,128)(2,1)S(1)} collective-permute-done((bf16[64,1024]{1,0:T(8,128)(2,1)S(1)}, bf16[64,1024]{1,0:T(8,128)(2,1)S(1)}, u32[]{:S(2)}, u32[]{:S(2)}) %collective-permute-start.35) | collective-permute-done | bytes 131104 | tf_op jit(solution)/shard_map/ppermute | solution.py:348
  176.8 3.3 %collective-permute-done.33 = bf16[64,1024]{1,0:T(8,128)(2,1)S(1)} collective-permute-done((bf16[64,1024]{1,0:T(8,128)(2,1)S(1)}, bf16[64,1024]{1,0:T(8,128)(2,1)S(1)}, u32[]{:S(2)}, u32[]{:S(2)}) %collective-permute-start.33) | collective-permute-done | bytes 131104 | tf_op jit(solution)/shard_map/ppermute | solution.py:348
  180.1 0.8 fusion.38
  (103 shorter events, 3.2 us)
Async XLA Ops:
  0.0 7.9 %copy-start.20 = (s32[64,8]{0,1:T(8,128)S(1)}, s32[64,8]{0,1:T(8,128)}, u32[]{:S(2)}) copy-start(s32[64,8]{0,1:T(8,128)} %param.19) | copy-start | bytes 6148
  0.0 7.9 %copy-start.4 = (bf16[64,2048]{1,0:T(8,128)(2,1)S(1)}, bf16[64,2048]{1,0:T(8,128)(2,1)}, u32[]{:S(2)}) copy-start(bf16[64,2048]{1,0:T(8,128)(2,1)} %q_ref.1) | copy-start | bytes 786436
  0.0 8.4 %copy-start.18 = (f32[64,8]{0,1:T(8,128)S(1)}, f32[64,8]{0,1:T(8,128)}, u32[]{:S(2)}) copy-start(f32[64,8]{0,1:T(8,128)} %param.24) | copy-start | bytes 6148
  0.0 8.4 %copy-start.21 = (s32[64,8]{0,1:T(8,128)S(1)}, s32[64,8]{0,1:T(8,128)}, u32[]{:S(2)}) copy-start(s32[64,8]{0,1:T(8,128)} %param.23) | copy-start | bytes 6148
  1.2 37.0 %copy-start.2 = (bf16[512,256]{1,0:T(8,128)(2,1)}, bf16[512,256]{1,0:T(8,128)(2,1)S(1)}, u32[]{:S(2)}) copy-start(bf16[512,256]{1,0:T(8,128)(2,1)S(1)} %pad_maximum_fusion.refs_5_) | copy-start | bytes 786436
  1.2 17.1 %collective-permute-start.8 = (bf16[512,256]{1,0:T(8,128)(2,1)S(1)}, bf16[512,256]{1,0:T(8,128)(2,1)S(1)}, u32[]{:S(2)}, u32[]{:S(2)}) collective-permute-start(bf16[512,256]{1,0:T(8,128)(2,1)S(1)} %pad_maximum_fusion.refs_5_), channel_id=1, source_target_pairs={{0,12},{1,13},{2,14},{3,15},{4,0},{5,1},{6,2},{7,3},{8,4},{9,5},{1... | collective-permute-start | bytes 786440 | tf_op jit(solution)/shard_map/ppermute | solution.py:348
  6.4 12.6 %collective-permute-start.4 = (bf16[512,256]{1,0:T(8,128)(2,1)S(1)}, bf16[512,256]{1,0:T(8,128)(2,1)S(1)}, u32[]{:S(2)}, u32[]{:S(2)}) collective-permute-start(bf16[512,256]{1,0:T(8,128)(2,1)S(1)} %pad_maximum_fusion.refs_5_), channel_id=1, source_target_pairs={{0,4},{1,5},{2,6},{3,7},{4,8},{5,9},{6,10},{7,11},{8,12},{9,13},{1... | collective-permute-start | bytes 786440 | tf_op jit(solution)/shard_map/ppermute | solution.py:348
  6.4 14.6 %collective-permute-start.2 = (bf16[512,256]{1,0:T(8,128)(2,1)S(1)}, bf16[512,256]{1,0:T(8,128)(2,1)S(1)}, u32[]{:S(2)}, u32[]{:S(2)}) collective-permute-start(bf16[512,256]{1,0:T(8,128)(2,1)S(1)} %pad_maximum_fusion.refs_5_), channel_id=1, source_target_pairs={{0,2},{1,3},{2,0},{3,1},{4,6},{5,7},{6,4},{7,5},{8,10},{9,11},{10,... | collective-permute-start | bytes 786440 | tf_op jit(solution)/shard_map/ppermute | solution.py:348
  7.9 6.6 %collective-permute-start.1 = (s32[64,8]{0,1:T(8,128)S(1)}, s32[64,8]{0,1:T(8,128)S(1)}, u32[]{:S(2)}, u32[]{:S(2)}) collective-permute-start(s32[64,8]{0,1:T(8,128)S(1)} %copy-done.20), channel_id=1, source_target_pairs={{0,1},{1,0},{2,3},{3,2},{4,5},{5,4},{6,7},{7,6},{8,9},{9,8},{10,11... | collective-permute-start | bytes 6152 | tf_op jit(solution)/shard_map/ppermute | solution.py:348
  7.9 10.4 %collective-permute-start = (bf16[64,2048]{1,0:T(8,128)(2,1)S(1)}, bf16[64,2048]{1,0:T(8,128)(2,1)}, u32[]{:S(2)}, u32[]{:S(2)}) collective-permute-start(bf16[64,2048]{1,0:T(8,128)(2,1)S(1)} %copy-done.4), channel_id=1, source_target_pairs={{0,1},{1,0},{2,3},{3,2},{4,5},{5,4},{6,7},{7,6},{8,9},{9,8},{10,11... | collective-permute-start | bytes 786440 | tf_op jit(solution)/shard_map/ppermute | solution.py:348
  8.5 29.8 %copy-start.3 = (bf16[512,256]{1,0:T(8,128)(2,1)}, bf16[512,256]{1,0:T(8,128)(2,1)S(1)}, u32[]{:S(2)}) copy-start(bf16[512,256]{1,0:T(8,128)(2,1)S(1)} %pad_maximum_fusion.1.refs_6_) | copy-start | bytes 786436
  14.5 19.2 %collective-permute-start.9 = (bf16[512,256]{1,0:T(8,128)(2,1)S(1)}, bf16[512,256]{1,0:T(8,128)(2,1)S(1)}, u32[]{:S(2)}, u32[]{:S(2)}) collective-permute-start(bf16[512,256]{1,0:T(8,128)(2,1)S(1)} %pad_maximum_fusion.1.refs_6_), channel_id=1, source_target_pairs={{0,12},{1,13},{2,14},{3,15},{4,0},{5,1},{6,2},{7,3},{8,4},{9,5},{1... | collective-permute-start | bytes 786440 | tf_op jit(solution)/shard_map/ppermute | solution.py:348
  18.3 12.8 %collective-permute-start.5 = (bf16[512,256]{1,0:T(8,128)(2,1)S(1)}, bf16[512,256]{1,0:T(8,128)(2,1)S(1)}, u32[]{:S(2)}, u32[]{:S(2)}) collective-permute-start(bf16[512,256]{1,0:T(8,128)(2,1)S(1)} %pad_maximum_fusion.1.refs_6_), channel_id=1, source_target_pairs={{0,4},{1,5},{2,6},{3,7},{4,8},{5,9},{6,10},{7,11},{8,12},{9,13},{1... | collective-permute-start | bytes 786440 | tf_op jit(solution)/shard_map/ppermute | solution.py:348
  18.3 37.3 %copy-start.5 = (bf16[512,256]{1,0:T(8,128)(2,1)}, bf16[512,256]{1,0:T(8,128)(2,1)S(1)}, u32[]{:S(2)}) copy-start(bf16[512,256]{1,0:T(8,128)(2,1)S(1)} %collective-permute-done.8.refs_5_) | copy-start | bytes 786436
  18.4 15.9 %collective-permute-start.3 = (bf16[512,256]{1,0:T(8,128)(2,1)S(1)}, bf16[512,256]{1,0:T(8,128)(2,1)S(1)}, u32[]{:S(2)}, u32[]{:S(2)}) collective-permute-start(bf16[512,256]{1,0:T(8,128)(2,1)S(1)} %pad_maximum_fusion.1.refs_6_), channel_id=1, source_target_pairs={{0,2},{1,3},{2,0},{3,1},{4,6},{5,7},{6,4},{7,5},{8,10},{9,11},{10,... | collective-permute-start | bytes 786440 | tf_op jit(solution)/shard_map/ppermute | solution.py:348
  19.0 36.7 %copy-start.6 = (bf16[512,256]{1,0:T(8,128)(2,1)}, bf16[512,256]{1,0:T(8,128)(2,1)S(1)}, u32[]{:S(2)}) copy-start(bf16[512,256]{1,0:T(8,128)(2,1)S(1)} %collective-permute-done.4.refs_5_) | copy-start | bytes 786436
  19.0 17.8 %collective-permute-start.12 = (bf16[512,256]{1,0:T(8,128)(2,1)S(1)}, bf16[512,256]{1,0:T(8,128)(2,1)S(1)}, u32[]{:S(2)}, u32[]{:S(2)}) collective-permute-start(bf16[512,256]{1,0:T(8,128)(2,1)S(1)} %collective-permute-done.4.refs_5_), channel_id=1, source_target_pairs={{0,4},{1,5},{2,6},{3,7},{4,8},{5,9},{6,10},{7,11},{8,12},{9,13},{1... | collective-permute-start | bytes 786440 | tf_op jit(solution)/shard_map/ppermute | solution.py:348
  21.0 27.4 %copy-start.7 = (bf16[512,256]{1,0:T(8,128)(2,1)}, bf16[512,256]{1,0:T(8,128)(2,1)S(1)}, u32[]{:S(2)}) copy-start(bf16[512,256]{1,0:T(8,128)(2,1)S(1)} %collective-permute-done.2.refs_5_) | copy-start | bytes 786436
  21.0 25.3 %collective-permute-start.6 = (bf16[512,256]{1,0:T(8,128)(2,1)S(1)}, bf16[512,256]{1,0:T(8,128)(2,1)}, u32[]{:S(2)}, u32[]{:S(2)}) collective-permute-start(bf16[512,256]{1,0:T(8,128)(2,1)S(1)} %collective-permute-done.4.refs_5_), channel_id=1, source_target_pairs={{0,2},{1,3},{2,0},{3,1},{4,6},{5,7},{6,4},{7,5},{8,10},{9,11},{10,... | collective-permute-start | bytes 786440 | tf_op jit(solution)/shard_map/ppermute | solution.py:348
  31.1 24.6 %copy-start.11 = (bf16[512,256]{1,0:T(8,128)(2,1)}, bf16[512,256]{1,0:T(8,128)(2,1)S(1)}, u32[]{:S(2)}) copy-start(bf16[512,256]{1,0:T(8,128)(2,1)S(1)} %collective-permute-done.5.refs_6_) | copy-start | bytes 786436
  31.1 16.7 %collective-permute-start.13 = (bf16[512,256]{1,0:T(8,128)(2,1)S(1)}, bf16[512,256]{1,0:T(8,128)(2,1)S(1)}, u32[]{:S(2)}, u32[]{:S(2)}) collective-permute-start(bf16[512,256]{1,0:T(8,128)(2,1)S(1)} %collective-permute-done.5.refs_6_), channel_id=1, source_target_pairs={{0,4},{1,5},{2,6},{3,7},{4,8},{5,9},{6,10},{7,11},{8,12},{9,13},{1... | collective-permute-start | bytes 786440 | tf_op jit(solution)/shard_map/ppermute | solution.py:348
  33.7 36.7 %copy-start.9 = (bf16[512,256]{1,0:T(8,128)(2,1)}, bf16[512,256]{1,0:T(8,128)(2,1)S(1)}, u32[]{:S(2)}) copy-start(bf16[512,256]{1,0:T(8,128)(2,1)S(1)} %collective-permute-done.9.refs_6_) | copy-start | bytes 786436
  33.7 29.3 %collective-permute-start.7 = (bf16[512,256]{1,0:T(8,128)(2,1)S(1)}, bf16[512,256]{1,0:T(8,128)(2,1)}, u32[]{:S(2)}, u32[]{:S(2)}) collective-permute-start(bf16[512,256]{1,0:T(8,128)(2,1)S(1)} %collective-permute-done.5.refs_6_), channel_id=1, source_target_pairs={{0,2},{1,3},{2,0},{3,1},{4,6},{5,7},{6,4},{7,5},{8,10},{9,11},{10,... | collective-permute-start | bytes 786440 | tf_op jit(solution)/shard_map/ppermute | solution.py:348
  34.2 14.2 %copy-start.14 = (bf16[512,256]{1,0:T(8,128)(2,1)}, bf16[512,256]{1,0:T(8,128)(2,1)S(1)}, u32[]{:S(2)}) copy-start(bf16[512,256]{1,0:T(8,128)(2,1)S(1)} %collective-permute-done.3.refs_6_) | copy-start | bytes 786436
  34.2 43.3 %collective-permute-start.10 = (bf16[512,256]{1,0:T(8,128)(2,1)S(1)}, bf16[512,256]{1,0:T(8,128)(2,1)S(1)}, u32[]{:S(2)}, u32[]{:S(2)}) collective-permute-start(bf16[512,256]{1,0:T(8,128)(2,1)S(1)} %collective-permute-done.8.refs_5_), channel_id=1, source_target_pairs={{0,2},{1,3},{2,0},{3,1},{4,6},{5,7},{6,4},{7,5},{8,10},{9,11},{10,... | collective-permute-start | bytes 786440 | tf_op jit(solution)/shard_map/ppermute | solution.py:348
  36.7 33.7 %copy-start.8 = (bf16[512,256]{1,0:T(8,128)(2,1)}, bf16[512,256]{1,0:T(8,128)(2,1)S(1)}, u32[]{:S(2)}) copy-start(bf16[512,256]{1,0:T(8,128)(2,1)S(1)} %collective-permute-done.12.refs_5_) | copy-start | bytes 786436
  36.7 40.8 %collective-permute-start.11 = (bf16[512,256]{1,0:T(8,128)(2,1)S(1)}, bf16[512,256]{1,0:T(8,128)(2,1)}, u32[]{:S(2)}, u32[]{:S(2)}) collective-permute-start(bf16[512,256]{1,0:T(8,128)(2,1)S(1)} %collective-permute-done.9.refs_6_), channel_id=1, source_target_pairs={{0,2},{1,3},{2,0},{3,1},{4,6},{5,7},{6,4},{7,5},{8,10},{9,11},{10,... | collective-permute-start | bytes 786440 | tf_op jit(solution)/shard_map/ppermute | solution.py:348
  38.2 0.8 copy-start.1
  46.4 46.5 %collective-permute-start.14 = (bf16[512,256]{1,0:T(8,128)(2,1)S(1)}, bf16[512,256]{1,0:T(8,128)(2,1)S(1)}, u32[]{:S(2)}, u32[]{:S(2)}) collective-permute-start(bf16[512,256]{1,0:T(8,128)(2,1)S(1)} %collective-permute-done.12.refs_5_), channel_id=1, source_target_pairs={{0,2},{1,3},{2,0},{3,1},{4,6},{5,7},{6,4},{7,5},{8,10},{9,11},{10,... | collective-permute-start | bytes 786440 | tf_op jit(solution)/shard_map/ppermute | solution.py:348
  47.8 15.1 %copy-start.10 = (bf16[512,256]{1,0:T(8,128)(2,1)}, bf16[512,256]{1,0:T(8,128)(2,1)S(1)}, u32[]{:S(2)}) copy-start(bf16[512,256]{1,0:T(8,128)(2,1)S(1)} %collective-permute-done.13.refs_6_) | copy-start | bytes 786436
  47.8 45.0 %collective-permute-start.15 = (bf16[512,256]{1,0:T(8,128)(2,1)S(1)}, bf16[512,256]{1,0:T(8,128)(2,1)S(1)}, u32[]{:S(2)}, u32[]{:S(2)}) collective-permute-start(bf16[512,256]{1,0:T(8,128)(2,1)S(1)} %collective-permute-done.13.refs_6_), channel_id=1, source_target_pairs={{0,2},{1,3},{2,0},{3,1},{4,6},{5,7},{6,4},{7,5},{8,10},{9,11},{10,... | collective-permute-start | bytes 786440 | tf_op jit(solution)/shard_map/ppermute | solution.py:348
  77.6 0.7 copy-start.13
  92.8 0.7 copy-start.12
  92.8 0.8 copy-start.15
  100.9 5.2 %copy-start = (f32[128,2048]{1,0:T(8,128)S(1)}, f32[128,2048]{1,0:T(8,128)}, u32[]{:S(2)}) copy-start(f32[128,2048]{1,0:T(8,128)} %get-tuple-element.56) | copy-start | bytes 3145732
  100.9 5.2 %copy-start.17 = (bf16[64,1024]{1,0:T(8,128)(2,1)S(1)}, bf16[64,1024]{1,0:T(8,128)(2,1)}, u32[]{:S(2)}) copy-start(bf16[64,1024]{1,0:T(8,128)(2,1)} %param.20) | copy-start | bytes 393220
  102.5 1.8 collective-permute-start.17
  102.5 1.8 collective-permute-start.16
  104.1 1.6 collective-permute-start.18
  106.1 3.5 %copy-start.19 = (f32[1024]{0:T(1024)S(1)}, f32[1024]{0:T(1024)}, u32[]{:S(2)}) copy-start(f32[1024]{0:T(1024)} %param.22) | copy-start | bytes 12292
  109.7 8.4 %collective-permute-start.20 = (bf16[64,1152]{1,0:T(8,128)(2,1)S(1)}, bf16[64,1152]{1,0:T(8,128)(2,1)S(1)}, u32[]{:S(2)}, u32[]{:S(2)}) collective-permute-start(bf16[64,1152]{1,0:T(8,128)(2,1)S(1)} %get-tuple-element.76), channel_id=1, source_target_pairs={{0,4},{1,5},{2,6},{3,7},{4,8},{5,9},{6,10},{7,11},{8,12},{9,13},{1... | collective-permute-start | bytes 442376 | tf_op jit(solution)/shard_map/ppermute | solution.py:348
  111.8 6.5 %collective-permute-start.19 = (bf16[64,1152]{1,0:T(8,128)(2,1)S(1)}, bf16[64,1152]{1,0:T(8,128)(2,1)S(1)}, u32[]{:S(2)}, u32[]{:S(2)}) collective-permute-start(bf16[64,1152]{1,0:T(8,128)(2,1)S(1)} %get-tuple-element.76), channel_id=1, source_target_pairs={{0,2},{1,3},{2,0},{3,1},{4,6},{5,7},{6,4},{7,5},{8,10},{9,11},{10,... | collective-permute-start | bytes 442376 | tf_op jit(solution)/shard_map/ppermute | solution.py:348
  113.3 33.9 %collective-permute-start.26 = (bf16[1,1024,768]{2,1,0:T(8,128)(2,1)}, bf16[1,1024,768]{2,1,0:T(8,128)(2,1)}, u32[]{:S(2)}, u32[]{:S(2)}) collective-permute-start(bf16[1,1024,768]{2,1,0:T(8,128)(2,1)} %param.25), channel_id=1, source_target_pairs={{0,1},{1,0},{2,3},{3,2},{4,5},{5,4},{6,7},{7,6},{8,9},{9,8},{10,11... | collective-permute-start | bytes 4718600 | tf_op jit(solution)/shard_map/ppermute | solution.py:348
  113.3 30.3 %collective-permute-start.27 = (bf16[1,1024,768]{2,1,0:T(8,128)(2,1)}, bf16[1,1024,768]{2,1,0:T(8,128)(2,1)}, u32[]{:S(2)}, u32[]{:S(2)}) collective-permute-start(bf16[1,1024,768]{2,1,0:T(8,128)(2,1)} %param.26), channel_id=1, source_target_pairs={{0,1},{1,0},{2,3},{3,2},{4,5},{5,4},{6,7},{7,6},{8,9},{9,8},{10,11... | collective-permute-start | bytes 4718600 | tf_op jit(solution)/shard_map/ppermute | solution.py:348
  113.8 10.1 %collective-permute-start.22 = (bf16[64,1152]{1,0:T(8,128)(2,1)S(1)}, bf16[64,1152]{1,0:T(8,128)(2,1)S(1)}, u32[]{:S(2)}, u32[]{:S(2)}) collective-permute-start(bf16[64,1152]{1,0:T(8,128)(2,1)S(1)} %get-tuple-element.76), channel_id=1, source_target_pairs={{0,8},{1,9},{2,10},{3,11},{4,12},{5,13},{6,14},{7,15},{8,0},{9,1},... | collective-permute-start | bytes 442376 | tf_op jit(solution)/shard_map/ppermute | solution.py:348
  118.1 7.7 %collective-permute-start.24 = (bf16[64,1152]{1,0:T(8,128)(2,1)S(1)}, bf16[64,1152]{1,0:T(8,128)(2,1)S(1)}, u32[]{:S(2)}, u32[]{:S(2)}) collective-permute-start(bf16[64,1152]{1,0:T(8,128)(2,1)S(1)} %get-tuple-element.76), channel_id=1, source_target_pairs={{0,12},{1,13},{2,14},{3,15},{4,0},{5,1},{6,2},{7,3},{8,4},{9,5},{1... | collective-permute-start | bytes 442376 | tf_op jit(solution)/shard_map/ppermute | solution.py:348
  118.3 8.9 %collective-permute-start.21 = (bf16[64,1152]{1,0:T(8,128)(2,1)S(1)}, bf16[64,1152]{1,0:T(8,128)(2,1)S(1)}, u32[]{:S(2)}, u32[]{:S(2)}) collective-permute-start(bf16[64,1152]{1,0:T(8,128)(2,1)S(1)} %collective-permute-done.20), channel_id=1, source_target_pairs={{0,2},{1,3},{2,0},{3,1},{4,6},{5,7},{6,4},{7,5},{8,10},{9,11},{10,... | collective-permute-start | bytes 442376 | tf_op jit(solution)/shard_map/ppermute | solution.py:348
  123.9 23.3 %collective-permute-start.28 = (bf16[1,768,1024]{2,1,0:T(8,128)(2,1)}, bf16[1,768,1024]{2,1,0:T(8,128)(2,1)}, u32[]{:S(2)}, u32[]{:S(2)}) collective-permute-start(bf16[1,768,1024]{2,1,0:T(8,128)(2,1)} %param.27), channel_id=1, source_target_pairs={{0,1},{1,0},{2,3},{3,2},{4,5},{5,4},{6,7},{7,6},{8,9},{9,8},{10,11... | collective-permute-start | bytes 4718600 | tf_op jit(solution)/shard_map/ppermute | solution.py:348
  125.8 6.2 %collective-permute-start.23 = (bf16[64,1152]{1,0:T(8,128)(2,1)S(1)}, bf16[64,1152]{1,0:T(8,128)(2,1)S(1)}, u32[]{:S(2)}, u32[]{:S(2)}) collective-permute-start(bf16[64,1152]{1,0:T(8,128)(2,1)S(1)} %collective-permute-done.22), channel_id=1, source_target_pairs={{0,2},{1,3},{2,0},{3,1},{4,6},{5,7},{6,4},{7,5},{8,10},{9,11},{10,... | collective-permute-start | bytes 442376 | tf_op jit(solution)/shard_map/ppermute | solution.py:348
  127.3 6.3 %collective-permute-start.25 = (bf16[64,1152]{1,0:T(8,128)(2,1)S(1)}, bf16[64,1152]{1,0:T(8,128)(2,1)S(1)}, u32[]{:S(2)}, u32[]{:S(2)}) collective-permute-start(bf16[64,1152]{1,0:T(8,128)(2,1)S(1)} %collective-permute-done.24), channel_id=1, source_target_pairs={{0,2},{1,3},{2,0},{3,1},{4,6},{5,7},{6,4},{7,5},{8,10},{9,11},{10,... | collective-permute-start | bytes 442376 | tf_op jit(solution)/shard_map/ppermute | solution.py:348
  133.6 10.1 %copy-start.16 = (bf16[512,1152]{1,0:T(8,128)(2,1)}, bf16[512,1152]{1,0:T(8,128)(2,1)S(1)}, u32[]{:S(2)}) copy-start(bf16[512,1152]{1,0:T(8,128)(2,1)S(1)} %constant_dynamic-update-slice_fusion.2) | copy-start | bytes 3538948
  153.0 6.4 %collective-permute-start.34 = (bf16[64,1024]{1,0:T(8,128)(2,1)S(1)}, bf16[64,1024]{1,0:T(8,128)(2,1)S(1)}, u32[]{:S(2)}, u32[]{:S(2)}) collective-permute-start(bf16[64,1024]{1,0:T(8,128)(2,1)S(1)} %get-tuple-element.67), channel_id=1, source_target_pairs={{0,2},{1,3},{2,0},{3,1},{4,6},{5,7},{6,4},{7,5},{8,10},{9,11},{10,... | collective-permute-start | bytes 393224 | tf_op jit(solution)/shard_map/ppermute | solution.py:348
  154.5 7.5 %collective-permute-start.32 = (bf16[64,1024]{1,0:T(8,128)(2,1)S(1)}, bf16[64,1024]{1,0:T(8,128)(2,1)S(1)}, u32[]{:S(2)}, u32[]{:S(2)}) collective-permute-start(bf16[64,1024]{1,0:T(8,128)(2,1)S(1)} %get-tuple-element.68), channel_id=1, source_target_pairs={{0,2},{1,3},{2,0},{3,1},{4,6},{5,7},{6,4},{7,5},{8,10},{9,11},{10,... | collective-permute-start | bytes 393224 | tf_op jit(solution)/shard_map/ppermute | solution.py:348
  155.1 8.4 %collective-permute-start.30 = (bf16[64,1024]{1,0:T(8,128)(2,1)S(1)}, bf16[64,1024]{1,0:T(8,128)(2,1)S(1)}, u32[]{:S(2)}, u32[]{:S(2)}) collective-permute-start(bf16[64,1024]{1,0:T(8,128)(2,1)S(1)} %get-tuple-element.69), channel_id=1, source_target_pairs={{0,2},{1,3},{2,0},{3,1},{4,6},{5,7},{6,4},{7,5},{8,10},{9,11},{10,... | collective-permute-start | bytes 393224 | tf_op jit(solution)/shard_map/ppermute | solution.py:348
  156.5 13.6 %collective-permute-start.29 = (bf16[64,1024]{1,0:T(8,128)(2,1)S(1)}, bf16[64,1024]{1,0:T(8,128)(2,1)S(1)}, u32[]{:S(2)}, u32[]{:S(2)}) collective-permute-start(bf16[64,1024]{1,0:T(8,128)(2,1)S(1)} %get-tuple-element.66), channel_id=1, source_target_pairs={{0,2},{1,3},{2,0},{3,1},{4,6},{5,7},{6,4},{7,5},{8,10},{9,11},{10,... | collective-permute-start | bytes 393224 | tf_op jit(solution)/shard_map/ppermute | solution.py:348
  163.6 9.2 %collective-permute-start.31 = (bf16[64,1024]{1,0:T(8,128)(2,1)S(1)}, bf16[64,1024]{1,0:T(8,128)(2,1)S(1)}, u32[]{:S(2)}, u32[]{:S(2)}) collective-permute-start(bf16[64,1024]{1,0:T(8,128)(2,1)S(1)} %get-tuple-element.63), channel_id=1, source_target_pairs={{0,12},{1,13},{2,14},{3,15},{4,0},{5,1},{6,2},{7,3},{8,4},{9,5},{1... | collective-permute-start | bytes 393224 | tf_op jit(solution)/shard_map/ppermute | solution.py:348
  169.5 7.3 %collective-permute-start.35 = (bf16[64,1024]{1,0:T(8,128)(2,1)S(1)}, bf16[64,1024]{1,0:T(8,128)(2,1)S(1)}, u32[]{:S(2)}, u32[]{:S(2)}) collective-permute-start(bf16[64,1024]{1,0:T(8,128)(2,1)S(1)} %get-tuple-element.64), channel_id=1, source_target_pairs={{0,4},{1,5},{2,6},{3,7},{4,8},{5,9},{6,10},{7,11},{8,12},{9,13},{1... | collective-permute-start | bytes 393224 | tf_op jit(solution)/shard_map/ppermute | solution.py:348
  169.5 10.5 %collective-permute-start.33 = (bf16[64,1024]{1,0:T(8,128)(2,1)S(1)}, bf16[64,1024]{1,0:T(8,128)(2,1)S(1)}, u32[]{:S(2)}, u32[]{:S(2)}) collective-permute-start(bf16[64,1024]{1,0:T(8,128)(2,1)S(1)} %get-tuple-element.65), channel_id=1, source_target_pairs={{0,8},{1,9},{2,10},{3,11},{4,12},{5,13},{6,14},{7,15},{8,0},{9,1},... | collective-permute-start | bytes 393224 | tf_op jit(solution)/shard_map/ppermute | solution.py:348

commit v2 on v0

--- a/solution.py
+++ b/solution.py
@@ -1,6 +1,8 @@
 import jax
 import jax.numpy as jnp
 from jax import lax
+from jax.experimental import pallas as pl
+from jax.experimental.pallas import tpu as pltpu
 from jax.sharding import PartitionSpec as P
 
 QUERY_HEADS = 16
@@ -70,7 +72,7 @@
     return (slot_index, filler)
 
 
-def body(
+def routed_body(
     queries,
     rotated_cache_keys,
     stored_cache_values,
@@ -175,6 +177,369 @@
     return (hidden_state + mixture).astype(jnp.bfloat16)
 
 
+CORES = 2
+LOG2_E = 1.4426950408889634
+UNSEEN = -1e20
+SKIPPED = 1e30
+LANES = 128
+TILE = 256
+ONES_ROWS = 16
+
+
+def grid_of(parties):
+    chips = parties // CORES
+    across = round(chips ** (1 / 3))
+    while chips % across:
+        across -= 1
+    return (chips // across, across)
+
+
+def gathers(mesh):
+    return mesh.shape["blk"] <= 4 * TOPB and mesh.shape["blk"] % CORES == 0
+
+
+def shift_pairs(deep, across, step_deep, step_across, step_core):
+    return [
+        (
+            (z * across + x) * CORES + c,
+            ((z + step_deep) % deep * across + (x + step_across) % across) * CORES
+            + (c + step_core) % CORES,
+        )
+        for z in range(deep)
+        for x in range(across)
+        for c in range(CORES)
+    ]
+
+
+def attention_kernel(pieces, first, count, *refs):
+    queries = refs[0:2]
+    chosen_ref = refs[2]
+    given = None if first else refs[3:7]
+    block_refs = refs[-4 - count : -4]
+    stats_refs = refs[-4:-2]
+    out_refs = refs[-2:]
+    tokens = queries[0].shape[0]
+    per_tile = TILE // tokens
+    heads_per_group = QUERY_HEADS // KEY_VALUE_HEADS
+    factor = HEAD_SIZE ** (-0.5) * LOG2_E
+    for group in range(KEY_VALUE_HEADS):
+        mine = []
+        for (of_group, column), block_ref in zip(pieces, block_refs):
+            if of_group == group:
+                values = block_ref[:, HEAD_SIZE:].astype(jnp.float32).T.astype(jnp.bfloat16)
+                ones = jnp.ones((ONES_ROWS, values.shape[1]), jnp.bfloat16)
+                mine.append((column, block_ref, jnp.concatenate([values, ones], axis=0)))
+        for owner in range(2):
+            for tile in range(heads_per_group // per_tile):
+                head = group * heads_per_group + tile * per_tile
+                at = slice(head * tokens, head * tokens + TILE)
+                rows = jnp.concatenate(
+                    [
+                        queries[owner][:, h * HEAD_SIZE : (h + 1) * HEAD_SIZE]
+                        for h in range(head, head + per_tile)
+                    ],
+                    axis=0,
+                )
+                if first:
+                    top = jnp.full((1, TILE), UNSEEN, jnp.float32)
+                    total = jnp.zeros((1, TILE), jnp.float32)
+                    out = jnp.zeros((HEAD_SIZE, TILE), jnp.float32)
+                else:
+                    top = given[owner][0:1, at]
+                    total = given[owner][1:2, at]
+                    out = given[2 + owner][:, at].astype(jnp.float32)
+                for column, block_ref, mixer in mine:
+                    if column is None and owner:
+                        continue
+                    scores = lax.dot_general(
+                        block_ref[:, :HEAD_SIZE],
+                        rows,
+                        (((1,), (1,)), ((), ())),
+                        preferred_element_type=jnp.float32,
+                    )
+                    if column is None:
+                        key = lax.broadcasted_iota(jnp.int32, scores.shape, 0)
+                        token = lax.broadcasted_iota(jnp.int32, scores.shape, 1) % tokens
+                        scores = jnp.where(key <= token, scores, -SKIPPED)
+                        high = jnp.maximum(top, jnp.max(scores, axis=0, keepdims=True) * factor)
+                        shift = high
+                    else:
+                        chosen = chosen_ref[
+                            column : column + 1, owner * TILE : (owner + 1) * TILE
+                        ]
+                        high = jnp.max(scores, axis=0, keepdims=True) * factor
+                        high = jnp.maximum(top, jnp.where(chosen > 0.5, high, UNSEEN))
+                        shift = jnp.where(chosen > 0.5, high, SKIPPED)
+                    weights = jnp.exp2(scores * factor - shift).astype(jnp.bfloat16)
+                    mixed = jnp.dot(mixer, weights, preferred_element_type=jnp.float32)
+                    fade = jnp.exp2(top - high)
+                    out = out * fade + mixed[:HEAD_SIZE]
+                    total = total * fade + mixed[HEAD_SIZE : HEAD_SIZE + 1]
+                    top = high
+                stats_refs[owner][0:1, at] = top
+                stats_refs[owner][1:2, at] = total
+                out_refs[owner][:, at] = out.astype(out_refs[owner].dtype)
+
+
+def attend(queries, chosen, state, pieces, blocks, last=False):
+    tokens = queries[0].shape[0]
+    span = QUERY_HEADS * tokens
+    stats = jax.ShapeDtypeStruct((8, span), jnp.float32)
+    out = jax.ShapeDtypeStruct((HEAD_SIZE, span), jnp.float32)
+    sent = jax.ShapeDtypeStruct((HEAD_SIZE, span), jnp.bfloat16)
+    count = len(blocks)
+    keys = sum(b.shape[0] for b in blocks)
+    return pl.pallas_call(
+        lambda *refs: attention_kernel(pieces, state is None, count, *refs),
+        out_shape=(stats, stats, out, sent if last else out),
+        cost_estimate=pl.CostEstimate(
+            flops=4 * keys * span * HEAD_SIZE,
+            bytes_accessed=16 * HEAD_SIZE * span + keys * HEAD_SIZE * 4,
+            transcendentals=keys * span,
+        ),
+        name="attend_blocks",
+    )(*queries, chosen, *(state or ()), *blocks)
+
+
+def finish_kernel(
+    near_stats,
+    near_out,
+    far_stats,
+    far_out,
+    weight_ref,
+    residual_ref,
+    gain_ref,
+    extra_ref,
+    hidden_ref,
+    packed_ref,
+):
+    tokens, width = residual_ref.shape
+    near_top, far_top = near_stats[0:1, :], far_stats[0:1, :]
+    ceiling = jnp.maximum(near_top, far_top)
+    near_scale = jnp.exp2(near_top - ceiling)
+    far_scale = jnp.exp2(far_top - ceiling)
+    total = near_stats[1:2, :] * near_scale + far_stats[1:2, :] * far_scale
+    mixed = near_out[...] * (near_scale / total) + far_out[...].astype(jnp.float32) * (
+        far_scale / total
+    )
+    per_turn = LANES // tokens
+    heads = []
+    for turn in range(QUERY_HEADS // per_turn):
+        turned = mixed[:, turn * LANES : (turn + 1) * LANES].T.astype(jnp.bfloat16)
+        heads.extend(turned[n * tokens : (n + 1) * tokens] for n in range(per_turn))
+    attention = jnp.concatenate(heads, axis=1)
+    hidden = residual_ref[...].astype(jnp.float32) + jnp.dot(
+        attention, weight_ref[...], preferred_element_type=jnp.float32
+    )
+    hidden_ref[...] = hidden
+    mean = jnp.mean(hidden * hidden, axis=-1, keepdims=True)
+    packed_ref[:, :width] = (hidden * lax.rsqrt(mean + NORM_EPSILON) * gain_ref[...]).astype(
+        jnp.bfloat16
+    )
+    packed_ref[:, width:] = extra_ref[...]
+
+
+def expert_kernel(parties, rows_count, *refs):
+    who_ref = refs[0]
+    row_refs = refs[1 : 1 + rows_count]
+    weight_refs = refs[1 + rows_count : 7 + rows_count]
+    out_refs = refs[7 + rows_count : 7 + 2 * rows_count]
+    (sum_ref,) = refs[7 + 2 * rows_count :]
+    step = pl.program_id(0)
+    tokens, width = out_refs[0].shape
+    block = jnp.concatenate([r[...] for r in row_refs], axis=0)
+    inputs = block[:, :width]
+    extra = block[:, width:].astype(jnp.float32)
+    lane = lax.broadcasted_iota(jnp.int32, extra.shape, 1)
+    result = None
+    for slot in range(2):
+        gate_ref, up_ref, down_ref = weight_refs[3 * slot : 3 * slot + 3]
+        expert = who_ref[slot]
+        here = (lane == expert) | (lane == expert + parties)
+        weight = jnp.sum(jnp.where(here, extra, 0.0), axis=1, keepdims=True)
+        gate = jnp.dot(inputs, gate_ref[0], preferred_element_type=jnp.float32)
+        up = jnp.dot(inputs, up_ref[0], preferred_element_type=jnp.float32)
+        inner = (gate / (1.0 + jnp.exp(-gate)) * up).astype(jnp.bfloat16)
+        part = weight * jnp.dot(inner, down_ref[0], preferred_element_type=jnp.float32)
+        result = part if result is None else result + part
+
+    @pl.when(step == 0)
+    def _():
+        sum_ref[...] = result
+
+    @pl.when(step > 0)
+    def _():
+        sum_ref[...] += result
+
+    @pl.when(step == pl.num_programs(0) - 1)
+    def _():
+        for n, out_ref in enumerate(out_refs):
+            out_ref[...] = sum_ref[n * tokens : (n + 1) * tokens, :].astype(out_ref.dtype)
+
+
+def run_experts(parties, who, rows, weights, out_types):
+    tokens, packed_width = rows[0].shape
+    width = weights[0].shape[1]
+    hidden = weights[0].shape[2]
+    step = 2 * LANES
+    whole = pl.BlockSpec((tokens, packed_width), lambda f: (0, 0))
+    out = pl.BlockSpec((tokens, width), lambda f: (0, 0))
+    into = pl.BlockSpec((1, width, step), lambda f: (0, 0, f))
+    back = pl.BlockSpec((1, step, width), lambda f: (0, f, 0))
+    return pl.pallas_call(
+        lambda *refs: expert_kernel(parties, len(rows), *refs),
+        grid=(hidden // step,),
+        in_specs=[pl.BlockSpec(memory_space=pltpu.SMEM)]
+        + [whole] * len(rows)
+        + [into, into, back] * 2,
+        out_specs=[out] * len(rows),
+        out_shape=[jax.ShapeDtypeStruct((tokens, width), t) for t in out_types],
+        scratch_shapes=[pltpu.VMEM((tokens * len(rows), width), jnp.float32)],
+        cost_estimate=pl.CostEstimate(
+            flops=12 * tokens * len(rows) * width * hidden,
+            bytes_accessed=12 * width * hidden,
+            transcendentals=0,
+        ),
+        name="run_experts",
+    )(who, *rows, *weights)
+
+
+def gathered_body(
+    queries,
+    rotated_cache_keys,
+    stored_cache_values,
+    segment_new_keys,
+    segment_new_values,
+    block_ids,
+    residual_in,
+    out_weight,
+    norm_gain,
+    expert_ids,
+    gate_scores,
+    w_gate,
+    w_up,
+    w_down,
+):
+    parties = lax.axis_size("blk")
+    deep, across = grid_of(parties)
+    tokens = queries.shape[0]
+    place = lax.axis_index("blk")
+    my_deep = place // (across * CORES)
+    my_across = place // CORES % across
+    my_core = place % CORES
+    groups = range(KEY_VALUE_HEADS)
+
+    def moved(array, step_deep, step_across, step_core=0):
+        return lax.ppermute(
+            array, "blk", shift_pairs(deep, across, step_deep, step_across, step_core)
+        )
+
+    spots = [(dz, dx) for dz in range(deep) for dx in range(across)]
+    order = [0] + [d for k in range(1, deep // 2 + 1) for d in sorted({k, deep - k})]
+    sources = jnp.stack(
+        [
+            ((my_deep - dz) % deep * across + (my_across - dx) % across) * CORES + my_core
+            for dz, dx in spots
+        ]
+    )
+
+    def paired(keys, values, group):
+        of = slice(group * HEAD_SIZE, (group + 1) * HEAD_SIZE)
+        return jnp.concatenate([keys[:, of], values[:, of]], axis=1)
+
+    blocks = {}
+    for dz in order:
+        for group in groups:
+            if dz == 0:
+                column = paired(rotated_cache_keys, stored_cache_values, group)
+            elif dz <= deep // 2:
+                column = moved(blocks[dz - 1, 0, group], 1, 0)
+            else:
+                column = moved(blocks[(dz + 1) % deep, 0, group], -1, 0)
+            blocks[dz, 0, group] = column
+            for dx in range(1, across):
+                blocks[dz, dx, group] = moved(column, 0, dx)
+
+    pair_queries = (queries, moved(queries, 0, 0, 1))
+    chosen = jnp.concatenate(
+        [
+            jnp.tile(
+                jnp.any(sources[:, None, None] == ids.T[None, :, :], axis=1).astype(jnp.float32),
+                (1, TILE // tokens),
+            )
+            for ids in (block_ids, moved(block_ids, 0, 0, 1))
+        ],
+        axis=1,
+    )
+    weights = [w_gate, w_up, w_down]
+    weights = weights + [moved(w, 0, 0, 1) for w in weights]
+    who = jnp.stack([place, place + 1 - 2 * my_core])
+
+    state = None
+    for dz in order:
+        for dx in range(across):
+            pieces = [(g, dz * across + dx) for g in groups]
+            given = [blocks[dz, dx, g] for g in groups]
+            if state is None:
+                pieces = [(g, None) for g in groups] + pieces
+                given = [paired(segment_new_keys, segment_new_values, g) for g in groups] + given
+            last = dz == order[-1] and dx == across - 1
+            state = attend(pair_queries, chosen, state, pieces, given, last)
+
+    mixing = gate_scores / jnp.sum(gate_scores, axis=1, keepdims=True)
+    experts = jnp.arange(parties, dtype=jnp.int32)
+    spread = jnp.sum(
+        jnp.where(expert_ids[:, :, None] == experts[None, None, :], mixing[:, :, None], 0.0), axis=1
+    )
+    coarse = spread.astype(jnp.bfloat16)
+    fine = (spread - coarse.astype(jnp.float32)).astype(jnp.bfloat16)
+    extra = jnp.concatenate([coarse, fine], axis=1)
+    extra = jnp.pad(extra, ((0, 0), (0, -extra.shape[1] % LANES)))
+
+    near_stats, far_stats, near_out, far_out = state
+    hidden_state, packed = pl.pallas_call(
+        finish_kernel,
+        out_shape=(
+            jax.ShapeDtypeStruct(residual_in.shape, jnp.float32),
+            jax.ShapeDtypeStruct((tokens, residual_in.shape[1] + extra.shape[1]), jnp.bfloat16),
+        ),
+        name="finish_attention",
+    )(
+        near_stats,
+        near_out,
+        moved(far_stats, 0, 0, 1),
+        moved(far_out, 0, 0, 1),
+        out_weight,
+        residual_in,
+        norm_gain.reshape(1, -1),
+        extra,
+    )
+
+    rows = {(0, 0): packed}
+    for dz in range(1, deep):
+        rows[dz, 0] = moved(packed, dz, 0)
+    for dz in range(deep):
+        for dx in range(1, across):
+            rows[dz, dx] = moved(rows[dz, 0], 0, dx)
+
+    mixture = hidden_state
+    for dz in order:
+        results = run_experts(
+            parties,
+            who,
+            [rows[dz, dx] for dx in range(across)],
+            weights,
+            [jnp.float32] + [jnp.bfloat16] * (across - 1),
+        )
+        column = results[0]
+        for dx in range(1, across):
+            column = column + moved(results[dx], 0, -dx).astype(jnp.float32)
+        if dz:
+            column = moved(column.astype(jnp.bfloat16), -dz, 0).astype(jnp.float32)
+        mixture = mixture + column
+    return mixture.astype(jnp.bfloat16)
+
+
 def solution(mesh):
     placed = (
         P(("groups", "blk"), None),
@@ -192,6 +557,7 @@
         P("blk", None, None),
         P("blk", None, None),
     )
+    body = gathered_body if gathers(mesh) else routed_body
     return jax.shard_map(
         body, mesh=mesh, in_specs=placed, out_specs=P(("groups", "blk"), None), check_vma=False
     )

time: 313 us -> 171 us (0.55); the launches traced: 308 us -> 170 us
  blocking collectives: 115 us -> 0 us
  Pallas kernels: 0 us -> 80.2 us
  local copies, waits for them, and re-layouts: 47.4 us -> 3.93 us
  matrix products: 29.4 us -> 0 us
  waiting for transfers between devices: 74.1 us -> 47.5 us
  other arithmetic: 23.5 us -> 2.94 us
  starting transfers between devices: 18.4 us -> 35.1 us
    all_to_all x2 -> x0, blocking collectives: 115 us -> none  [the longest x1 65.6 us: body(): lax.all_to_all(outgoing, 'blk', split_axis=0, concat_axis=0, tiled=True)]
    pallas_call x0 -> x13, Pallas kernels: none -> 80.2 us  [the longest x8 48.9 us: attend(): pl.pallas_call(lambda *refs: attention_kernel(pieces, state is None, coun...]
    all_to_all x4 -> x0, waiting for transfers between devices: 74.1 us -> none  [the longest x1 35.5 us: body(): lax.all_to_all(far_out.astype(jnp.bfloat16).reshape(senders, items, row_w...]
    ppermute x0 -> x35, waiting for transfers between devices: none -> 47.5 us  [moved(): lax.ppermute(array, 'blk', shift_pairs(deep, across, step_deep, step_acro...]
    ppermute x0 -> x35, starting transfers between devices: none -> 35.1 us  [moved(): lax.ppermute(array, 'blk', shift_pairs(deep, across, step_deep, step_acro...]
    dot_general x13 -> x0, matrix products: 29.4 us -> none  [the longest x4 7.43 us: partials(): lax.dot_general(group_queries, group_keys, (((1,), (1,)), ((), ())), pref...]
    gather x6 -> x0, local copies, waits for them, and re-layouts: 19 us -> none  [the longest x1 7.29 us: body(): back_out.reshape(-1, QUERY_HEADS * HEAD_SIZE)[owner_slots]]
    all_to_all x4 -> x0, starting transfers between devices: 18.4 us -> none  [the longest x1 5.22 us: body(): lax.all_to_all(far_max.reshape(senders, items, QUERY_HEADS), 'blk', split...]
  transfers between devices with their start and end apart: 4 -> 35, of which waited for: 4 -> 13; matrix products, arithmetic and copies ran while one was open for 7% -> 2% of each run, Pallas kernels for 0% -> 47%
where the time goes in v2:
time: 171 us; the launch traced here: 170 us
  Pallas kernels  80.2 us (47%)
  waiting for transfers between devices  47.5 us (28%)
  starting transfers between devices  35.1 us (21%)
  local copies, waits for them, and re-layouts  3.93 us (2%)
  other arithmetic  2.94 us (2%)
    pallas_call x8, Pallas kernels, attend(): pl.pallas_call(lambda *refs: attention_kernel(pieces, state is None, coun...  48.9 us
    ppermute x35, waiting for transfers between devices, moved(): lax.ppermute(array, 'blk', shift_pairs(deep, across, step_deep, step_acro...  47.5 us
    ppermute x35, starting transfers between devices, moved(): lax.ppermute(array, 'blk', shift_pairs(deep, across, step_deep, step_acro...  35.1 us
    pallas_call x4, Pallas kernels, run_experts(): pl.pallas_call(lambda *refs: expert_kernel(parties, len(rows), *refs), gr...  27.1 us
    pallas_call x1, Pallas kernels, gathered_body(): pl.pallas_call(finish_kernel, out_shape=(jax.ShapeDtypeStruct(residual_in...  4.22 us
  transfers between devices with their start and end apart: 35, of which 13 were waited for; matrix products, arithmetic and copies ran while one was open for 2% of the time, Pallas kernels for 47%

profile of v2, /device:TPU:0, one launch (start us, length us, event | category | flops | bytes accessed | tf_op | source)
XLA Modules:
  0.0 170.2 jit_solution(14553607150028225207)
XLA Ops:
  0.0 1.3 fusion.3
  1.4 3.0 %collective-permute-start.2 = (bf16[512,256]{1,0:T(8,128)(2,1)S(1)}, bf16[512,256]{1,0:T(8,128)(2,1)S(1)}, u32[]{:S(2)}, u32[]{:S(2)}) collective-permute-start(bf16[512,256]{1,0:T(8,128)(2,1)S(1)} %pad_maximum_fusion.refs_5_), channel_id=1, source_target_pairs={{0,2},{1,3},{2,0},{3,1},{4,6},{5,7},{6,4},{7,5},{8,10},{9,11},{10,... | collective-permute-start | bytes 786440 | tf_op jit(solution)/shard_map/ppermute | solution.py:433
  4.4 1.6 collective-permute-start.4
  6.0 0.5 collective-permute-start.1
  6.5 1.6 collective-permute-start.5
  8.2 2.3 %collective-permute-start.8 = (bf16[512,256]{1,0:T(8,128)(2,1)S(1)}, bf16[512,256]{1,0:T(8,128)(2,1)}, u32[]{:S(2)}, u32[]{:S(2)}) collective-permute-start(bf16[512,256]{1,0:T(8,128)(2,1)S(1)} %pad_maximum_fusion.refs_5_), channel_id=1, source_target_pairs={{0,12},{1,13},{2,14},{3,15},{4,0},{5,1},{6,2},{7,3},{8,4},{9,5},{1... | collective-permute-start | bytes 786440 | tf_op jit(solution)/shard_map/ppermute | solution.py:433
  10.5 1.1 collective-permute-start.9
  11.6 0.8 collective-permute-start.3
  12.4 3.1 %collective-permute-done.4.refs_7_ = bf16[512,256]{1,0:T(8,128)(2,1)} collective-permute-done((bf16[512,256]{1,0:T(8,128)(2,1)S(1)}, bf16[512,256]{1,0:T(8,128)(2,1)}, u32[]{:S(2)}, u32[]{:S(2)}) %collective-permute-start.4) | collective-permute-done | bytes 262176 | tf_op jit(solution)/shard_map/ppermute | solution.py:433
  15.6 0.3 collective-permute-start.6
  15.9 5.2 %collective-permute-done.5.refs_8_ = bf16[512,256]{1,0:T(8,128)(2,1)} collective-permute-done((bf16[512,256]{1,0:T(8,128)(2,1)S(1)}, bf16[512,256]{1,0:T(8,128)(2,1)}, u32[]{:S(2)}, u32[]{:S(2)}) %collective-permute-start.5) | collective-permute-done | bytes 262176 | tf_op jit(solution)/shard_map/ppermute | solution.py:433
  21.5 4.0 %collective-permute-done.8.refs_7_ = bf16[512,256]{1,0:T(8,128)(2,1)} collective-permute-done((bf16[512,256]{1,0:T(8,128)(2,1)S(1)}, bf16[512,256]{1,0:T(8,128)(2,1)}, u32[]{:S(2)}, u32[]{:S(2)}) %collective-permute-start.8) | collective-permute-done | bytes 262176 | tf_op jit(solution)/shard_map/ppermute | solution.py:433
  25.5 0.5 collective-permute-start.10
  26.0 4.9 %collective-permute-done.9.refs_8_ = bf16[512,256]{1,0:T(8,128)(2,1)S(1)} collective-permute-done((bf16[512,256]{1,0:T(8,128)(2,1)S(1)}, bf16[512,256]{1,0:T(8,128)(2,1)S(1)}, u32[]{:S(2)}, u32[]{:S(2)}) %collective-permute-start.9) | collective-permute-done | bytes 262176 | tf_op jit(solution)/shard_map/ppermute | solution.py:433
  30.9 0.5 collective-permute-start.11
  32.0 0.5 collective-permute-start.20
  32.6 0.6 pad_maximum_fusion.2
  33.5 4.3 %collective-permute-done.10.refs_7_ = bf16[512,256]{1,0:T(8,128)(2,1)} collective-permute-done((bf16[512,256]{1,0:T(8,128)(2,1)}, bf16[512,256]{1,0:T(8,128)(2,1)}, u32[]{:S(2)}, u32[]{:S(2)}) %collective-permute-start.10) | collective-permute-done | bytes 262176 | tf_op jit(solution)/shard_map/ppermute | solution.py:433
  37.8 0.9 collective-permute-start.12
  38.8 3.3 %collective-permute-done.11.refs_8_ = bf16[512,256]{1,0:T(8,128)(2,1)} collective-permute-done((bf16[512,256]{1,0:T(8,128)(2,1)S(1)}, bf16[512,256]{1,0:T(8,128)(2,1)}, u32[]{:S(2)}, u32[]{:S(2)}) %collective-permute-start.11) | collective-permute-done | bytes 262176 | tf_op jit(solution)/shard_map/ppermute | solution.py:433
  42.1 0.6 collective-permute-start.13
  42.6 0.6 copy-done.4
  43.2 5.8 %attend_blocks.8 = (f32[8,1024]{1,0:T(8,128)}, f32[8,1024]{1,0:T(8,128)}, f32[128,1024]{1,0:T(8,128)}, f32[128,1024]{1,0:T(8,128)}) custom-call(bf16[64,2048]{1,0:T(8,128)(2,1)} %refs_0_.15, bf16[64,2048]{1,0:T(8,128)(2,1)} %copy-done.3, f32[8,512]{1,0:T(8,128)} %copy-done.4, bf16[64,256]{1,0:T(8,128)(2,1)} %get-tuple-element.99.refs_3_, ...), custom_call_target="tpu_custom_call" | custom-call | flops 603979776 | bytes 2686976 | tf_op jit(solution)/shard_map/attend_blocks/pallas_call | solution.py:292
  49.0 0.7 collective-permute-done.12.refs_7_
  49.7 0.8 collective-permute-start.14
  50.6 2.7 %collective-permute-done.13.refs_8_ = bf16[512,256]{1,0:T(8,128)(2,1)} collective-permute-done((bf16[512,256]{1,0:T(8,128)(2,1)}, bf16[512,256]{1,0:T(8,128)(2,1)}, u32[]{:S(2)}, u32[]{:S(2)}) %collective-permute-start.13) | collective-permute-done | bytes 262176 | tf_op jit(solution)/shard_map/ppermute | solution.py:433
  53.3 0.8 collective-permute-start.15
  54.1 6.1 %attend_blocks.9 = (f32[8,1024]{1,0:T(8,128)}, f32[8,1024]{1,0:T(8,128)}, f32[128,1024]{1,0:T(8,128)}, f32[128,1024]{1,0:T(8,128)}) custom-call(bf16[64,2048]{1,0:T(8,128)(2,1)} %refs_0_.15, bf16[64,2048]{1,0:T(8,128)(2,1)} %copy-done.3, f32[8,512]{1,0:T(8,128)} %copy-done.4, f32[8,1024]{1,0:T(8,128)} %get-tuple-element.47.refs_3_, ...), custom_call_target="tpu_custom_call" | custom-call | flops 536870912 | bytes 2621440 | tf_op jit(solution)/shard_map/attend_blocks/pallas_call | solution.py:292
  60.3 6.2 %attend_blocks.10 = (f32[8,1024]{1,0:T(8,128)}, f32[8,1024]{1,0:T(8,128)}, f32[128,1024]{1,0:T(8,128)}, f32[128,1024]{1,0:T(8,128)}) custom-call(bf16[64,2048]{1,0:T(8,128)(2,1)} %refs_0_.15, bf16[64,2048]{1,0:T(8,128)(2,1)} %copy-done.3, f32[8,512]{1,0:T(8,128)} %copy-done.4, f32[8,1024]{1,0:T(8,128)} %get-tuple-element.51.refs_3_, ...), custom_call_target="tpu_custom_call" | custom-call | flops 536870912 | bytes 2621440 | tf_op jit(solution)/shard_map/attend_blocks/pallas_call | solution.py:292
  66.5 6.1 %attend_blocks.11 = (f32[8,1024]{1,0:T(8,128)}, f32[8,1024]{1,0:T(8,128)}, f32[128,1024]{1,0:T(8,128)}, f32[128,1024]{1,0:T(8,128)}) custom-call(bf16[64,2048]{1,0:T(8,128)(2,1)} %refs_0_.15, bf16[64,2048]{1,0:T(8,128)(2,1)} %copy-done.3, f32[8,512]{1,0:T(8,128)} %copy-done.4, f32[8,1024]{1,0:T(8,128)} %get-tuple-element.55.refs_3_, ...), custom_call_target="tpu_custom_call" | custom-call | flops 536870912 | bytes 2621440 | tf_op jit(solution)/shard_map/attend_blocks/pallas_call | solution.py:292
  72.6 6.3 %attend_blocks.12 = (f32[8,1024]{1,0:T(8,128)}, f32[8,1024]{1,0:T(8,128)}, f32[128,1024]{1,0:T(8,128)}, f32[128,1024]{1,0:T(8,128)}) custom-call(bf16[64,2048]{1,0:T(8,128)(2,1)} %refs_0_.15, bf16[64,2048]{1,0:T(8,128)(2,1)} %copy-done.3, f32[8,512]{1,0:T(8,128)} %copy-done.4, f32[8,1024]{1,0:T(8,128)} %get-tuple-element.59.refs_3_, ...), custom_call_target="tpu_custom_call" | custom-call | flops 536870912 | bytes 2621440 | tf_op jit(solution)/shard_map/attend_blocks/pallas_call | solution.py:292
  78.9 6.1 %attend_blocks.13 = (f32[8,1024]{1,0:T(8,128)}, f32[8,1024]{1,0:T(8,128)}, f32[128,1024]{1,0:T(8,128)}, f32[128,1024]{1,0:T(8,128)}) custom-call(bf16[64,2048]{1,0:T(8,128)(2,1)} %refs_0_.15, bf16[64,2048]{1,0:T(8,128)(2,1)} %copy-done.3, f32[8,512]{1,0:T(8,128)} %copy-done.4, f32[8,1024]{1,0:T(8,128)} %get-tuple-element.63.refs_3_, ...), custom_call_target="tpu_custom_call" | custom-call | flops 536870912 | bytes 2621440 | tf_op jit(solution)/shard_map/attend_blocks/pallas_call | solution.py:292
  85.1 6.1 %attend_blocks.14 = (f32[8,1024]{1,0:T(8,128)}, f32[8,1024]{1,0:T(8,128)}, f32[128,1024]{1,0:T(8,128)}, f32[128,1024]{1,0:T(8,128)}) custom-call(bf16[64,2048]{1,0:T(8,128)(2,1)} %refs_0_.15, bf16[64,2048]{1,0:T(8,128)(2,1)} %copy-done.3, f32[8,512]{1,0:T(8,128)} %copy-done.4, f32[8,1024]{1,0:T(8,128)} %get-tuple-element.67.refs_3_, ...), custom_call_target="tpu_custom_call" | custom-call | flops 536870912 | bytes 2621440 | tf_op jit(solution)/shard_map/attend_blocks/pallas_call | solution.py:292
  91.2 6.1 %attend_blocks.15 = (f32[8,1024]{1,0:T(8,128)}, f32[8,1024]{1,0:T(8,128)}, f32[128,1024]{1,0:T(8,128)}, bf16[128,1024]{1,0:T(8,128)(2,1)}) custom-call(bf16[64,2048]{1,0:T(8,128)(2,1)} %refs_0_.15, bf16[64,2048]{1,0:T(8,128)(2,1)} %copy-done.3, f32[8,512]{1,0:T(8,128)} %copy-done.4, f32[8,1024]{1,0:T(8,128)} %get-tuple-element.71.refs_3_, ...), custom_call_target="tpu_custom_call" | custom-call | flops 536870912 | bytes 2621440 | tf_op jit(solution)/shard_map/attend_blocks/pallas_call | solution.py:292
  97.3 0.5 collective-permute-start.16
  97.8 0.7 fusion.2.extra_ref
  98.5 0.6 collective-permute-done.16.far_stats
  99.1 0.6 copy-done.18
  99.8 4.2 %finish_attention.1 = (f32[64,1024]{1,0:T(8,128)}, bf16[64,1152]{1,0:T(8,128)(2,1)}) custom-call(f32[8,1024]{1,0:T(8,128)} %get-tuple-element.75.near_stats, f32[128,1024]{1,0:T(8,128)} %get-tuple-element.76.near_out, f32[8,1024]{1,0:T(8,128)} %copy-done.18, bf16[128,1024]{1,0:T(8,128)(2,1)} %copy-done.7, bf16[2048,1024]{1,0:T(8,128)(2,1)} %weight_ref.1, ...), custom_call_target="tpu_custom_call" | custom-call | tf_op jit(solution)/shard_map/finish_attention/pallas_call | solution.py:500
  104.0 0.9 collective-permute-start.31
  104.9 0.9 collective-permute-start.27
  105.8 7.7 %collective-permute-done.31.refs_1_ = bf16[64,1152]{1,0:T(8,128)(2,1)} collective-permute-done((bf16[64,1152]{1,0:T(8,128)(2,1)}, bf16[64,1152]{1,0:T(8,128)(2,1)}, u32[]{:S(2)}, u32[]{:S(2)}) %collective-permute-start.31) | collective-permute-done | bytes 147488 | tf_op jit(solution)/shard_map/ppermute | solution.py:433
  113.5 2.9 %collective-permute-start.23 = (bf16[64,1152]{1,0:T(8,128)(2,1)}, bf16[64,1152]{1,0:T(8,128)(2,1)S(1)}, u32[]{:S(2)}, u32[]{:S(2)}) collective-permute-start(bf16[64,1152]{1,0:T(8,128)(2,1)} %get-tuple-element.80.refs_1_), channel_id=1, source_target_pairs={{0,4},{1,5},{2,6},{3,7},{4,8},{5,9},{6,10},{7,11},{8,12},{9,13},{1... | collective-permute-start | bytes 442376 | tf_op jit(solution)/shard_map/ppermute | solution.py:433
  116.4 1.2 collective-permute-start.32
  117.6 5.8 %collective-permute-done.23.refs_1_ = bf16[64,1152]{1,0:T(8,128)(2,1)S(1)} collective-permute-done((bf16[64,1152]{1,0:T(8,128)(2,1)}, bf16[64,1152]{1,0:T(8,128)(2,1)S(1)}, u32[]{:S(2)}, u32[]{:S(2)}) %collective-permute-start.23) | collective-permute-done | bytes 147488 | tf_op jit(solution)/shard_map/ppermute | solution.py:433
  123.4 1.0 collective-permute-start.28
  124.4 0.6 pad_add_fusion.refs_0_
  125.0 1.0 collective-permute-start.18
  126.0 1.0 collective-permute-start.24
  127.2 6.7 %run_experts.7 = (f32[64,1024]{1,0:T(8,128)}, bf16[64,1024]{1,0:T(8,128)(2,1)}) custom-call(s32[2]{0:T(128)} %pad_add_fusion.refs_0_, bf16[64,1152]{1,0:T(8,128)(2,1)} %collective-permute-done.31.refs_1_, bf16[64,1152]{1,0:T(8,128)(2,1)} %collective-permute-done.32.refs_2_, bf16[1,1024,768]{2,1,0:T(8,128)(2,1)} %refs_3_.7, bf16[1,1024,768]{2,1,0:T(8,128)(2,1)} %refs_4_.7, ...), custom_call_target="tpu_custom_call" | custom-call | flops 1207959552 | bytes 9437184 | tf_op jit(solution)/shard_map/run_experts/pallas_call | solution.py:389
  134.0 1.1 collective-permute-start.33
  135.0 6.8 %run_experts.6 = (f32[64,1024]{1,0:T(8,128)}, bf16[64,1024]{1,0:T(8,128)(2,1)}) custom-call(s32[2]{0:T(128)} %pad_add_fusion.refs_0_, bf16[64,1152]{1,0:T(8,128)(2,1)} %copy-done.16, bf16[64,1152]{1,0:T(8,128)(2,1)} %collective-permute-done.28.refs_2_, bf16[1,1024,768]{2,1,0:T(8,128)(2,1)} %refs_3_.7, bf16[1,1024,768]{2,1,0:T(8,128)(2,1)} %refs_4_.7, ...), custom_call_target="tpu_custom_call" | custom-call | flops 1207959552 | bytes 9437184 | tf_op jit(solution)/shard_map/run_experts/pallas_call | solution.py:389
  141.8 1.0 collective-permute-start.29
  142.9 0.7 copy-done.17
  143.5 6.8 %run_experts.5 = (f32[64,1024]{1,0:T(8,128)}, bf16[64,1024]{1,0:T(8,128)(2,1)}) custom-call(s32[2]{0:T(128)} %pad_add_fusion.refs_0_, bf16[64,1152]{1,0:T(8,128)(2,1)} %copy-done.15, bf16[64,1152]{1,0:T(8,128)(2,1)} %copy-done.17, bf16[1,1024,768]{2,1,0:T(8,128)(2,1)} %refs_3_.7, bf16[1,1024,768]{2,1,0:T(8,128)(2,1)} %refs_4_.7, ...), custom_call_target="tpu_custom_call" | custom-call | flops 1207959552 | bytes 9437184 | tf_op jit(solution)/shard_map/run_experts/pallas_call | solution.py:389
  150.3 1.1 collective-permute-start.25
  151.4 6.8 %run_experts.4 = (f32[64,1024]{1,0:T(8,128)}, bf16[64,1024]{1,0:T(8,128)(2,1)}) custom-call(s32[2]{0:T(128)} %pad_add_fusion.refs_0_, bf16[64,1152]{1,0:T(8,128)(2,1)} %get-tuple-element.80.refs_1_, bf16[64,1152]{1,0:T(8,128)(2,1)} %collective-permute-done.18.refs_2_, bf16[1,1024,768]{2,1,0:T(8,128)(2,1)} %refs_3_.7, bf16[1,1024,768]{2,1,0:T(8,128)(2,1)} %refs_4_.7, ...), custom_call_target="tpu_custom_call" | custom-call | flops 1207959552 | bytes 9437184 | tf_op jit(solution)/shard_map/run_experts/pallas_call | solution.py:389
  158.2 1.1 collective-permute-start.22
  159.3 1.1 collective-permute-start.34
  160.5 1.3 collective-permute-start.30
  161.8 2.6 %collective-permute-start.26 = (bf16[64,1024]{1,0:T(8,128)(2,1)S(1)}, bf16[64,1024]{1,0:T(8,128)(2,1)S(1)}, u32[]{:S(2)}, u32[]{:S(2)}) collective-permute-start(bf16[64,1024]{1,0:T(8,128)(2,1)S(1)} %add_convert_fusion.3), channel_id=1, source_target_pairs={{0,12},{1,13},{2,14},{3,15},{4,0},{5,1},{6,2},{7,3},{8,4},{9,5},{1... | collective-permute-start | bytes 393224 | tf_op jit(solution)/shard_map/ppermute | solution.py:433
  164.5 4.4 %collective-permute-done.34 = bf16[64,1024]{1,0:T(8,128)(2,1)S(1)} collective-permute-done((bf16[64,1024]{1,0:T(8,128)(2,1)S(1)}, bf16[64,1024]{1,0:T(8,128)(2,1)S(1)}, u32[]{:S(2)}, u32[]{:S(2)}) %collective-permute-start.34) | collective-permute-done | bytes 131104 | tf_op jit(solution)/shard_map/ppermute | solution.py:433
  168.9 0.5 collective-permute-done.26
  169.4 0.8 add_convert_fusion
  (96 shorter events, 1.7 us)
Async XLA Ops:
  0.0 6.0 %copy-start.2 = (bf16[64,2048]{1,0:T(8,128)(2,1)S(1)}, bf16[64,2048]{1,0:T(8,128)(2,1)}, u32[]{:S(2)}) copy-start(bf16[64,2048]{1,0:T(8,128)(2,1)} %refs_0_.15) | copy-start | bytes 786436
  0.0 6.0 %copy-start.22 = (s32[64,8]{0,1:T(8,128)S(1)}, s32[64,8]{0,1:T(8,128)}, u32[]{:S(2)}) copy-start(s32[64,8]{0,1:T(8,128)} %param.19) | copy-start | bytes 6148
  0.0 8.2 %copy-start.19 = (bf16[64,256]{1,0:T(8,128)(2,1)S(1)}, bf16[64,256]{1,0:T(8,128)(2,1)}, u32[]{:S(2)}) copy-start(bf16[64,256]{1,0:T(8,128)(2,1)} %param.18) | copy-start | bytes 98308
  0.0 11.6 %copy-start.20 = (bf16[64,256]{1,0:T(8,128)(2,1)S(1)}, bf16[64,256]{1,0:T(8,128)(2,1)}, u32[]{:S(2)}) copy-start(bf16[64,256]{1,0:T(8,128)(2,1)} %param.17) | copy-start | bytes 98308
  0.0 11.6 %copy-start.21 = (f32[64,8]{0,1:T(8,128)S(1)}, f32[64,8]{0,1:T(8,128)}, u32[]{:S(2)}) copy-start(f32[64,8]{0,1:T(8,128)} %param.24) | copy-start | bytes 6148
  0.0 31.4 %copy-start.23 = (s32[64,8]{0,1:T(8,128)S(1)}, s32[64,8]{0,1:T(8,128)}, u32[]{:S(2)}) copy-start(s32[64,8]{0,1:T(8,128)} %param.23) | copy-start | bytes 6148
  0.0 31.9 %copy-start = (bf16[1,1024,768]{2,1,0:T(8,128)(2,1)S(1)}, bf16[1,1024,768]{2,1,0:T(8,128)(2,1)}, u32[]{:S(2)}) copy-start(bf16[1,1024,768]{2,1,0:T(8,128)(2,1)} %refs_3_.7) | copy-start | bytes 4718596
  1.3 30.5 %copy-start.8 = (bf16[512,256]{1,0:T(8,128)(2,1)}, bf16[512,256]{1,0:T(8,128)(2,1)S(1)}, u32[]{:S(2)}) copy-start(bf16[512,256]{1,0:T(8,128)(2,1)S(1)} %pad_maximum_fusion.refs_5_) | copy-start | bytes 786436
  1.4 10.3 %collective-permute-start.2 = (bf16[512,256]{1,0:T(8,128)(2,1)S(1)}, bf16[512,256]{1,0:T(8,128)(2,1)S(1)}, u32[]{:S(2)}, u32[]{:S(2)}) collective-permute-start(bf16[512,256]{1,0:T(8,128)(2,1)S(1)} %pad_maximum_fusion.refs_5_), channel_id=1, source_target_pairs={{0,2},{1,3},{2,0},{3,1},{4,6},{5,7},{6,4},{7,5},{8,10},{9,11},{10,... | collective-permute-start | bytes 786440 | tf_op jit(solution)/shard_map/ppermute | solution.py:433
  4.4 11.2 %collective-permute-start.4 = (bf16[512,256]{1,0:T(8,128)(2,1)S(1)}, bf16[512,256]{1,0:T(8,128)(2,1)}, u32[]{:S(2)}, u32[]{:S(2)}) collective-permute-start(bf16[512,256]{1,0:T(8,128)(2,1)S(1)} %pad_maximum_fusion.refs_5_), channel_id=1, source_target_pairs={{0,4},{1,5},{2,6},{3,7},{4,8},{5,9},{6,10},{7,11},{8,12},{9,13},{1... | collective-permute-start | bytes 786440 | tf_op jit(solution)/shard_map/ppermute | solution.py:433
  6.0 4.5 %collective-permute-start = (bf16[64,2048]{1,0:T(8,128)(2,1)S(1)}, bf16[64,2048]{1,0:T(8,128)(2,1)S(1)}, u32[]{:S(2)}, u32[]{:S(2)}) collective-permute-start(bf16[64,2048]{1,0:T(8,128)(2,1)S(1)} %copy-done.2), channel_id=1, source_target_pairs={{0,1},{1,0},{2,3},{3,2},{4,5},{5,4},{6,7},{7,6},{8,9},{9,8},{10,11... | collective-permute-start | bytes 786440 | tf_op jit(solution)/shard_map/ppermute | solution.py:433
  6.0 2.2 %collective-permute-start.1 = (s32[64,8]{0,1:T(8,128)S(1)}, s32[64,8]{0,1:T(8,128)S(1)}, u32[]{:S(2)}, u32[]{:S(2)}) collective-permute-start(s32[64,8]{0,1:T(8,128)S(1)} %copy-done.22), channel_id=1, source_target_pairs={{0,1},{1,0},{2,3},{3,2},{4,5},{5,4},{6,7},{7,6},{8,9},{9,8},{10,11... | collective-permute-start | bytes 6152 | tf_op jit(solution)/shard_map/ppermute | solution.py:433
  6.5 25.4 %copy-start.9 = (bf16[512,256]{1,0:T(8,128)(2,1)}, bf16[512,256]{1,0:T(8,128)(2,1)S(1)}, u32[]{:S(2)}) copy-start(bf16[512,256]{1,0:T(8,128)(2,1)S(1)} %pad_maximum_fusion.1.refs_6_) | copy-start | bytes 786436
  6.5 14.6 %collective-permute-start.5 = (bf16[512,256]{1,0:T(8,128)(2,1)S(1)}, bf16[512,256]{1,0:T(8,128)(2,1)}, u32[]{:S(2)}, u32[]{:S(2)}) collective-permute-start(bf16[512,256]{1,0:T(8,128)(2,1)S(1)} %pad_maximum_fusion.1.refs_6_), channel_id=1, source_target_pairs={{0,4},{1,5},{2,6},{3,7},{4,8},{5,9},{6,10},{7,11},{8,12},{9,13},{1... | collective-permute-start | bytes 786440 | tf_op jit(solution)/shard_map/ppermute | solution.py:433
  8.2 17.3 %collective-permute-start.8 = (bf16[512,256]{1,0:T(8,128)(2,1)S(1)}, bf16[512,256]{1,0:T(8,128)(2,1)}, u32[]{:S(2)}, u32[]{:S(2)}) collective-permute-start(bf16[512,256]{1,0:T(8,128)(2,1)S(1)} %pad_maximum_fusion.refs_5_), channel_id=1, source_target_pairs={{0,12},{1,13},{2,14},{3,15},{4,0},{5,1},{6,2},{7,3},{8,4},{9,5},{1... | collective-permute-start | bytes 786440 | tf_op jit(solution)/shard_map/ppermute | solution.py:433
  10.5 21.4 %copy-start.3 = (bf16[64,2048]{1,0:T(8,128)(2,1)}, bf16[64,2048]{1,0:T(8,128)(2,1)S(1)}, u32[]{:S(2)}) copy-start(bf16[64,2048]{1,0:T(8,128)(2,1)S(1)} %collective-permute-done.refs_1_) | copy-start | bytes 786436
  10.5 20.4 %collective-permute-start.9 = (bf16[512,256]{1,0:T(8,128)(2,1)S(1)}, bf16[512,256]{1,0:T(8,128)(2,1)S(1)}, u32[]{:S(2)}, u32[]{:S(2)}) collective-permute-start(bf16[512,256]{1,0:T(8,128)(2,1)S(1)} %pad_maximum_fusion.1.refs_6_), channel_id=1, source_target_pairs={{0,12},{1,13},{2,14},{3,15},{4,0},{5,1},{6,2},{7,3},{8,4},{9,5},{1... | collective-permute-start | bytes 786440 | tf_op jit(solution)/shard_map/ppermute | solution.py:433
  11.6 20.3 %copy-start.5 = (bf16[512,256]{1,0:T(8,128)(2,1)}, bf16[512,256]{1,0:T(8,128)(2,1)S(1)}, u32[]{:S(2)}) copy-start(bf16[512,256]{1,0:T(8,128)(2,1)S(1)} %collective-permute-done.2.refs_7_) | copy-start | bytes 786436
  11.6 20.3 %collective-permute-start.3 = (bf16[512,256]{1,0:T(8,128)(2,1)S(1)}, bf16[512,256]{1,0:T(8,128)(2,1)}, u32[]{:S(2)}, u32[]{:S(2)}) collective-permute-start(bf16[512,256]{1,0:T(8,128)(2,1)S(1)} %pad_maximum_fusion.1.refs_6_), channel_id=1, source_target_pairs={{0,2},{1,3},{2,0},{3,1},{4,6},{5,7},{6,4},{7,5},{8,10},{9,11},{10,... | collective-permute-start | bytes 786440 | tf_op jit(solution)/shard_map/ppermute | solution.py:433
  15.6 16.4 %collective-permute-start.6 = (bf16[512,256]{1,0:T(8,128)(2,1)}, bf16[512,256]{1,0:T(8,128)(2,1)}, u32[]{:S(2)}, u32[]{:S(2)}) collective-permute-start(bf16[512,256]{1,0:T(8,128)(2,1)} %collective-permute-done.4.refs_7_), channel_id=1, source_target_pairs={{0,2},{1,3},{2,0},{3,1},{4,6},{5,7},{6,4},{7,5},{8,10},{9,11},{10,... | collective-permute-start | bytes 786440 | tf_op jit(solution)/shard_map/ppermute | solution.py:433
  21.1 11.4 %collective-permute-start.7 = (bf16[512,256]{1,0:T(8,128)(2,1)}, bf16[512,256]{1,0:T(8,128)(2,1)}, u32[]{:S(2)}, u32[]{:S(2)}) collective-permute-start(bf16[512,256]{1,0:T(8,128)(2,1)} %collective-permute-done.5.refs_8_), channel_id=1, source_target_pairs={{0,2},{1,3},{2,0},{3,1},{4,6},{5,7},{6,4},{7,5},{8,10},{9,11},{10,... | collective-permute-start | bytes 786440 | tf_op jit(solution)/shard_map/ppermute | solution.py:433
  25.5 12.4 %collective-permute-start.10 = (bf16[512,256]{1,0:T(8,128)(2,1)}, bf16[512,256]{1,0:T(8,128)(2,1)}, u32[]{:S(2)}, u32[]{:S(2)}) collective-permute-start(bf16[512,256]{1,0:T(8,128)(2,1)} %collective-permute-done.8.refs_7_), channel_id=1, source_target_pairs={{0,2},{1,3},{2,0},{3,1},{4,6},{5,7},{6,4},{7,5},{8,10},{9,11},{10,... | collective-permute-start | bytes 786440 | tf_op jit(solution)/shard_map/ppermute | solution.py:433
  30.9 29.4 %copy-start.6 = (bf16[512,256]{1,0:T(8,128)(2,1)}, bf16[512,256]{1,0:T(8,128)(2,1)S(1)}, u32[]{:S(2)}) copy-start(bf16[512,256]{1,0:T(8,128)(2,1)S(1)} %collective-permute-done.9.refs_8_) | copy-start | bytes 786436
  30.9 11.2 %collective-permute-start.11 = (bf16[512,256]{1,0:T(8,128)(2,1)S(1)}, bf16[512,256]{1,0:T(8,128)(2,1)}, u32[]{:S(2)}, u32[]{:S(2)}) collective-permute-start(bf16[512,256]{1,0:T(8,128)(2,1)S(1)} %collective-permute-done.9.refs_8_), channel_id=1, source_target_pairs={{0,2},{1,3},{2,0},{3,1},{4,6},{5,7},{6,4},{7,5},{8,10},{9,11},{10,... | collective-permute-start | bytes 786440 | tf_op jit(solution)/shard_map/ppermute | solution.py:433
  31.9 94.1 %collective-permute-start.19 = (bf16[1,1024,768]{2,1,0:T(8,128)(2,1)S(1)}, bf16[1,1024,768]{2,1,0:T(8,128)(2,1)S(1)}, u32[]{:S(2)}, u32[]{:S(2)}) collective-permute-start(bf16[1,1024,768]{2,1,0:T(8,128)(2,1)S(1)} %copy-done), channel_id=1, source_target_pairs={{0,1},{1,0},{2,3},{3,2},{4,5},{5,4},{6,7},{7,6},{8,9},{9,8},{10,11... | collective-permute-start | bytes 4718600 | tf_op jit(solution)/shard_map/ppermute | solution.py:433
  32.0 95.0 %collective-permute-start.20 = (bf16[1,1024,768]{2,1,0:T(8,128)(2,1)}, bf16[1,1024,768]{2,1,0:T(8,128)(2,1)}, u32[]{:S(2)}, u32[]{:S(2)}) collective-permute-start(bf16[1,1024,768]{2,1,0:T(8,128)(2,1)} %refs_4_.7), channel_id=1, source_target_pairs={{0,1},{1,0},{2,3},{3,2},{4,5},{5,4},{6,7},{7,6},{8,9},{9,8},{10,11... | collective-permute-start | bytes 4718600 | tf_op jit(solution)/shard_map/ppermute | solution.py:433
  32.5 94.5 %collective-permute-start.21 = (bf16[1,768,1024]{2,1,0:T(8,128)(2,1)}, bf16[1,768,1024]{2,1,0:T(8,128)(2,1)}, u32[]{:S(2)}, u32[]{:S(2)}) collective-permute-start(bf16[1,768,1024]{2,1,0:T(8,128)(2,1)} %refs_5_.7), channel_id=1, source_target_pairs={{0,1},{1,0},{2,3},{3,2},{4,5},{5,4},{6,7},{7,6},{8,9},{9,8},{10,11... | collective-permute-start | bytes 4718600 | tf_op jit(solution)/shard_map/ppermute | solution.py:433
  37.8 11.9 %collective-permute-start.12 = (bf16[512,256]{1,0:T(8,128)(2,1)}, bf16[512,256]{1,0:T(8,128)(2,1)}, u32[]{:S(2)}, u32[]{:S(2)}) collective-permute-start(bf16[512,256]{1,0:T(8,128)(2,1)} %collective-permute-done.4.refs_7_), channel_id=1, source_target_pairs={{0,4},{1,5},{2,6},{3,7},{4,8},{5,9},{6,10},{7,11},{8,12},{9,13},{1... | collective-permute-start | bytes 786440 | tf_op jit(solution)/shard_map/ppermute | solution.py:433
  42.1 11.2 %collective-permute-start.13 = (bf16[512,256]{1,0:T(8,128)(2,1)}, bf16[512,256]{1,0:T(8,128)(2,1)}, u32[]{:S(2)}, u32[]{:S(2)}) collective-permute-start(bf16[512,256]{1,0:T(8,128)(2,1)} %collective-permute-done.5.refs_8_), channel_id=1, source_target_pairs={{0,4},{1,5},{2,6},{3,7},{4,8},{5,9},{6,10},{7,11},{8,12},{9,13},{1... | collective-permute-start | bytes 786440 | tf_op jit(solution)/shard_map/ppermute | solution.py:433
  42.6 0.6 copy-start.4
  49.7 41.5 %collective-permute-start.14 = (bf16[512,256]{1,0:T(8,128)(2,1)}, bf16[512,256]{1,0:T(8,128)(2,1)}, u32[]{:S(2)}, u32[]{:S(2)}) collective-permute-start(bf16[512,256]{1,0:T(8,128)(2,1)} %collective-permute-done.12.refs_7_), channel_id=1, source_target_pairs={{0,2},{1,3},{2,0},{3,1},{4,6},{5,7},{6,4},{7,5},{8,10},{9,11},{10,... | collective-permute-start | bytes 786440 | tf_op jit(solution)/shard_map/ppermute | solution.py:433
  53.3 37.9 %collective-permute-start.15 = (bf16[512,256]{1,0:T(8,128)(2,1)}, bf16[512,256]{1,0:T(8,128)(2,1)}, u32[]{:S(2)}, u32[]{:S(2)}) collective-permute-start(bf16[512,256]{1,0:T(8,128)(2,1)} %collective-permute-done.13.refs_8_), channel_id=1, source_target_pairs={{0,2},{1,3},{2,0},{3,1},{4,6},{5,7},{6,4},{7,5},{8,10},{9,11},{10,... | collective-permute-start | bytes 786440 | tf_op jit(solution)/shard_map/ppermute | solution.py:433
  97.3 1.8 %collective-permute-start.17 = (bf16[128,1024]{1,0:T(8,128)(2,1)}, bf16[128,1024]{1,0:T(8,128)(2,1)S(1)}, u32[]{:S(2)}, u32[]{:S(2)}) collective-permute-start(bf16[128,1024]{1,0:T(8,128)(2,1)} %get-tuple-element.78), channel_id=1, source_target_pairs={{0,1},{1,0},{2,3},{3,2},{4,5},{5,4},{6,7},{7,6},{8,9},{9,8},{10,11... | collective-permute-start | bytes 786440 | tf_op jit(solution)/shard_map/ppermute | solution.py:433
  97.3 1.8 %collective-permute-start.16 = (f32[8,1024]{1,0:T(8,128)}, f32[8,1024]{1,0:T(8,128)S(1)}, u32[]{:S(2)}, u32[]{:S(2)}) collective-permute-start(f32[8,1024]{1,0:T(8,128)} %get-tuple-element.77), channel_id=1, source_target_pairs={{0,1},{1,0},{2,3},{3,2},{4,5},{5,4},{6,7},{7,6},{8,9},{9,8},{10,11... | collective-permute-start | bytes 98312 | tf_op jit(solution)/shard_map/ppermute | solution.py:433
  99.1 0.6 copy-start.18
  99.1 0.7 copy-start.7
  104.0 9.5 %collective-permute-start.31 = (bf16[64,1152]{1,0:T(8,128)(2,1)}, bf16[64,1152]{1,0:T(8,128)(2,1)}, u32[]{:S(2)}, u32[]{:S(2)}) collective-permute-start(bf16[64,1152]{1,0:T(8,128)(2,1)} %get-tuple-element.80.refs_1_), channel_id=1, source_target_pairs={{0,8},{1,9},{2,10},{3,11},{4,12},{5,13},{6,14},{7,15},{8,0},{9,1},... | collective-permute-start | bytes 442376 | tf_op jit(solution)/shard_map/ppermute | solution.py:433
  104.9 11.5 %collective-permute-start.27 = (bf16[64,1152]{1,0:T(8,128)(2,1)}, bf16[64,1152]{1,0:T(8,128)(2,1)S(1)}, u32[]{:S(2)}, u32[]{:S(2)}) collective-permute-start(bf16[64,1152]{1,0:T(8,128)(2,1)} %get-tuple-element.80.refs_1_), channel_id=1, source_target_pairs={{0,12},{1,13},{2,14},{3,15},{4,0},{5,1},{6,2},{7,3},{8,4},{9,5},{1... | collective-permute-start | bytes 442376 | tf_op jit(solution)/shard_map/ppermute | solution.py:433
  113.5 9.9 %collective-permute-start.23 = (bf16[64,1152]{1,0:T(8,128)(2,1)}, bf16[64,1152]{1,0:T(8,128)(2,1)S(1)}, u32[]{:S(2)}, u32[]{:S(2)}) collective-permute-start(bf16[64,1152]{1,0:T(8,128)(2,1)} %get-tuple-element.80.refs_1_), channel_id=1, source_target_pairs={{0,4},{1,5},{2,6},{3,7},{4,8},{5,9},{6,10},{7,11},{8,12},{9,13},{1... | collective-permute-start | bytes 442376 | tf_op jit(solution)/shard_map/ppermute | solution.py:433
  116.4 17.6 %copy-start.16 = (bf16[64,1152]{1,0:T(8,128)(2,1)}, bf16[64,1152]{1,0:T(8,128)(2,1)S(1)}, u32[]{:S(2)}) copy-start(bf16[64,1152]{1,0:T(8,128)(2,1)S(1)} %collective-permute-done.27.refs_1_) | copy-start | bytes 442372
  116.4 8.6 %collective-permute-start.32 = (bf16[64,1152]{1,0:T(8,128)(2,1)}, bf16[64,1152]{1,0:T(8,128)(2,1)}, u32[]{:S(2)}, u32[]{:S(2)}) collective-permute-start(bf16[64,1152]{1,0:T(8,128)(2,1)} %collective-permute-done.31.refs_1_), channel_id=1, source_target_pairs={{0,2},{1,3},{2,0},{3,1},{4,6},{5,7},{6,4},{7,5},{8,10},{9,11},{10,... | collective-permute-start | bytes 442376 | tf_op jit(solution)/shard_map/ppermute | solution.py:433
  123.4 10.6 %copy-start.15 = (bf16[64,1152]{1,0:T(8,128)(2,1)}, bf16[64,1152]{1,0:T(8,128)(2,1)S(1)}, u32[]{:S(2)}) copy-start(bf16[64,1152]{1,0:T(8,128)(2,1)S(1)} %collective-permute-done.23.refs_1_) | copy-start | bytes 442372
  123.4 11.6 %collective-permute-start.28 = (bf16[64,1152]{1,0:T(8,128)(2,1)S(1)}, bf16[64,1152]{1,0:T(8,128)(2,1)}, u32[]{:S(2)}, u32[]{:S(2)}) collective-permute-start(bf16[64,1152]{1,0:T(8,128)(2,1)S(1)} %collective-permute-done.27.refs_1_), channel_id=1, source_target_pairs={{0,2},{1,3},{2,0},{3,1},{4,6},{5,7},{6,4},{7,5},{8,10},{9,11},{10,... | collective-permute-start | bytes 442376 | tf_op jit(solution)/shard_map/ppermute | solution.py:433
  125.0 26.4 %collective-permute-start.18 = (bf16[64,1152]{1,0:T(8,128)(2,1)}, bf16[64,1152]{1,0:T(8,128)(2,1)}, u32[]{:S(2)}, u32[]{:S(2)}) collective-permute-start(bf16[64,1152]{1,0:T(8,128)(2,1)} %get-tuple-element.80.refs_1_), channel_id=1, source_target_pairs={{0,2},{1,3},{2,0},{3,1},{4,6},{5,7},{6,4},{7,5},{8,10},{9,11},{10,... | collective-permute-start | bytes 442376 | tf_op jit(solution)/shard_map/ppermute | solution.py:433
  126.0 1.2 copy-start.1
  126.0 16.9 %collective-permute-start.24 = (bf16[64,1152]{1,0:T(8,128)(2,1)S(1)}, bf16[64,1152]{1,0:T(8,128)(2,1)S(1)}, u32[]{:S(2)}, u32[]{:S(2)}) collective-permute-start(bf16[64,1152]{1,0:T(8,128)(2,1)S(1)} %collective-permute-done.23.refs_1_), channel_id=1, source_target_pairs={{0,2},{1,3},{2,0},{3,1},{4,6},{5,7},{6,4},{7,5},{8,10},{9,11},{10,... | collective-permute-start | bytes 442376 | tf_op jit(solution)/shard_map/ppermute | solution.py:433
  134.0 25.3 %collective-permute-start.33 = (bf16[64,1024]{1,0:T(8,128)(2,1)}, bf16[64,1024]{1,0:T(8,128)(2,1)S(1)}, u32[]{:S(2)}, u32[]{:S(2)}) collective-permute-start(bf16[64,1024]{1,0:T(8,128)(2,1)} %get-tuple-element.88), channel_id=1, source_target_pairs={{0,2},{1,3},{2,0},{3,1},{4,6},{5,7},{6,4},{7,5},{8,10},{9,11},{10,... | collective-permute-start | bytes 393224 | tf_op jit(solution)/shard_map/ppermute | solution.py:433
  141.8 18.6 %collective-permute-start.29 = (bf16[64,1024]{1,0:T(8,128)(2,1)}, bf16[64,1024]{1,0:T(8,128)(2,1)S(1)}, u32[]{:S(2)}, u32[]{:S(2)}) collective-permute-start(bf16[64,1024]{1,0:T(8,128)(2,1)} %get-tuple-element.86), channel_id=1, source_target_pairs={{0,2},{1,3},{2,0},{3,1},{4,6},{5,7},{6,4},{7,5},{8,10},{9,11},{10,... | collective-permute-start | bytes 393224 | tf_op jit(solution)/shard_map/ppermute | solution.py:433
  142.9 0.7 copy-start.17
  150.3 9.0 %copy-start.10 = (f32[64,1024]{1,0:T(8,128)S(1)}, f32[64,1024]{1,0:T(8,128)}, u32[]{:S(2)}) copy-start(f32[64,1024]{1,0:T(8,128)} %get-tuple-element.87) | copy-start | bytes 786436
  150.3 10.2 %copy-start.11 = (f32[64,1024]{1,0:T(8,128)S(1)}, f32[64,1024]{1,0:T(8,128)}, u32[]{:S(2)}) copy-start(f32[64,1024]{1,0:T(8,128)} %get-tuple-element.85) | copy-start | bytes 786436
  150.3 11.5 %copy-start.12 = (f32[64,1024]{1,0:T(8,128)S(1)}, f32[64,1024]{1,0:T(8,128)}, u32[]{:S(2)}) copy-start(f32[64,1024]{1,0:T(8,128)} %get-tuple-element.83) | copy-start | bytes 786436
  150.3 11.5 %collective-permute-start.25 = (bf16[64,1024]{1,0:T(8,128)(2,1)}, bf16[64,1024]{1,0:T(8,128)(2,1)S(1)}, u32[]{:S(2)}, u32[]{:S(2)}) collective-permute-start(bf16[64,1024]{1,0:T(8,128)(2,1)} %get-tuple-element.84), channel_id=1, source_target_pairs={{0,2},{1,3},{2,0},{3,1},{4,6},{5,7},{6,4},{7,5},{8,10},{9,11},{10,... | collective-permute-start | bytes 393224 | tf_op jit(solution)/shard_map/ppermute | solution.py:433
  158.2 11.2 %copy-start.13 = (f32[64,1024]{1,0:T(8,128)S(1)}, f32[64,1024]{1,0:T(8,128)}, u32[]{:S(2)}) copy-start(f32[64,1024]{1,0:T(8,128)} %get-tuple-element.79) | copy-start | bytes 786436
  158.2 11.2 %copy-start.14 = (f32[64,1024]{1,0:T(8,128)S(1)}, f32[64,1024]{1,0:T(8,128)}, u32[]{:S(2)}) copy-start(f32[64,1024]{1,0:T(8,128)} %get-tuple-element.81) | copy-start | bytes 786436
  158.2 6.3 %collective-permute-start.22 = (bf16[64,1024]{1,0:T(8,128)(2,1)}, bf16[64,1024]{1,0:T(8,128)(2,1)S(1)}, u32[]{:S(2)}, u32[]{:S(2)}) collective-permute-start(bf16[64,1024]{1,0:T(8,128)(2,1)} %get-tuple-element.82), channel_id=1, source_target_pairs={{0,2},{1,3},{2,0},{3,1},{4,6},{5,7},{6,4},{7,5},{8,10},{9,11},{10,... | collective-permute-start | bytes 393224 | tf_op jit(solution)/shard_map/ppermute | solution.py:433
  159.3 9.6 %collective-permute-start.34 = (bf16[64,1024]{1,0:T(8,128)(2,1)S(1)}, bf16[64,1024]{1,0:T(8,128)(2,1)S(1)}, u32[]{:S(2)}, u32[]{:S(2)}) collective-permute-start(bf16[64,1024]{1,0:T(8,128)(2,1)S(1)} %add_convert_fusion.1), channel_id=1, source_target_pairs={{0,8},{1,9},{2,10},{3,11},{4,12},{5,13},{6,14},{7,15},{8,0},{9,1},... | collective-permute-start | bytes 393224 | tf_op jit(solution)/shard_map/ppermute | solution.py:433
  160.5 8.4 %collective-permute-start.30 = (bf16[64,1024]{1,0:T(8,128)(2,1)S(1)}, bf16[64,1024]{1,0:T(8,128)(2,1)S(1)}, u32[]{:S(2)}, u32[]{:S(2)}) collective-permute-start(bf16[64,1024]{1,0:T(8,128)(2,1)S(1)} %add_convert_fusion.2), channel_id=1, source_target_pairs={{0,4},{1,5},{2,6},{3,7},{4,8},{5,9},{6,10},{7,11},{8,12},{9,13},{1... | collective-permute-start | bytes 393224 | tf_op jit(solution)/shard_map/ppermute | solution.py:433
  161.8 7.6 %collective-permute-start.26 = (bf16[64,1024]{1,0:T(8,128)(2,1)S(1)}, bf16[64,1024]{1,0:T(8,128)(2,1)S(1)}, u32[]{:S(2)}, u32[]{:S(2)}) collective-permute-start(bf16[64,1024]{1,0:T(8,128)(2,1)S(1)} %add_convert_fusion.3), channel_id=1, source_target_pairs={{0,12},{1,13},{2,14},{3,15},{4,0},{5,1},{6,2},{7,3},{8,4},{9,5},{1... | collective-permute-start | bytes 393224 | tf_op jit(solution)/shard_map/ppermute | solution.py:433

commit v3 on v2

--- a/solution.py
+++ b/solution.py
@@ -4,6 +4,7 @@
 from jax.experimental import pallas as pl
 from jax.experimental.pallas import tpu as pltpu
 from jax.sharding import PartitionSpec as P
+
 
 QUERY_HEADS = 16
 KEY_VALUE_HEADS = 2
@@ -184,6 +185,9 @@
 LANES = 128
 TILE = 256
 ONES_ROWS = 16
+PIECE = 256
+MIX_PIECE = 512
+KERNEL_BYTES = 20 << 20
 
 
 def grid_of(parties):
@@ -194,6 +198,10 @@
     return (chips // across, across)
 
 
+def visiting_order(deep):
+    return [0] + [d for k in range(1, deep // 2 + 1) for d in sorted({k, deep - k})]
+
+
 def gathers(mesh):
     return mesh.shape["blk"] <= 4 * TOPB and mesh.shape["blk"] % CORES == 0
 
@@ -215,13 +223,15 @@
     queries = refs[0:2]
     chosen_ref = refs[2]
     given = None if first else refs[3:7]
-    block_refs = refs[-4 - count : -4]
-    stats_refs = refs[-4:-2]
-    out_refs = refs[-2:]
+    block_refs = refs[-6 - count : -6]
+    stats_refs = refs[-6:-4]
+    out_refs = refs[-4:-2]
+    score_refs = refs[-2:]
     tokens = queries[0].shape[0]
     per_tile = TILE // tokens
     heads_per_group = QUERY_HEADS // KEY_VALUE_HEADS
     factor = HEAD_SIZE ** (-0.5) * LOG2_E
+    tasks = []
     for group in range(KEY_VALUE_HEADS):
         mine = []
         for (of_group, column), block_ref in zip(pieces, block_refs):
@@ -232,53 +242,77 @@
         for owner in range(2):
             for tile in range(heads_per_group // per_tile):
                 head = group * heads_per_group + tile * per_tile
-                at = slice(head * tokens, head * tokens + TILE)
-                rows = jnp.concatenate(
-                    [
-                        queries[owner][:, h * HEAD_SIZE : (h + 1) * HEAD_SIZE]
-                        for h in range(head, head + per_tile)
-                    ],
-                    axis=0,
-                )
-                if first:
-                    top = jnp.full((1, TILE), UNSEEN, jnp.float32)
-                    total = jnp.zeros((1, TILE), jnp.float32)
-                    out = jnp.zeros((HEAD_SIZE, TILE), jnp.float32)
-                else:
-                    top = given[owner][0:1, at]
-                    total = given[owner][1:2, at]
-                    out = given[2 + owner][:, at].astype(jnp.float32)
-                for column, block_ref, mixer in mine:
-                    if column is None and owner:
-                        continue
-                    scores = lax.dot_general(
-                        block_ref[:, :HEAD_SIZE],
-                        rows,
-                        (((1,), (1,)), ((), ())),
-                        preferred_element_type=jnp.float32,
-                    )
-                    if column is None:
-                        key = lax.broadcasted_iota(jnp.int32, scores.shape, 0)
-                        token = lax.broadcasted_iota(jnp.int32, scores.shape, 1) % tokens
-                        scores = jnp.where(key <= token, scores, -SKIPPED)
-                        high = jnp.maximum(top, jnp.max(scores, axis=0, keepdims=True) * factor)
-                        shift = high
-                    else:
-                        chosen = chosen_ref[
-                            column : column + 1, owner * TILE : (owner + 1) * TILE
-                        ]
-                        high = jnp.max(scores, axis=0, keepdims=True) * factor
-                        high = jnp.maximum(top, jnp.where(chosen > 0.5, high, UNSEEN))
-                        shift = jnp.where(chosen > 0.5, high, SKIPPED)
-                    weights = jnp.exp2(scores * factor - shift).astype(jnp.bfloat16)
-                    mixed = jnp.dot(mixer, weights, preferred_element_type=jnp.float32)
-                    fade = jnp.exp2(top - high)
-                    out = out * fade + mixed[:HEAD_SIZE]
-                    total = total * fade + mixed[HEAD_SIZE : HEAD_SIZE + 1]
-                    top = high
-                stats_refs[owner][0:1, at] = top
-                stats_refs[owner][1:2, at] = total
-                out_refs[owner][:, at] = out.astype(out_refs[owner].dtype)
+                tasks += [
+                    (owner, head, column, block_ref, mixer)
+                    for column, block_ref, mixer in mine
+                    if not (column is None and owner)
+                ]
+
+    def score(number):
+        owner, head, column, block_ref, _ = tasks[number]
+        rows = jnp.concatenate(
+            [
+                queries[owner][:, h * HEAD_SIZE : (h + 1) * HEAD_SIZE]
+                for h in range(head, head + per_tile)
+            ],
+            axis=0,
+        )
+        keys = block_ref.shape[0]
+        high = None
+        for low in range(0, keys, PIECE):
+            cut = slice(low, min(low + PIECE, keys))
+            scores = lax.dot_general(
+                block_ref[cut, :HEAD_SIZE],
+                rows,
+                (((1,), (1,)), ((), ())),
+                preferred_element_type=jnp.float32,
+            )
+            if column is None:
+                key = lax.broadcasted_iota(jnp.int32, scores.shape, 0) + low
+                token = lax.broadcasted_iota(jnp.int32, scores.shape, 1) % tokens
+                scores = jnp.where(key <= token, scores, -SKIPPED)
+            score_refs[number % 2][cut, :] = scores
+            part = jnp.max(scores, axis=0, keepdims=True)
+            high = part if high is None else jnp.maximum(high, part)
+        return high * factor
+
+    seen = set()
+    high = score(0)
+    for number, (owner, head, column, block_ref, mixer) in enumerate(tasks):
+        following = score(number + 1) if number + 1 < len(tasks) else None
+        at = slice(head * tokens, head * tokens + TILE)
+        if (owner, head) in seen:
+            source = (stats_refs[owner], out_refs[owner])
+        elif first:
+            source = None
+        else:
+            source = (given[owner], given[2 + owner])
+        seen.add((owner, head))
+        top = source[0][0:1, at] if source else jnp.full((1, TILE), UNSEEN, jnp.float32)
+        if column is None:
+            high = jnp.maximum(top, high)
+            shift = high
+        else:
+            chosen = chosen_ref[column : column + 1, owner * TILE : (owner + 1) * TILE] > 0.5
+            high = jnp.maximum(top, jnp.where(chosen, high, UNSEEN))
+            shift = jnp.where(chosen, high, SKIPPED)
+        mixed = None
+        keys = block_ref.shape[0]
+        for low in range(0, keys, MIX_PIECE):
+            cut = slice(low, min(low + MIX_PIECE, keys))
+            scores = score_refs[number % 2][cut, :]
+            weights = jnp.exp2(scores * factor - shift).astype(jnp.bfloat16)
+            part = jnp.dot(mixer[:, cut], weights, preferred_element_type=jnp.float32)
+            mixed = part if mixed is None else mixed + part
+        out, total = mixed[:HEAD_SIZE], mixed[HEAD_SIZE : HEAD_SIZE + 1]
+        if source:
+            fade = jnp.exp2(top - high)
+            out = source[1][:, at].astype(jnp.float32) * fade + out
+            total = source[0][1:2, at] * fade + total
+        stats_refs[owner][0:1, at] = high
+        stats_refs[owner][1:2, at] = total
+        out_refs[owner][:, at] = out.astype(out_refs[owner].dtype)
+        high = following
 
 
 def attend(queries, chosen, state, pieces, blocks, last=False):
@@ -292,11 +326,13 @@
     return pl.pallas_call(
         lambda *refs: attention_kernel(pieces, state is None, count, *refs),
         out_shape=(stats, stats, out, sent if last else out),
+        scratch_shapes=[pltpu.VMEM((max(b.shape[0] for b in blocks), TILE), jnp.float32)] * 2,
         cost_estimate=pl.CostEstimate(
             flops=4 * keys * span * HEAD_SIZE,
             bytes_accessed=16 * HEAD_SIZE * span + keys * HEAD_SIZE * 4,
             transcendentals=keys * span,
         ),
+        compiler_params=pltpu.CompilerParams(vmem_limit_bytes=KERNEL_BYTES),
         name="attend_blocks",
     )(*queries, chosen, *(state or ()), *blocks)
 
@@ -343,9 +379,7 @@
     who_ref = refs[0]
     row_refs = refs[1 : 1 + rows_count]
     weight_refs = refs[1 + rows_count : 7 + rows_count]
-    out_refs = refs[7 + rows_count : 7 + 2 * rows_count]
-    (sum_ref,) = refs[7 + 2 * rows_count :]
-    step = pl.program_id(0)
+    out_refs = refs[7 + rows_count :]
     tokens, width = out_refs[0].shape
     block = jnp.concatenate([r[...] for r in row_refs], axis=0)
     inputs = block[:, :width]
@@ -354,52 +388,36 @@
     result = None
     for slot in range(2):
         gate_ref, up_ref, down_ref = weight_refs[3 * slot : 3 * slot + 3]
-        expert = who_ref[slot]
-        here = (lane == expert) | (lane == expert + parties)
+        here = (lane == who_ref[slot]) | (lane == who_ref[slot] + parties)
         weight = jnp.sum(jnp.where(here, extra, 0.0), axis=1, keepdims=True)
-        gate = jnp.dot(inputs, gate_ref[0], preferred_element_type=jnp.float32)
-        up = jnp.dot(inputs, up_ref[0], preferred_element_type=jnp.float32)
-        inner = (gate / (1.0 + jnp.exp(-gate)) * up).astype(jnp.bfloat16)
-        part = weight * jnp.dot(inner, down_ref[0], preferred_element_type=jnp.float32)
+        inner = []
+        for low in range(0, gate_ref.shape[2], TILE):
+            cut = slice(low, low + TILE)
+            gate = jnp.dot(inputs, gate_ref[0, :, cut], preferred_element_type=jnp.float32)
+            up = jnp.dot(inputs, up_ref[0, :, cut], preferred_element_type=jnp.float32)
+            inner.append((gate / (1.0 + jnp.exp(-gate)) * up).astype(jnp.bfloat16))
+        part = weight * jnp.dot(
+            jnp.concatenate(inner, axis=1), down_ref[0], preferred_element_type=jnp.float32
+        )
         result = part if result is None else result + part
-
-    @pl.when(step == 0)
-    def _():
-        sum_ref[...] = result
-
-    @pl.when(step > 0)
-    def _():
-        sum_ref[...] += result
-
-    @pl.when(step == pl.num_programs(0) - 1)
-    def _():
-        for n, out_ref in enumerate(out_refs):
-            out_ref[...] = sum_ref[n * tokens : (n + 1) * tokens, :].astype(out_ref.dtype)
+    for n, out_ref in enumerate(out_refs):
+        out_ref[...] = result[n * tokens : (n + 1) * tokens, :].astype(out_ref.dtype)
 
 
 def run_experts(parties, who, rows, weights, out_types):
-    tokens, packed_width = rows[0].shape
-    width = weights[0].shape[1]
-    hidden = weights[0].shape[2]
-    step = 2 * LANES
-    whole = pl.BlockSpec((tokens, packed_width), lambda f: (0, 0))
-    out = pl.BlockSpec((tokens, width), lambda f: (0, 0))
-    into = pl.BlockSpec((1, width, step), lambda f: (0, 0, f))
-    back = pl.BlockSpec((1, step, width), lambda f: (0, f, 0))
+    tokens = rows[0].shape[0]
+    _, width, hidden = weights[0].shape
+    vmem = pl.BlockSpec(memory_space=pltpu.VMEM)
     return pl.pallas_call(
         lambda *refs: expert_kernel(parties, len(rows), *refs),
-        grid=(hidden // step,),
-        in_specs=[pl.BlockSpec(memory_space=pltpu.SMEM)]
-        + [whole] * len(rows)
-        + [into, into, back] * 2,
-        out_specs=[out] * len(rows),
+        in_specs=[pl.BlockSpec(memory_space=pltpu.SMEM)] + [vmem] * (len(rows) + len(weights)),
         out_shape=[jax.ShapeDtypeStruct((tokens, width), t) for t in out_types],
-        scratch_shapes=[pltpu.VMEM((tokens * len(rows), width), jnp.float32)],
         cost_estimate=pl.CostEstimate(
             flops=12 * tokens * len(rows) * width * hidden,
             bytes_accessed=12 * width * hidden,
             transcendentals=0,
         ),
+        compiler_params=pltpu.CompilerParams(vmem_limit_bytes=KERNEL_BYTES),
         name="run_experts",
     )(who, *rows, *weights)
 
@@ -435,7 +453,7 @@
         )
 
     spots = [(dz, dx) for dz in range(deep) for dx in range(across)]
-    order = [0] + [d for k in range(1, deep // 2 + 1) for d in sorted({k, deep - k})]
+    order = visiting_order(deep)
     sources = jnp.stack(
         [
             ((my_deep - dz) % deep * across + (my_across - dx) % across) * CORES + my_core
@@ -497,22 +515,18 @@
     extra = jnp.pad(extra, ((0, 0), (0, -extra.shape[1] % LANES)))
 
     near_stats, far_stats, near_out, far_out = state
-    hidden_state, packed = pl.pallas_call(
+    finish = pl.pallas_call(
         finish_kernel,
         out_shape=(
             jax.ShapeDtypeStruct(residual_in.shape, jnp.float32),
             jax.ShapeDtypeStruct((tokens, residual_in.shape[1] + extra.shape[1]), jnp.bfloat16),
         ),
+        compiler_params=pltpu.CompilerParams(vmem_limit_bytes=KERNEL_BYTES),
         name="finish_attention",
-    )(
-        near_stats,
-        near_out,
-        moved(far_stats, 0, 0, 1),
-        moved(far_out, 0, 0, 1),
-        out_weight,
-        residual_in,
-        norm_gain.reshape(1, -1),
-        extra,
+    )
+    arrived = (moved(far_stats, 0, 0, 1), moved(far_out, 0, 0, 1))
+    hidden_state, packed = finish(
+        near_stats, near_out, *arrived, out_weight, residual_in, norm_gain.reshape(1, -1), extra
     )
 
     rows = {(0, 0): packed}
@@ -557,7 +571,13 @@
         P("blk", None, None),
         P("blk", None, None),
     )
-    body = gathered_body if gathers(mesh) else routed_body
-    return jax.shard_map(
-        body, mesh=mesh, in_specs=placed, out_specs=P(("groups", "blk"), None), check_vma=False
-    )
+
+    def shared(body):
+        return jax.shard_map(
+            body, mesh=mesh, in_specs=placed, out_specs=P(("groups", "blk"), None), check_vma=False
+        )
+
+    if not gathers(mesh):
+        return shared(routed_body)
+
+    return shared(gathered_body)

time: 171 us -> 131 us (0.77)
  Pallas kernels: 80.2 us -> 37.5 us
  starting transfers between devices: 35.1 us -> 37.5 us
    pallas_call x8, Pallas kernels: 48.9 us -> 20.7 us  [attend(): pl.pallas_call(lambda *refs: attention_kernel(pieces, state is None, coun...]
    pallas_call x5, Pallas kernels: 31.3 us -> 16.9 us  [the longest x4 15.8 us: run_experts(): pl.pallas_call(lambda *refs: expert_kernel(parties, len(rows), *refs), in...]
    ppermute x35, starting transfers between devices: 35.1 us -> 37.5 us  [moved(): lax.ppermute(array, 'blk', shift_pairs(deep, across, step_deep, step_acro...]
  transfers between devices with their start and end apart: 35 -> 35, of which waited for: 13 -> 14; matrix products, arithmetic and copies ran while one was open for 2% -> 3% of each run, Pallas kernels for 47% -> 29%
where the time goes in v3:
time: 131 us
  waiting for transfers between devices  46.2 us (35%)
  starting transfers between devices  37.5 us (29%)
  Pallas kernels  37.5 us (29%)
  local copies, waits for them, and re-layouts  4.94 us (4%)
  other arithmetic  4.06 us (3%)
    ppermute x35, waiting for transfers between devices, moved(): lax.ppermute(array, 'blk', shift_pairs(deep, across, step_deep, step_acro...  46.2 us
    ppermute x35, starting transfers between devices, moved(): lax.ppermute(array, 'blk', shift_pairs(deep, across, step_deep, step_acro...  37.5 us
    pallas_call x8, Pallas kernels, attend(): pl.pallas_call(lambda *refs: attention_kernel(pieces, state is None, coun...  20.7 us
    pallas_call x4, Pallas kernels, run_experts(): pl.pallas_call(lambda *refs: expert_kernel(parties, len(rows), *refs), in...  15.8 us
  transfers between devices with their start and end apart: 35, of which 14 were waited for; matrix products, arithmetic and copies ran while one was open for 3% of the time, Pallas kernels for 29%

profile of v3, /device:TPU:0, one launch (start us, length us, event | category | flops | bytes accessed | tf_op | source)
XLA Modules:
  0.0 130.8 jit_solution(8963456395712820350)
XLA Ops:
  0.0 1.3 fusion.3
  1.3 0.7 pad_maximum_fusion.refs_5_
  2.0 3.0 %collective-permute-start.2 = (bf16[512,256]{1,0:T(8,128)(2,1)}, bf16[512,256]{1,0:T(8,128)(2,1)S(1)}, u32[]{:S(2)}, u32[]{:S(2)}) collective-permute-start(bf16[512,256]{1,0:T(8,128)(2,1)} %pad_maximum_fusion.refs_5_), channel_id=1, source_target_pairs={{0,2},{1,3},{2,0},{3,1},{4,6},{5,7},{6,4},{7,5},{8,10},{9,11},{10,... | collective-permute-start | bytes 786440 | tf_op jit(solution)/shard_map/ppermute | solution.py:451
  5.0 1.6 %collective-permute-start.4 = (bf16[512,256]{1,0:T(8,128)(2,1)}, bf16[512,256]{1,0:T(8,128)(2,1)S(1)}, u32[]{:S(2)}, u32[]{:S(2)}) collective-permute-start(bf16[512,256]{1,0:T(8,128)(2,1)} %pad_maximum_fusion.refs_5_), channel_id=1, source_target_pairs={{0,4},{1,5},{2,6},{3,7},{4,8},{5,9},{6,10},{7,11},{8,12},{9,13},{1... | collective-permute-start | bytes 786440 | tf_op jit(solution)/shard_map/ppermute | solution.py:451
  6.6 0.5 collective-permute-start.1
  7.1 0.7 pad_maximum_fusion.1.refs_6_
  7.8 1.6 %collective-permute-start.5 = (bf16[512,256]{1,0:T(8,128)(2,1)}, bf16[512,256]{1,0:T(8,128)(2,1)S(1)}, u32[]{:S(2)}, u32[]{:S(2)}) collective-permute-start(bf16[512,256]{1,0:T(8,128)(2,1)} %pad_maximum_fusion.1.refs_6_), channel_id=1, source_target_pairs={{0,4},{1,5},{2,6},{3,7},{4,8},{5,9},{6,10},{7,11},{8,12},{9,13},{1... | collective-permute-start | bytes 786440 | tf_op jit(solution)/shard_map/ppermute | solution.py:451
  9.4 2.3 %collective-permute-start.8 = (bf16[512,256]{1,0:T(8,128)(2,1)}, bf16[512,256]{1,0:T(8,128)(2,1)S(1)}, u32[]{:S(2)}, u32[]{:S(2)}) collective-permute-start(bf16[512,256]{1,0:T(8,128)(2,1)} %pad_maximum_fusion.refs_5_), channel_id=1, source_target_pairs={{0,12},{1,13},{2,14},{3,15},{4,0},{5,1},{6,2},{7,3},{8,4},{9,5},{1... | collective-permute-start | bytes 786440 | tf_op jit(solution)/shard_map/ppermute | solution.py:451
  12.2 0.6 fusion.5
  12.8 0.6 collective-permute-start.3
  13.4 2.9 %collective-permute-done.4.refs_7_ = bf16[512,256]{1,0:T(8,128)(2,1)S(1)} collective-permute-done((bf16[512,256]{1,0:T(8,128)(2,1)}, bf16[512,256]{1,0:T(8,128)(2,1)S(1)}, u32[]{:S(2)}, u32[]{:S(2)}) %collective-permute-start.4) | collective-permute-done | bytes 262176 | tf_op jit(solution)/shard_map/ppermute | solution.py:451
  16.6 5.2 %collective-permute-done.5.refs_8_ = bf16[512,256]{1,0:T(8,128)(2,1)S(1)} collective-permute-done((bf16[512,256]{1,0:T(8,128)(2,1)}, bf16[512,256]{1,0:T(8,128)(2,1)S(1)}, u32[]{:S(2)}, u32[]{:S(2)}) %collective-permute-start.5) | collective-permute-done | bytes 262176 | tf_op jit(solution)/shard_map/ppermute | solution.py:451
  22.2 4.0 %collective-permute-done.8.refs_7_ = bf16[512,256]{1,0:T(8,128)(2,1)S(1)} collective-permute-done((bf16[512,256]{1,0:T(8,128)(2,1)}, bf16[512,256]{1,0:T(8,128)(2,1)S(1)}, u32[]{:S(2)}, u32[]{:S(2)}) %collective-permute-start.8) | collective-permute-done | bytes 262176 | tf_op jit(solution)/shard_map/ppermute | solution.py:451
  26.2 0.5 collective-permute-start.10
  26.7 5.0 %collective-permute-done.9.refs_8_ = bf16[512,256]{1,0:T(8,128)(2,1)S(1)} collective-permute-done((bf16[512,256]{1,0:T(8,128)(2,1)}, bf16[512,256]{1,0:T(8,128)(2,1)S(1)}, u32[]{:S(2)}, u32[]{:S(2)}) %collective-permute-start.9) | collective-permute-done | bytes 262176 | tf_op jit(solution)/shard_map/ppermute | solution.py:451
  31.7 0.5 collective-permute-start.11
  32.7 0.6 stack.44
  33.3 0.5 collective-permute-start.20
  33.8 0.7 pad_maximum_fusion.2
  34.6 0.8 compare_reduce_fusion
  35.6 3.7 %collective-permute-done.10.refs_7_ = bf16[512,256]{1,0:T(8,128)(2,1)} collective-permute-done((bf16[512,256]{1,0:T(8,128)(2,1)S(1)}, bf16[512,256]{1,0:T(8,128)(2,1)}, u32[]{:S(2)}, u32[]{:S(2)}) %collective-permute-start.10) | collective-permute-done | bytes 262176 | tf_op jit(solution)/shard_map/ppermute | solution.py:451
  39.2 1.6 %collective-permute-start.12 = (bf16[512,256]{1,0:T(8,128)(2,1)S(1)}, bf16[512,256]{1,0:T(8,128)(2,1)S(1)}, u32[]{:S(2)}, u32[]{:S(2)}) collective-permute-start(bf16[512,256]{1,0:T(8,128)(2,1)S(1)} %collective-permute-done.4.refs_7_), channel_id=1, source_target_pairs={{0,4},{1,5},{2,6},{3,7},{4,8},{5,9},{6,10},{7,11},{8,12},{9,13},{1... | collective-permute-start | bytes 786440 | tf_op jit(solution)/shard_map/ppermute | solution.py:451
  40.8 2.7 %collective-permute-done.11.refs_8_ = bf16[512,256]{1,0:T(8,128)(2,1)} collective-permute-done((bf16[512,256]{1,0:T(8,128)(2,1)S(1)}, bf16[512,256]{1,0:T(8,128)(2,1)}, u32[]{:S(2)}, u32[]{:S(2)}) %collective-permute-start.11) | collective-permute-done | bytes 262176 | tf_op jit(solution)/shard_map/ppermute | solution.py:451
  43.5 1.2 collective-permute-start.13
  44.7 3.6 %attend_blocks.8 = (f32[8,1024]{1,0:T(8,128)S(1)}, f32[8,1024]{1,0:T(8,128)S(1)}, f32[128,1024]{1,0:T(8,128)S(1)}, f32[128,1024]{1,0:T(8,128)S(1)}) custom-call(bf16[64,2048]{1,0:T(8,128)(2,1)S(1)} %copy-done.3, bf16[64,2048]{1,0:T(8,128)(2,1)S(1)} %collective-permute-done.refs_1_, f32[8,512]{1,0:T(8,128)S(1)} %constant_dynamic-update-slice_fusion.refs_2_, ...), custom_call_target="tpu_custom_call" | custom-call | flops 603979776 | bytes 2686976 | tf_op jit(solution)/shard_map/attend_blocks/pallas_call | solution.py:326
  48.3 1.9 %collective-permute-done.12.refs_7_ = bf16[512,256]{1,0:T(8,128)(2,1)S(1)} collective-permute-done((bf16[512,256]{1,0:T(8,128)(2,1)S(1)}, bf16[512,256]{1,0:T(8,128)(2,1)S(1)}, u32[]{:S(2)}, u32[]{:S(2)}) %collective-permute-start.12) | collective-permute-done | bytes 262176 | tf_op jit(solution)/shard_map/ppermute | solution.py:451
  50.2 0.9 collective-permute-start.14
  51.2 3.4 %collective-permute-done.13.refs_8_ = bf16[512,256]{1,0:T(8,128)(2,1)S(1)} collective-permute-done((bf16[512,256]{1,0:T(8,128)(2,1)S(1)}, bf16[512,256]{1,0:T(8,128)(2,1)S(1)}, u32[]{:S(2)}, u32[]{:S(2)}) %collective-permute-start.13) | collective-permute-done | bytes 262176 | tf_op jit(solution)/shard_map/ppermute | solution.py:451
  54.6 0.9 collective-permute-start.15
  55.6 2.9 %attend_blocks.9 = (f32[8,1024]{1,0:T(8,128)S(1)}, f32[8,1024]{1,0:T(8,128)S(1)}, f32[128,1024]{1,0:T(8,128)S(1)}, f32[128,1024]{1,0:T(8,128)S(1)}) custom-call(bf16[64,2048]{1,0:T(8,128)(2,1)S(1)} %copy-done.3, bf16[64,2048]{1,0:T(8,128)(2,1)S(1)} %collective-permute-done.refs_1_, f32[8,512]{1,0:T(8,128)S(1)} %constant_dynamic-update-slice_fusion.refs_2_, ...), custom_call_target="tpu_custom_call" | custom-call | flops 536870912 | bytes 2621440 | tf_op jit(solution)/shard_map/attend_blocks/pallas_call | solution.py:326
  58.5 2.0 %attend_blocks.10 = (f32[8,1024]{1,0:T(8,128)S(1)}, f32[8,1024]{1,0:T(8,128)S(1)}, f32[128,1024]{1,0:T(8,128)S(1)}, f32[128,1024]{1,0:T(8,128)S(1)}) custom-call(bf16[64,2048]{1,0:T(8,128)(2,1)S(1)} %copy-done.3, bf16[64,2048]{1,0:T(8,128)(2,1)S(1)} %collective-permute-done.refs_1_, f32[8,512]{1,0:T(8,128)S(1)} %constant_dynamic-update-slice_fusion.refs_2_, ...), custom_call_target="tpu_custom_call" | custom-call | flops 536870912 | bytes 2621440 | tf_op jit(solution)/shard_map/attend_blocks/pallas_call | solution.py:326
  60.5 3.0 %attend_blocks.11 = (f32[8,1024]{1,0:T(8,128)S(1)}, f32[8,1024]{1,0:T(8,128)S(1)}, f32[128,1024]{1,0:T(8,128)S(1)}, f32[128,1024]{1,0:T(8,128)S(1)}) custom-call(bf16[64,2048]{1,0:T(8,128)(2,1)S(1)} %copy-done.3, bf16[64,2048]{1,0:T(8,128)(2,1)S(1)} %collective-permute-done.refs_1_, f32[8,512]{1,0:T(8,128)S(1)} %constant_dynamic-update-slice_fusion.refs_2_, ...), custom_call_target="tpu_custom_call" | custom-call | flops 536870912 | bytes 2621440 | tf_op jit(solution)/shard_map/attend_blocks/pallas_call | solution.py:326
  63.5 2.0 %attend_blocks.12 = (f32[8,1024]{1,0:T(8,128)S(1)}, f32[8,1024]{1,0:T(8,128)S(1)}, f32[128,1024]{1,0:T(8,128)S(1)}, f32[128,1024]{1,0:T(8,128)S(1)}) custom-call(bf16[64,2048]{1,0:T(8,128)(2,1)S(1)} %copy-done.3, bf16[64,2048]{1,0:T(8,128)(2,1)S(1)} %collective-permute-done.refs_1_, f32[8,512]{1,0:T(8,128)S(1)} %constant_dynamic-update-slice_fusion.refs_2_, ...), custom_call_target="tpu_custom_call" | custom-call | flops 536870912 | bytes 2621440 | tf_op jit(solution)/shard_map/attend_blocks/pallas_call | solution.py:326
  65.5 3.0 %attend_blocks.13 = (f32[8,1024]{1,0:T(8,128)S(1)}, f32[8,1024]{1,0:T(8,128)S(1)}, f32[128,1024]{1,0:T(8,128)S(1)}, f32[128,1024]{1,0:T(8,128)S(1)}) custom-call(bf16[64,2048]{1,0:T(8,128)(2,1)S(1)} %copy-done.3, bf16[64,2048]{1,0:T(8,128)(2,1)S(1)} %collective-permute-done.refs_1_, f32[8,512]{1,0:T(8,128)S(1)} %constant_dynamic-update-slice_fusion.refs_2_, ...), custom_call_target="tpu_custom_call" | custom-call | flops 536870912 | bytes 2621440 | tf_op jit(solution)/shard_map/attend_blocks/pallas_call | solution.py:326
  68.5 2.2 %attend_blocks.14 = (f32[8,1024]{1,0:T(8,128)S(1)}, f32[8,1024]{1,0:T(8,128)S(1)}, f32[128,1024]{1,0:T(8,128)S(1)}, f32[128,1024]{1,0:T(8,128)S(1)}) custom-call(bf16[64,2048]{1,0:T(8,128)(2,1)S(1)} %copy-done.3, bf16[64,2048]{1,0:T(8,128)(2,1)S(1)} %collective-permute-done.refs_1_, f32[8,512]{1,0:T(8,128)S(1)} %constant_dynamic-update-slice_fusion.refs_2_, ...), custom_call_target="tpu_custom_call" | custom-call | flops 536870912 | bytes 2621440 | tf_op jit(solution)/shard_map/attend_blocks/pallas_call | solution.py:326
  70.8 2.0 %attend_blocks.15 = (f32[8,1024]{1,0:T(8,128)S(1)}, f32[8,1024]{1,0:T(8,128)S(1)}, f32[128,1024]{1,0:T(8,128)S(1)}, bf16[128,1024]{1,0:T(8,128)(2,1)S(1)}) custom-call(bf16[64,2048]{1,0:T(8,128)(2,1)S(1)} %copy-done.3, bf16[64,2048]{1,0:T(8,128)(2,1)S(1)} %collective-permute-done.refs_1_, f32[8,512]{1,0:T(8,128)S(1)} %constant_dynamic-update-slice_fusion.refs_2_, ...), custom_call_target="tpu_custom_call" | custom-call | flops 536870912 | bytes 2621440 | tf_op jit(solution)/shard_map/attend_blocks/pallas_call | solution.py:326
  72.8 0.5 collective-permute-start.16
  73.4 1.0 collective-permute-done.16.far_stats
  74.4 1.0 finish_attention.1
  75.5 0.8 collective-permute-start.31
  76.3 1.0 collective-permute-start.27
  77.3 7.5 %collective-permute-done.31.refs_1_ = bf16[64,1152]{1,0:T(8,128)(2,1)} collective-permute-done((bf16[64,1152]{1,0:T(8,128)(2,1)S(1)}, bf16[64,1152]{1,0:T(8,128)(2,1)}, u32[]{:S(2)}, u32[]{:S(2)}) %collective-permute-start.31) | collective-permute-done | bytes 147488 | tf_op jit(solution)/shard_map/ppermute | solution.py:451
  84.8 2.7 %collective-permute-start.23 = (bf16[64,1152]{1,0:T(8,128)(2,1)S(1)}, bf16[64,1152]{1,0:T(8,128)(2,1)}, u32[]{:S(2)}, u32[]{:S(2)}) collective-permute-start(bf16[64,1152]{1,0:T(8,128)(2,1)S(1)} %get-tuple-element.80.refs_1_), channel_id=1, source_target_pairs={{0,4},{1,5},{2,6},{3,7},{4,8},{5,9},{6,10},{7,11},{8,12},{9,13},{1... | collective-permute-start | bytes 442376 | tf_op jit(solution)/shard_map/ppermute | solution.py:451
  87.5 0.7 copy-done.5
  88.1 1.2 collective-permute-start.32
  89.3 5.2 %collective-permute-done.23.refs_1_ = bf16[64,1152]{1,0:T(8,128)(2,1)} collective-permute-done((bf16[64,1152]{1,0:T(8,128)(2,1)S(1)}, bf16[64,1152]{1,0:T(8,128)(2,1)}, u32[]{:S(2)}, u32[]{:S(2)}) %collective-permute-start.23) | collective-permute-done | bytes 147488 | tf_op jit(solution)/shard_map/ppermute | solution.py:451
  94.5 0.8 collective-permute-start.28
  95.4 1.2 collective-permute-start.18
  96.7 0.8 collective-permute-start.24
  97.5 1.4 %copy-done.2 = bf16[1,768,1024]{2,1,0:T(8,128)(2,1)S(1)} copy-done((bf16[1,768,1024]{2,1,0:T(8,128)(2,1)S(1)}, bf16[1,768,1024]{2,1,0:T(8,128)(2,1)}, u32[]{:S(2)}) %copy-start.2) | copy-done | bytes 1572888
  98.9 4.1 %run_experts.7 = (f32[64,1024]{1,0:T(8,128)S(1)}, bf16[64,1024]{1,0:T(8,128)(2,1)S(1)}) custom-call(s32[2]{0:T(128)S(1)} %pad_add_fusion.refs_0_, bf16[64,1152]{1,0:T(8,128)(2,1)} %collective-permute-done.31.refs_1_, bf16[64,1152]{1,0:T(8,128)(2,1)} %collective-permute-done.32.refs_2_, bf16[1,1024,768]{2,1,0:T(8,128)(2,1)S(1)} %copy-done, ...), custom_call_target="tpu_custom_call" | custom-call | flops 1207959552 | bytes 9437184 | tf_op jit(solution)/shard_map/run_experts/pallas_call | solution.py:411
  103.0 1.3 collective-permute-start.33
  104.3 3.9 %run_experts.6 = (f32[64,1024]{1,0:T(8,128)S(1)}, bf16[64,1024]{1,0:T(8,128)(2,1)S(1)}) custom-call(s32[2]{0:T(128)S(1)} %pad_add_fusion.refs_0_, bf16[64,1152]{1,0:T(8,128)(2,1)S(1)} %copy-done.6, bf16[64,1152]{1,0:T(8,128)(2,1)S(1)} %collective-permute-done.28.refs_2_, bf16[1,1024,768]{2,1,0:T(8,128)(2,1)S(1)} %copy-done, ...), custom_call_target="tpu_custom_call" | custom-call | flops 1207959552 | bytes 9437184 | tf_op jit(solution)/shard_map/run_experts/pallas_call | solution.py:411
  108.2 0.9 collective-permute-start.29
  109.0 4.0 %run_experts.5 = (f32[64,1024]{1,0:T(8,128)S(1)}, bf16[64,1024]{1,0:T(8,128)(2,1)S(1)}) custom-call(s32[2]{0:T(128)S(1)} %pad_add_fusion.refs_0_, bf16[64,1152]{1,0:T(8,128)(2,1)} %collective-permute-done.23.refs_1_, bf16[64,1152]{1,0:T(8,128)(2,1)S(1)} %collective-permute-done.24.refs_2_, bf16[1,1024,768]{2,1,0:T(8,128)(2,1)S(1)} %copy-done, ...), custom_call_target="tpu_custom_call" | custom-call | flops 1207959552 | bytes 9437184 | tf_op jit(solution)/shard_map/run_experts/pallas_call | solution.py:411
  113.0 1.3 collective-permute-start.25
  114.3 3.9 %run_experts.4 = (f32[64,1024]{1,0:T(8,128)S(1)}, bf16[64,1024]{1,0:T(8,128)(2,1)S(1)}) custom-call(s32[2]{0:T(128)S(1)} %pad_add_fusion.refs_0_, bf16[64,1152]{1,0:T(8,128)(2,1)S(1)} %get-tuple-element.80.refs_1_, bf16[64,1152]{1,0:T(8,128)(2,1)S(1)} %collective-permute-done.18.refs_2_, bf16[1,1024,768]{2,1,0:T(8,128)(2,1)S(1)} %copy-done, ...), custom_call_target="tpu_custom_call" | custom-call | flops 1207959552 | bytes 9437184 | tf_op jit(solution)/shard_map/run_experts/pallas_call | solution.py:411
  118.2 0.9 collective-permute-start.22
  119.1 3.2 %collective-permute-start.34 = (bf16[64,1024]{1,0:T(8,128)(2,1)S(1)}, bf16[64,1024]{1,0:T(8,128)(2,1)S(1)}, u32[]{:S(2)}, u32[]{:S(2)}) collective-permute-start(bf16[64,1024]{1,0:T(8,128)(2,1)S(1)} %add_convert_fusion.1), channel_id=1, source_target_pairs={{0,8},{1,9},{2,10},{3,11},{4,12},{5,13},{6,14},{7,15},{8,0},{9,1},... | collective-permute-start | bytes 393224 | tf_op jit(solution)/shard_map/ppermute | solution.py:451
  122.5 3.9 %collective-permute-start.26 = (bf16[64,1024]{1,0:T(8,128)(2,1)S(1)}, bf16[64,1024]{1,0:T(8,128)(2,1)S(1)}, u32[]{:S(2)}, u32[]{:S(2)}) collective-permute-start(bf16[64,1024]{1,0:T(8,128)(2,1)S(1)} %add_convert_fusion.3), channel_id=1, source_target_pairs={{0,12},{1,13},{2,14},{3,15},{4,0},{5,1},{6,2},{7,3},{8,4},{9,5},{1... | collective-permute-start | bytes 393224 | tf_op jit(solution)/shard_map/ppermute | solution.py:451
  126.3 1.4 %collective-permute-done.34 = bf16[64,1024]{1,0:T(8,128)(2,1)S(1)} collective-permute-done((bf16[64,1024]{1,0:T(8,128)(2,1)S(1)}, bf16[64,1024]{1,0:T(8,128)(2,1)S(1)}, u32[]{:S(2)}, u32[]{:S(2)}) %collective-permute-start.34) | collective-permute-done | bytes 131104 | tf_op jit(solution)/shard_map/ppermute | solution.py:451
  127.7 1.5 %collective-permute-done.30 = bf16[64,1024]{1,0:T(8,128)(2,1)S(1)} collective-permute-done((bf16[64,1024]{1,0:T(8,128)(2,1)S(1)}, bf16[64,1024]{1,0:T(8,128)(2,1)S(1)}, u32[]{:S(2)}, u32[]{:S(2)}) %collective-permute-start.30) | collective-permute-done | bytes 131104 | tf_op jit(solution)/shard_map/ppermute | solution.py:451
  129.3 0.8 collective-permute-done.26
  130.0 0.8 add_convert_fusion
  (78 shorter events, 2.2 us)
Async XLA Ops:
  0.0 6.6 %copy-start.3 = (bf16[64,2048]{1,0:T(8,128)(2,1)S(1)}, bf16[64,2048]{1,0:T(8,128)(2,1)}, u32[]{:S(2)}) copy-start(bf16[64,2048]{1,0:T(8,128)(2,1)} %refs_0_.15) | copy-start | bytes 786436
  0.0 6.6 %copy-start.12 = (s32[64,8]{0,1:T(8,128)S(1)}, s32[64,8]{0,1:T(8,128)}, u32[]{:S(2)}) copy-start(s32[64,8]{0,1:T(8,128)} %param.19) | copy-start | bytes 6148
  0.0 9.4 %copy-start.9 = (bf16[64,256]{1,0:T(8,128)(2,1)S(1)}, bf16[64,256]{1,0:T(8,128)(2,1)}, u32[]{:S(2)}) copy-start(bf16[64,256]{1,0:T(8,128)(2,1)} %param.18) | copy-start | bytes 98308
  0.0 12.2 %copy-start.10 = (bf16[64,256]{1,0:T(8,128)(2,1)S(1)}, bf16[64,256]{1,0:T(8,128)(2,1)}, u32[]{:S(2)}) copy-start(bf16[64,256]{1,0:T(8,128)(2,1)} %param.17) | copy-start | bytes 98308
  0.0 12.8 %copy-start.11 = (f32[64,8]{0,1:T(8,128)S(1)}, f32[64,8]{0,1:T(8,128)}, u32[]{:S(2)}) copy-start(f32[64,8]{0,1:T(8,128)} %param.24) | copy-start | bytes 6148
  0.0 32.3 %copy-start.14 = (s32[64,8]{0,1:T(8,128)S(1)}, s32[64,8]{0,1:T(8,128)}, u32[]{:S(2)}) copy-start(s32[64,8]{0,1:T(8,128)} %param.23) | copy-start | bytes 6148
  0.0 33.2 %copy-start = (bf16[1,1024,768]{2,1,0:T(8,128)(2,1)S(1)}, bf16[1,1024,768]{2,1,0:T(8,128)(2,1)}, u32[]{:S(2)}) copy-start(bf16[1,1024,768]{2,1,0:T(8,128)(2,1)} %refs_3_.7) | copy-start | bytes 4718596
  2.0 10.8 %collective-permute-start.2 = (bf16[512,256]{1,0:T(8,128)(2,1)}, bf16[512,256]{1,0:T(8,128)(2,1)S(1)}, u32[]{:S(2)}, u32[]{:S(2)}) collective-permute-start(bf16[512,256]{1,0:T(8,128)(2,1)} %pad_maximum_fusion.refs_5_), channel_id=1, source_target_pairs={{0,2},{1,3},{2,0},{3,1},{4,6},{5,7},{6,4},{7,5},{8,10},{9,11},{10,... | collective-permute-start | bytes 786440 | tf_op jit(solution)/shard_map/ppermute | solution.py:451
  5.0 11.3 %collective-permute-start.4 = (bf16[512,256]{1,0:T(8,128)(2,1)}, bf16[512,256]{1,0:T(8,128)(2,1)S(1)}, u32[]{:S(2)}, u32[]{:S(2)}) collective-permute-start(bf16[512,256]{1,0:T(8,128)(2,1)} %pad_maximum_fusion.refs_5_), channel_id=1, source_target_pairs={{0,4},{1,5},{2,6},{3,7},{4,8},{5,9},{6,10},{7,11},{8,12},{9,13},{1... | collective-permute-start | bytes 786440 | tf_op jit(solution)/shard_map/ppermute | solution.py:451
  6.6 5.1 %collective-permute-start = (bf16[64,2048]{1,0:T(8,128)(2,1)S(1)}, bf16[64,2048]{1,0:T(8,128)(2,1)S(1)}, u32[]{:S(2)}, u32[]{:S(2)}) collective-permute-start(bf16[64,2048]{1,0:T(8,128)(2,1)S(1)} %copy-done.3), channel_id=1, source_target_pairs={{0,1},{1,0},{2,3},{3,2},{4,5},{5,4},{6,7},{7,6},{8,9},{9,8},{10,11... | collective-permute-start | bytes 786440 | tf_op jit(solution)/shard_map/ppermute | solution.py:451
  6.6 2.8 %collective-permute-start.1 = (s32[64,8]{0,1:T(8,128)S(1)}, s32[64,8]{0,1:T(8,128)S(1)}, u32[]{:S(2)}, u32[]{:S(2)}) collective-permute-start(s32[64,8]{0,1:T(8,128)S(1)} %copy-done.12), channel_id=1, source_target_pairs={{0,1},{1,0},{2,3},{3,2},{4,5},{5,4},{6,7},{7,6},{8,9},{9,8},{10,11... | collective-permute-start | bytes 6152 | tf_op jit(solution)/shard_map/ppermute | solution.py:451
  7.8 14.0 %collective-permute-start.5 = (bf16[512,256]{1,0:T(8,128)(2,1)}, bf16[512,256]{1,0:T(8,128)(2,1)S(1)}, u32[]{:S(2)}, u32[]{:S(2)}) collective-permute-start(bf16[512,256]{1,0:T(8,128)(2,1)} %pad_maximum_fusion.1.refs_6_), channel_id=1, source_target_pairs={{0,4},{1,5},{2,6},{3,7},{4,8},{5,9},{6,10},{7,11},{8,12},{9,13},{1... | collective-permute-start | bytes 786440 | tf_op jit(solution)/shard_map/ppermute | solution.py:451
  9.4 12.4 %copy-start.13 = (s32[64,8]{0,1:T(8,128)}, s32[64,8]{0,1:T(8,128)S(1)}, u32[]{:S(2)}) copy-start(s32[64,8]{0,1:T(8,128)S(1)} %collective-permute-done.1) | copy-start | bytes 6148
  9.4 16.8 %collective-permute-start.8 = (bf16[512,256]{1,0:T(8,128)(2,1)}, bf16[512,256]{1,0:T(8,128)(2,1)S(1)}, u32[]{:S(2)}, u32[]{:S(2)}) collective-permute-start(bf16[512,256]{1,0:T(8,128)(2,1)} %pad_maximum_fusion.refs_5_), channel_id=1, source_target_pairs={{0,12},{1,13},{2,14},{3,15},{4,0},{5,1},{6,2},{7,3},{8,4},{9,5},{1... | collective-permute-start | bytes 786440 | tf_op jit(solution)/shard_map/ppermute | solution.py:451
  11.7 20.0 %collective-permute-start.9 = (bf16[512,256]{1,0:T(8,128)(2,1)}, bf16[512,256]{1,0:T(8,128)(2,1)S(1)}, u32[]{:S(2)}, u32[]{:S(2)}) collective-permute-start(bf16[512,256]{1,0:T(8,128)(2,1)} %pad_maximum_fusion.1.refs_6_), channel_id=1, source_target_pairs={{0,12},{1,13},{2,14},{3,15},{4,0},{5,1},{6,2},{7,3},{8,4},{9,5},{1... | collective-permute-start | bytes 786440 | tf_op jit(solution)/shard_map/ppermute | solution.py:451
  12.8 20.4 %collective-permute-start.3 = (bf16[512,256]{1,0:T(8,128)(2,1)}, bf16[512,256]{1,0:T(8,128)(2,1)}, u32[]{:S(2)}, u32[]{:S(2)}) collective-permute-start(bf16[512,256]{1,0:T(8,128)(2,1)} %pad_maximum_fusion.1.refs_6_), channel_id=1, source_target_pairs={{0,2},{1,3},{2,0},{3,1},{4,6},{5,7},{6,4},{7,5},{8,10},{9,11},{10,... | collective-permute-start | bytes 786440 | tf_op jit(solution)/shard_map/ppermute | solution.py:451
  16.3 17.0 %collective-permute-start.6 = (bf16[512,256]{1,0:T(8,128)(2,1)S(1)}, bf16[512,256]{1,0:T(8,128)(2,1)}, u32[]{:S(2)}, u32[]{:S(2)}) collective-permute-start(bf16[512,256]{1,0:T(8,128)(2,1)S(1)} %collective-permute-done.4.refs_7_), channel_id=1, source_target_pairs={{0,2},{1,3},{2,0},{3,1},{4,6},{5,7},{6,4},{7,5},{8,10},{9,11},{10,... | collective-permute-start | bytes 786440 | tf_op jit(solution)/shard_map/ppermute | solution.py:451
  21.9 11.9 %collective-permute-start.7 = (bf16[512,256]{1,0:T(8,128)(2,1)S(1)}, bf16[512,256]{1,0:T(8,128)(2,1)}, u32[]{:S(2)}, u32[]{:S(2)}) collective-permute-start(bf16[512,256]{1,0:T(8,128)(2,1)S(1)} %collective-permute-done.5.refs_8_), channel_id=1, source_target_pairs={{0,2},{1,3},{2,0},{3,1},{4,6},{5,7},{6,4},{7,5},{8,10},{9,11},{10,... | collective-permute-start | bytes 786440 | tf_op jit(solution)/shard_map/ppermute | solution.py:451
  26.2 13.0 %collective-permute-start.10 = (bf16[512,256]{1,0:T(8,128)(2,1)S(1)}, bf16[512,256]{1,0:T(8,128)(2,1)}, u32[]{:S(2)}, u32[]{:S(2)}) collective-permute-start(bf16[512,256]{1,0:T(8,128)(2,1)S(1)} %collective-permute-done.8.refs_7_), channel_id=1, source_target_pairs={{0,2},{1,3},{2,0},{3,1},{4,6},{5,7},{6,4},{7,5},{8,10},{9,11},{10,... | collective-permute-start | bytes 786440 | tf_op jit(solution)/shard_map/ppermute | solution.py:451
  31.7 11.7 %collective-permute-start.11 = (bf16[512,256]{1,0:T(8,128)(2,1)S(1)}, bf16[512,256]{1,0:T(8,128)(2,1)}, u32[]{:S(2)}, u32[]{:S(2)}) collective-permute-start(bf16[512,256]{1,0:T(8,128)(2,1)S(1)} %collective-permute-done.9.refs_8_), channel_id=1, source_target_pairs={{0,2},{1,3},{2,0},{3,1},{4,6},{5,7},{6,4},{7,5},{8,10},{9,11},{10,... | collective-permute-start | bytes 786440 | tf_op jit(solution)/shard_map/ppermute | solution.py:451
  33.2 63.4 %collective-permute-start.19 = (bf16[1,1024,768]{2,1,0:T(8,128)(2,1)S(1)}, bf16[1,1024,768]{2,1,0:T(8,128)(2,1)}, u32[]{:S(2)}, u32[]{:S(2)}) collective-permute-start(bf16[1,1024,768]{2,1,0:T(8,128)(2,1)S(1)} %copy-done), channel_id=1, source_target_pairs={{0,1},{1,0},{2,3},{3,2},{4,5},{5,4},{6,7},{7,6},{8,9},{9,8},{10,11... | collective-permute-start | bytes 4718600 | tf_op jit(solution)/shard_map/ppermute | solution.py:451
  33.3 64.2 %collective-permute-start.20 = (bf16[1,1024,768]{2,1,0:T(8,128)(2,1)}, bf16[1,1024,768]{2,1,0:T(8,128)(2,1)}, u32[]{:S(2)}, u32[]{:S(2)}) collective-permute-start(bf16[1,1024,768]{2,1,0:T(8,128)(2,1)} %refs_4_.7), channel_id=1, source_target_pairs={{0,1},{1,0},{2,3},{3,2},{4,5},{5,4},{6,7},{7,6},{8,9},{9,8},{10,11... | collective-permute-start | bytes 4718600 | tf_op jit(solution)/shard_map/ppermute | solution.py:451
  33.8 63.7 %collective-permute-start.21 = (bf16[1,768,1024]{2,1,0:T(8,128)(2,1)}, bf16[1,768,1024]{2,1,0:T(8,128)(2,1)}, u32[]{:S(2)}, u32[]{:S(2)}) collective-permute-start(bf16[1,768,1024]{2,1,0:T(8,128)(2,1)} %refs_5_.7), channel_id=1, source_target_pairs={{0,1},{1,0},{2,3},{3,2},{4,5},{5,4},{6,7},{7,6},{8,9},{9,8},{10,11... | collective-permute-start | bytes 4718600 | tf_op jit(solution)/shard_map/ppermute | solution.py:451
  39.2 11.0 %collective-permute-start.12 = (bf16[512,256]{1,0:T(8,128)(2,1)S(1)}, bf16[512,256]{1,0:T(8,128)(2,1)S(1)}, u32[]{:S(2)}, u32[]{:S(2)}) collective-permute-start(bf16[512,256]{1,0:T(8,128)(2,1)S(1)} %collective-permute-done.4.refs_7_), channel_id=1, source_target_pairs={{0,4},{1,5},{2,6},{3,7},{4,8},{5,9},{6,10},{7,11},{8,12},{9,13},{1... | collective-permute-start | bytes 786440 | tf_op jit(solution)/shard_map/ppermute | solution.py:451
  43.5 11.2 %collective-permute-start.13 = (bf16[512,256]{1,0:T(8,128)(2,1)S(1)}, bf16[512,256]{1,0:T(8,128)(2,1)S(1)}, u32[]{:S(2)}, u32[]{:S(2)}) collective-permute-start(bf16[512,256]{1,0:T(8,128)(2,1)S(1)} %collective-permute-done.5.refs_8_), channel_id=1, source_target_pairs={{0,4},{1,5},{2,6},{3,7},{4,8},{5,9},{6,10},{7,11},{8,12},{9,13},{1... | collective-permute-start | bytes 786440 | tf_op jit(solution)/shard_map/ppermute | solution.py:451
  50.2 20.5 %collective-permute-start.14 = (bf16[512,256]{1,0:T(8,128)(2,1)S(1)}, bf16[512,256]{1,0:T(8,128)(2,1)S(1)}, u32[]{:S(2)}, u32[]{:S(2)}) collective-permute-start(bf16[512,256]{1,0:T(8,128)(2,1)S(1)} %collective-permute-done.12.refs_7_), channel_id=1, source_target_pairs={{0,2},{1,3},{2,0},{3,1},{4,6},{5,7},{6,4},{7,5},{8,10},{9,11},{10,... | collective-permute-start | bytes 786440 | tf_op jit(solution)/shard_map/ppermute | solution.py:451
  54.6 16.1 %collective-permute-start.15 = (bf16[512,256]{1,0:T(8,128)(2,1)S(1)}, bf16[512,256]{1,0:T(8,128)(2,1)S(1)}, u32[]{:S(2)}, u32[]{:S(2)}) collective-permute-start(bf16[512,256]{1,0:T(8,128)(2,1)S(1)} %collective-permute-done.13.refs_8_), channel_id=1, source_target_pairs={{0,2},{1,3},{2,0},{3,1},{4,6},{5,7},{6,4},{7,5},{8,10},{9,11},{10,... | collective-permute-start | bytes 786440 | tf_op jit(solution)/shard_map/ppermute | solution.py:451
  68.5 5.9 %copy-start.4 = (bf16[2048,1024]{1,0:T(8,128)(2,1)S(1)}, bf16[2048,1024]{1,0:T(8,128)(2,1)}, u32[]{:S(2)}) copy-start(bf16[2048,1024]{1,0:T(8,128)(2,1)} %weight_ref.1) | copy-start | bytes 12582916
  70.7 3.7 %copy-start.7 = (bf16[64,1024]{1,0:T(8,128)(2,1)S(1)}, bf16[64,1024]{1,0:T(8,128)(2,1)}, u32[]{:S(2)}) copy-start(bf16[64,1024]{1,0:T(8,128)(2,1)} %residual_ref.1) | copy-start | bytes 393220
  70.7 3.7 %copy-start.8 = (f32[1024]{0:T(1024)S(1)}, f32[1024]{0:T(1024)}, u32[]{:S(2)}) copy-start(f32[1024]{0:T(1024)} %param.22) | copy-start | bytes 12292
  72.7 1.7 %collective-permute-start.17 = (bf16[128,1024]{1,0:T(8,128)(2,1)S(1)}, bf16[128,1024]{1,0:T(8,128)(2,1)S(1)}, u32[]{:S(2)}, u32[]{:S(2)}) collective-permute-start(bf16[128,1024]{1,0:T(8,128)(2,1)S(1)} %get-tuple-element.78), channel_id=1, source_target_pairs={{0,1},{1,0},{2,3},{3,2},{4,5},{5,4},{6,7},{7,6},{8,9},{9,8},{10,11... | collective-permute-start | bytes 786440 | tf_op jit(solution)/shard_map/ppermute | solution.py:451
  72.8 1.6 %collective-permute-start.16 = (f32[8,1024]{1,0:T(8,128)S(1)}, f32[8,1024]{1,0:T(8,128)S(1)}, u32[]{:S(2)}, u32[]{:S(2)}) collective-permute-start(f32[8,1024]{1,0:T(8,128)S(1)} %get-tuple-element.77), channel_id=1, source_target_pairs={{0,1},{1,0},{2,3},{3,2},{4,5},{5,4},{6,7},{7,6},{8,9},{9,8},{10,11... | collective-permute-start | bytes 98312 | tf_op jit(solution)/shard_map/ppermute | solution.py:451
  74.4 23.1 %copy-start.1 = (bf16[1,1024,768]{2,1,0:T(8,128)(2,1)S(1)}, bf16[1,1024,768]{2,1,0:T(8,128)(2,1)}, u32[]{:S(2)}) copy-start(bf16[1,1024,768]{2,1,0:T(8,128)(2,1)} %refs_4_.7) | copy-start | bytes 4718596
  75.5 9.3 %collective-permute-start.31 = (bf16[64,1152]{1,0:T(8,128)(2,1)S(1)}, bf16[64,1152]{1,0:T(8,128)(2,1)}, u32[]{:S(2)}, u32[]{:S(2)}) collective-permute-start(bf16[64,1152]{1,0:T(8,128)(2,1)S(1)} %get-tuple-element.80.refs_1_), channel_id=1, source_target_pairs={{0,8},{1,9},{2,10},{3,11},{4,12},{5,13},{6,14},{7,15},{8,0},{9,1},... | collective-permute-start | bytes 442376 | tf_op jit(solution)/shard_map/ppermute | solution.py:451
  76.3 11.2 %collective-permute-start.27 = (bf16[64,1152]{1,0:T(8,128)(2,1)S(1)}, bf16[64,1152]{1,0:T(8,128)(2,1)S(1)}, u32[]{:S(2)}, u32[]{:S(2)}) collective-permute-start(bf16[64,1152]{1,0:T(8,128)(2,1)S(1)} %get-tuple-element.80.refs_1_), channel_id=1, source_target_pairs={{0,12},{1,13},{2,14},{3,15},{4,0},{5,1},{6,2},{7,3},{8,4},{9,5},{1... | collective-permute-start | bytes 442376 | tf_op jit(solution)/shard_map/ppermute | solution.py:451
  84.8 9.7 %collective-permute-start.23 = (bf16[64,1152]{1,0:T(8,128)(2,1)S(1)}, bf16[64,1152]{1,0:T(8,128)(2,1)}, u32[]{:S(2)}, u32[]{:S(2)}) collective-permute-start(bf16[64,1152]{1,0:T(8,128)(2,1)S(1)} %get-tuple-element.80.refs_1_), channel_id=1, source_target_pairs={{0,4},{1,5},{2,6},{3,7},{4,8},{5,9},{6,10},{7,11},{8,12},{9,13},{1... | collective-permute-start | bytes 442376 | tf_op jit(solution)/shard_map/ppermute | solution.py:451
  87.5 0.7 copy-start.5
  88.1 7.3 %collective-permute-start.32 = (bf16[64,1152]{1,0:T(8,128)(2,1)}, bf16[64,1152]{1,0:T(8,128)(2,1)}, u32[]{:S(2)}, u32[]{:S(2)}) collective-permute-start(bf16[64,1152]{1,0:T(8,128)(2,1)} %collective-permute-done.31.refs_1_), channel_id=1, source_target_pairs={{0,2},{1,3},{2,0},{3,1},{4,6},{5,7},{6,4},{7,5},{8,10},{9,11},{10,... | collective-permute-start | bytes 442376 | tf_op jit(solution)/shard_map/ppermute | solution.py:451
  94.5 9.7 %collective-permute-start.28 = (bf16[64,1152]{1,0:T(8,128)(2,1)}, bf16[64,1152]{1,0:T(8,128)(2,1)S(1)}, u32[]{:S(2)}, u32[]{:S(2)}) collective-permute-start(bf16[64,1152]{1,0:T(8,128)(2,1)} %copy-done.5), channel_id=1, source_target_pairs={{0,2},{1,3},{2,0},{3,1},{4,6},{5,7},{6,4},{7,5},{8,10},{9,11},{10,... | collective-permute-start | bytes 442376 | tf_op jit(solution)/shard_map/ppermute | solution.py:451
  95.4 18.9 %collective-permute-start.18 = (bf16[64,1152]{1,0:T(8,128)(2,1)S(1)}, bf16[64,1152]{1,0:T(8,128)(2,1)S(1)}, u32[]{:S(2)}, u32[]{:S(2)}) collective-permute-start(bf16[64,1152]{1,0:T(8,128)(2,1)S(1)} %get-tuple-element.80.refs_1_), channel_id=1, source_target_pairs={{0,2},{1,3},{2,0},{3,1},{4,6},{5,7},{6,4},{7,5},{8,10},{9,11},{10,... | collective-permute-start | bytes 442376 | tf_op jit(solution)/shard_map/ppermute | solution.py:451
  96.7 12.4 %collective-permute-start.24 = (bf16[64,1152]{1,0:T(8,128)(2,1)}, bf16[64,1152]{1,0:T(8,128)(2,1)S(1)}, u32[]{:S(2)}, u32[]{:S(2)}) collective-permute-start(bf16[64,1152]{1,0:T(8,128)(2,1)} %collective-permute-done.23.refs_1_), channel_id=1, source_target_pairs={{0,2},{1,3},{2,0},{3,1},{4,6},{5,7},{6,4},{7,5},{8,10},{9,11},{10,... | collective-permute-start | bytes 442376 | tf_op jit(solution)/shard_map/ppermute | solution.py:451
  97.5 1.4 %copy-start.2 = (bf16[1,768,1024]{2,1,0:T(8,128)(2,1)S(1)}, bf16[1,768,1024]{2,1,0:T(8,128)(2,1)}, u32[]{:S(2)}) copy-start(bf16[1,768,1024]{2,1,0:T(8,128)(2,1)} %refs_5_.7) | copy-start | bytes 4718596
  98.9 5.4 %copy-start.6 = (bf16[64,1152]{1,0:T(8,128)(2,1)S(1)}, bf16[64,1152]{1,0:T(8,128)(2,1)}, u32[]{:S(2)}) copy-start(bf16[64,1152]{1,0:T(8,128)(2,1)} %copy-done.5) | copy-start | bytes 442372
  103.0 16.1 %collective-permute-start.33 = (bf16[64,1024]{1,0:T(8,128)(2,1)S(1)}, bf16[64,1024]{1,0:T(8,128)(2,1)S(1)}, u32[]{:S(2)}, u32[]{:S(2)}) collective-permute-start(bf16[64,1024]{1,0:T(8,128)(2,1)S(1)} %get-tuple-element.88), channel_id=1, source_target_pairs={{0,2},{1,3},{2,0},{3,1},{4,6},{5,7},{6,4},{7,5},{8,10},{9,11},{10,... | collective-permute-start | bytes 393224 | tf_op jit(solution)/shard_map/ppermute | solution.py:451
  108.2 14.1 %collective-permute-start.29 = (bf16[64,1024]{1,0:T(8,128)(2,1)S(1)}, bf16[64,1024]{1,0:T(8,128)(2,1)S(1)}, u32[]{:S(2)}, u32[]{:S(2)}) collective-permute-start(bf16[64,1024]{1,0:T(8,128)(2,1)S(1)} %get-tuple-element.86), channel_id=1, source_target_pairs={{0,2},{1,3},{2,0},{3,1},{4,6},{5,7},{6,4},{7,5},{8,10},{9,11},{10,... | collective-permute-start | bytes 393224 | tf_op jit(solution)/shard_map/ppermute | solution.py:451
  113.0 9.4 %collective-permute-start.25 = (bf16[64,1024]{1,0:T(8,128)(2,1)S(1)}, bf16[64,1024]{1,0:T(8,128)(2,1)S(1)}, u32[]{:S(2)}, u32[]{:S(2)}) collective-permute-start(bf16[64,1024]{1,0:T(8,128)(2,1)S(1)} %get-tuple-element.84), channel_id=1, source_target_pairs={{0,2},{1,3},{2,0},{3,1},{4,6},{5,7},{6,4},{7,5},{8,10},{9,11},{10,... | collective-permute-start | bytes 393224 | tf_op jit(solution)/shard_map/ppermute | solution.py:451
  118.2 8.1 %collective-permute-start.22 = (bf16[64,1024]{1,0:T(8,128)(2,1)S(1)}, bf16[64,1024]{1,0:T(8,128)(2,1)S(1)}, u32[]{:S(2)}, u32[]{:S(2)}) collective-permute-start(bf16[64,1024]{1,0:T(8,128)(2,1)S(1)} %get-tuple-element.82), channel_id=1, source_target_pairs={{0,2},{1,3},{2,0},{3,1},{4,6},{5,7},{6,4},{7,5},{8,10},{9,11},{10,... | collective-permute-start | bytes 393224 | tf_op jit(solution)/shard_map/ppermute | solution.py:451
  119.1 8.6 %collective-permute-start.34 = (bf16[64,1024]{1,0:T(8,128)(2,1)S(1)}, bf16[64,1024]{1,0:T(8,128)(2,1)S(1)}, u32[]{:S(2)}, u32[]{:S(2)}) collective-permute-start(bf16[64,1024]{1,0:T(8,128)(2,1)S(1)} %add_convert_fusion.1), channel_id=1, source_target_pairs={{0,8},{1,9},{2,10},{3,11},{4,12},{5,13},{6,14},{7,15},{8,0},{9,1},... | collective-permute-start | bytes 393224 | tf_op jit(solution)/shard_map/ppermute | solution.py:451
  122.3 6.9 %collective-permute-start.30 = (bf16[64,1024]{1,0:T(8,128)(2,1)S(1)}, bf16[64,1024]{1,0:T(8,128)(2,1)S(1)}, u32[]{:S(2)}, u32[]{:S(2)}) collective-permute-start(bf16[64,1024]{1,0:T(8,128)(2,1)S(1)} %add_convert_fusion.2), channel_id=1, source_target_pairs={{0,4},{1,5},{2,6},{3,7},{4,8},{5,9},{6,10},{7,11},{8,12},{9,13},{1... | collective-permute-start | bytes 393224 | tf_op jit(solution)/shard_map/ppermute | solution.py:451
  122.5 7.6 %collective-permute-start.26 = (bf16[64,1024]{1,0:T(8,128)(2,1)S(1)}, bf16[64,1024]{1,0:T(8,128)(2,1)S(1)}, u32[]{:S(2)}, u32[]{:S(2)}) collective-permute-start(bf16[64,1024]{1,0:T(8,128)(2,1)S(1)} %add_convert_fusion.3), channel_id=1, source_target_pairs={{0,12},{1,13},{2,14},{3,15},{4,0},{5,1},{6,2},{7,3},{8,4},{9,5},{1... | collective-permute-start | bytes 393224 | tf_op jit(solution)/shard_map/ppermute | solution.py:451

commit v4 on v3

--- a/solution.py
+++ b/solution.py
@@ -185,9 +185,11 @@
 LANES = 128
 TILE = 256
 ONES_ROWS = 16
+PARTS = 4
+WEIGHT_PARTS = 8
 PIECE = 256
-MIX_PIECE = 512
 KERNEL_BYTES = 20 << 20
+ATTEND_BYTES = 10 << 20
 
 
 def grid_of(parties):
@@ -202,6 +204,15 @@
     return [0] + [d for k in range(1, deep // 2 + 1) for d in sorted({k, deep - k})]
 
 
+def stages_of(deep, across):
+    wide = range(1, across)
+    later = [dz for dz in visiting_order(deep) if 1 < dz < deep - 1]
+    stages = [[(0, 0)]] + [[(0, dx)] for dx in wide] + [[(1, 0)]] + [[(1, dx)] for dx in wide]
+    stages += [[(dz, 0)] for dz in later] + [[(deep - 1, 0)]]
+    stages += [[(dz, dx)] for dz in later + [deep - 1] for dx in wide]
+    return [stage for stage in stages if stage]
+
+
 def gathers(mesh):
     return mesh.shape["blk"] <= 4 * TOPB and mesh.shape["blk"] % CORES == 0
 
@@ -219,37 +230,56 @@
     ]
 
 
-def attention_kernel(pieces, first, count, *refs):
+def fetch(source, target, arrived, first, parts):
+    rows = source.shape[-2] // parts
+    copies = []
+    for part in range(parts):
+        cut = (*(slice(None),) * (len(source.shape) - 2), slice(part * rows, (part + 1) * rows))
+        copies.append(
+            pltpu.make_async_copy(source.at[cut], target.at[cut], arrived.at[first + part])
+        )
+        copies[-1].start()
+    return copies
+
+
+def attention_kernel(columns, first, *refs):
+    count = len(columns)
     queries = refs[0:2]
     chosen_ref = refs[2]
     given = None if first else refs[3:7]
-    block_refs = refs[-6 - count : -6]
-    stats_refs = refs[-6:-4]
-    out_refs = refs[-4:-2]
-    score_refs = refs[-2:]
+    inputs = 3 if first else 7
+    sources = refs[inputs : inputs + 2 * count]
+    results = refs[inputs + 2 * count :]
+    stats_refs = results[0:2]
+    out_refs = results[2:4]
+    score_refs = results[4:6]
+    held_ref, arrived = results[6:]
+    copies = []
+    held = []
+    for number, source in enumerate(sources):
+        held.append(held_ref.at[number, : source.shape[0], :])
+        copies.append(fetch(source, held[-1], arrived, number * PARTS, PARTS))
     tokens = queries[0].shape[0]
     per_tile = TILE // tokens
     heads_per_group = QUERY_HEADS // KEY_VALUE_HEADS
     factor = HEAD_SIZE ** (-0.5) * LOG2_E
-    tasks = []
-    for group in range(KEY_VALUE_HEADS):
-        mine = []
-        for (of_group, column), block_ref in zip(pieces, block_refs):
-            if of_group == group:
-                values = block_ref[:, HEAD_SIZE:].astype(jnp.float32).T.astype(jnp.bfloat16)
-                ones = jnp.ones((ONES_ROWS, values.shape[1]), jnp.bfloat16)
-                mine.append((column, block_ref, jnp.concatenate([values, ones], axis=0)))
-        for owner in range(2):
-            for tile in range(heads_per_group // per_tile):
-                head = group * heads_per_group + tile * per_tile
-                tasks += [
-                    (owner, head, column, block_ref, mixer)
-                    for column, block_ref, mixer in mine
-                    if not (column is None and owner)
-                ]
-
-    def score(number):
-        owner, head, column, block_ref, _ = tasks[number]
+    tasks = [
+        (owner, group * heads_per_group + tile * per_tile, group, number)
+        for number in range(count)
+        for group in range(KEY_VALUE_HEADS)
+        for owner in range(1 if columns[number] is None else 2)
+        for tile in range(heads_per_group // per_tile)
+    ]
+    mixers = {}
+
+    def score(index):
+        owner, head, group, number = tasks[index]
+        of = slice(group * HEAD_SIZE, (group + 1) * HEAD_SIZE)
+        if (number, group) not in mixers:
+            if not group:
+                for copy in copies[2 * number]:
+                    copy.wait()
+            mixers[number, group] = None
         rows = jnp.concatenate(
             [
                 queries[owner][:, h * HEAD_SIZE : (h + 1) * HEAD_SIZE]
@@ -257,29 +287,29 @@
             ],
             axis=0,
         )
-        keys = block_ref.shape[0]
+        keys = held[2 * number].shape[0]
         high = None
         for low in range(0, keys, PIECE):
             cut = slice(low, min(low + PIECE, keys))
             scores = lax.dot_general(
-                block_ref[cut, :HEAD_SIZE],
+                held[2 * number][cut, of],
                 rows,
                 (((1,), (1,)), ((), ())),
                 preferred_element_type=jnp.float32,
             )
-            if column is None:
+            if columns[number] is None:
                 key = lax.broadcasted_iota(jnp.int32, scores.shape, 0) + low
                 token = lax.broadcasted_iota(jnp.int32, scores.shape, 1) % tokens
                 scores = jnp.where(key <= token, scores, -SKIPPED)
-            score_refs[number % 2][cut, :] = scores
+            score_refs[index % 2][cut, :] = scores
             part = jnp.max(scores, axis=0, keepdims=True)
             high = part if high is None else jnp.maximum(high, part)
         return high * factor
 
     seen = set()
     high = score(0)
-    for number, (owner, head, column, block_ref, mixer) in enumerate(tasks):
-        following = score(number + 1) if number + 1 < len(tasks) else None
+    for index, (owner, head, group, number) in enumerate(tasks):
+        following = score(index + 1) if index + 1 < len(tasks) else None
         at = slice(head * tokens, head * tokens + TILE)
         if (owner, head) in seen:
             source = (stats_refs[owner], out_refs[owner])
@@ -289,6 +319,7 @@
             source = (given[owner], given[2 + owner])
         seen.add((owner, head))
         top = source[0][0:1, at] if source else jnp.full((1, TILE), UNSEEN, jnp.float32)
+        column = columns[number]
         if column is None:
             high = jnp.maximum(top, high)
             shift = high
@@ -296,14 +327,17 @@
             chosen = chosen_ref[column : column + 1, owner * TILE : (owner + 1) * TILE] > 0.5
             high = jnp.maximum(top, jnp.where(chosen, high, UNSEEN))
             shift = jnp.where(chosen, high, SKIPPED)
-        mixed = None
-        keys = block_ref.shape[0]
-        for low in range(0, keys, MIX_PIECE):
-            cut = slice(low, min(low + MIX_PIECE, keys))
-            scores = score_refs[number % 2][cut, :]
-            weights = jnp.exp2(scores * factor - shift).astype(jnp.bfloat16)
-            part = jnp.dot(mixer[:, cut], weights, preferred_element_type=jnp.float32)
-            mixed = part if mixed is None else mixed + part
+        if mixers[number, group] is None:
+            if not group:
+                for copy in copies[2 * number + 1]:
+                    copy.wait()
+            of = slice(group * HEAD_SIZE, (group + 1) * HEAD_SIZE)
+            values = held[2 * number + 1][:, of].astype(jnp.float32).T.astype(jnp.bfloat16)
+            ones = jnp.ones((ONES_ROWS, values.shape[1]), jnp.bfloat16)
+            mixers[number, group] = jnp.concatenate([values, ones], axis=0)
+        scores = score_refs[index % 2][: held[2 * number].shape[0], :]
+        weights = jnp.exp2(scores * factor - shift).astype(jnp.bfloat16)
+        mixed = jnp.dot(mixers[number, group], weights, preferred_element_type=jnp.float32)
         out, total = mixed[:HEAD_SIZE], mixed[HEAD_SIZE : HEAD_SIZE + 1]
         if source:
             fade = jnp.exp2(top - high)
@@ -315,24 +349,34 @@
         high = following
 
 
-def attend(queries, chosen, state, pieces, blocks, last=False):
+def attend(queries, chosen, state, columns, blocks, last=False):
     tokens = queries[0].shape[0]
     span = QUERY_HEADS * tokens
     stats = jax.ShapeDtypeStruct((8, span), jnp.float32)
     out = jax.ShapeDtypeStruct((HEAD_SIZE, span), jnp.float32)
     sent = jax.ShapeDtypeStruct((HEAD_SIZE, span), jnp.bfloat16)
     count = len(blocks)
-    keys = sum(b.shape[0] for b in blocks)
+    keys = sum(b.shape[0] for b in blocks) // 2
+    longest = max(b.shape[0] for b in blocks)
+    here = pl.BlockSpec(memory_space=pltpu.HBM)
+    aliases = {3: 0, 4: 1, 5: 2} | ({} if last else {6: 3}) if state else {}
     return pl.pallas_call(
-        lambda *refs: attention_kernel(pieces, state is None, count, *refs),
+        lambda *refs: attention_kernel(columns, state is None, *refs),
         out_shape=(stats, stats, out, sent if last else out),
-        scratch_shapes=[pltpu.VMEM((max(b.shape[0] for b in blocks), TILE), jnp.float32)] * 2,
+        input_output_aliases=aliases,
+        in_specs=[pl.BlockSpec()] * (3 + len(state or ()))
+        + [here] * count,
+        scratch_shapes=[pltpu.VMEM((longest, TILE), jnp.float32)] * 2
+        + [
+            pltpu.VMEM((count, longest, blocks[0].shape[1]), jnp.bfloat16),
+            pltpu.SemaphoreType.DMA((count * PARTS,)),
+        ],
         cost_estimate=pl.CostEstimate(
-            flops=4 * keys * span * HEAD_SIZE,
-            bytes_accessed=16 * HEAD_SIZE * span + keys * HEAD_SIZE * 4,
-            transcendentals=keys * span,
+            flops=8 * keys * span * HEAD_SIZE,
+            bytes_accessed=16 * HEAD_SIZE * span + keys * HEAD_SIZE * 8,
+            transcendentals=2 * keys * span,
         ),
-        compiler_params=pltpu.CompilerParams(vmem_limit_bytes=KERNEL_BYTES),
+        compiler_params=pltpu.CompilerParams(vmem_limit_bytes=ATTEND_BYTES),
         name="attend_blocks",
     )(*queries, chosen, *(state or ()), *blocks)
 
@@ -346,9 +390,9 @@
     residual_ref,
     gain_ref,
     extra_ref,
-    hidden_ref,
-    packed_ref,
+    *refs,
 ):
+    hidden_ref, packed_ref = refs[-2:]
     tokens, width = residual_ref.shape
     near_top, far_top = near_stats[0:1, :], far_stats[0:1, :]
     ceiling = jnp.maximum(near_top, far_top)
@@ -375,11 +419,19 @@
     packed_ref[:, width:] = extra_ref[...]
 
 
-def expert_kernel(parties, rows_count, *refs):
+def expert_kernel(parties, rows_count, load, *refs):
     who_ref = refs[0]
     row_refs = refs[1 : 1 + rows_count]
     weight_refs = refs[1 + rows_count : 7 + rows_count]
-    out_refs = refs[7 + rows_count :]
+    out_refs = refs[7 + rows_count : 7 + 2 * rows_count]
+    copies = [[]] * 6
+    if load:
+        held_refs, arrived = refs[-7:-1], refs[-1]
+        copies = [
+            fetch(source, held_ref, arrived, number * WEIGHT_PARTS, WEIGHT_PARTS)
+            for number, (source, held_ref) in enumerate(zip(weight_refs, held_refs))
+        ]
+        weight_refs = held_refs
     tokens, width = out_refs[0].shape
     block = jnp.concatenate([r[...] for r in row_refs], axis=0)
     inputs = block[:, :width]
@@ -391,11 +443,15 @@
         here = (lane == who_ref[slot]) | (lane == who_ref[slot] + parties)
         weight = jnp.sum(jnp.where(here, extra, 0.0), axis=1, keepdims=True)
         inner = []
+        for copy in copies[3 * slot] + copies[3 * slot + 1]:
+            copy.wait()
         for low in range(0, gate_ref.shape[2], TILE):
             cut = slice(low, low + TILE)
             gate = jnp.dot(inputs, gate_ref[0, :, cut], preferred_element_type=jnp.float32)
             up = jnp.dot(inputs, up_ref[0, :, cut], preferred_element_type=jnp.float32)
             inner.append((gate / (1.0 + jnp.exp(-gate)) * up).astype(jnp.bfloat16))
+        for copy in copies[3 * slot + 2]:
+            copy.wait()
         part = weight * jnp.dot(
             jnp.concatenate(inner, axis=1), down_ref[0], preferred_element_type=jnp.float32
         )
@@ -404,14 +460,17 @@
         out_ref[...] = result[n * tokens : (n + 1) * tokens, :].astype(out_ref.dtype)
 
 
-def run_experts(parties, who, rows, weights, out_types):
+def run_experts(parties, who, rows, weights, out_types, load=False):
     tokens = rows[0].shape[0]
     _, width, hidden = weights[0].shape
-    vmem = pl.BlockSpec(memory_space=pltpu.VMEM)
+    held = [jax.ShapeDtypeStruct(w.shape, w.dtype) for w in weights] if load else []
     return pl.pallas_call(
-        lambda *refs: expert_kernel(parties, len(rows), *refs),
-        in_specs=[pl.BlockSpec(memory_space=pltpu.SMEM)] + [vmem] * (len(rows) + len(weights)),
-        out_shape=[jax.ShapeDtypeStruct((tokens, width), t) for t in out_types],
+        lambda *refs: expert_kernel(parties, len(rows), load, *refs),
+        in_specs=[pl.BlockSpec(memory_space=pltpu.SMEM)]
+        + [pl.BlockSpec()] * len(rows)
+        + [pl.BlockSpec(memory_space=pltpu.HBM) if load else pl.BlockSpec()] * len(weights),
+        out_shape=[jax.ShapeDtypeStruct((tokens, width), t) for t in out_types] + held,
+        scratch_shapes=[pltpu.SemaphoreType.DMA((len(weights) * WEIGHT_PARTS,))] if load else [],
         cost_estimate=pl.CostEstimate(
             flops=12 * tokens * len(rows) * width * hidden,
             bytes_accessed=12 * width * hidden,
@@ -445,7 +504,6 @@
     my_deep = place // (across * CORES)
     my_across = place // CORES % across
     my_core = place % CORES
-    groups = range(KEY_VALUE_HEADS)
 
     def moved(array, step_deep, step_across, step_core=0):
         return lax.ppermute(
@@ -461,22 +519,21 @@
         ]
     )
 
-    def paired(keys, values, group):
-        of = slice(group * HEAD_SIZE, (group + 1) * HEAD_SIZE)
-        return jnp.concatenate([keys[:, of], values[:, of]], axis=1)
-
     blocks = {}
-    for dz in order:
-        for group in groups:
+    for part, array in (("k", rotated_cache_keys), ("v", stored_cache_values)):
+        for dz in order:
             if dz == 0:
-                column = paired(rotated_cache_keys, stored_cache_values, group)
+                column = array
             elif dz <= deep // 2:
-                column = moved(blocks[dz - 1, 0, group], 1, 0)
+                column = moved(blocks[dz - 1, 0, part], 1, 0)
             else:
-                column = moved(blocks[(dz + 1) % deep, 0, group], -1, 0)
-            blocks[dz, 0, group] = column
+                column = moved(blocks[(dz + 1) % deep, 0, part], -1, 0)
+            blocks[dz, 0, part] = column
             for dx in range(1, across):
-                blocks[dz, dx, group] = moved(column, 0, dx)
+                if part == "v" and dz == deep - 1:
+                    blocks[dz, dx, part] = moved(blocks[0, dx, part], -1, 0)
+                else:
+                    blocks[dz, dx, part] = moved(column, 0, dx)
 
     pair_queries = (queries, moved(queries, 0, 0, 1))
     chosen = jnp.concatenate(
@@ -494,15 +551,15 @@
     who = jnp.stack([place, place + 1 - 2 * my_core])
 
     state = None
-    for dz in order:
-        for dx in range(across):
-            pieces = [(g, dz * across + dx) for g in groups]
-            given = [blocks[dz, dx, g] for g in groups]
-            if state is None:
-                pieces = [(g, None) for g in groups] + pieces
-                given = [paired(segment_new_keys, segment_new_values, g) for g in groups] + given
-            last = dz == order[-1] and dx == across - 1
-            state = attend(pair_queries, chosen, state, pieces, given, last)
+    stages = stages_of(deep, across)
+    for number, stage in enumerate(stages):
+        columns = [dz * across + dx for dz, dx in stage]
+        given = [blocks[dz, dx, part] for dz, dx in stage for part in "kv"]
+        if state is None:
+            columns = [None] + columns
+            given = [segment_new_keys, segment_new_values] + given
+        last = number == len(stages) - 1
+        state = attend(pair_queries, chosen, state, columns, given, last)
 
     mixing = gate_scores / jnp.sum(gate_scores, axis=1, keepdims=True)
     experts = jnp.arange(parties, dtype=jnp.int32)
@@ -525,8 +582,9 @@
         name="finish_attention",
     )
     arrived = (moved(far_stats, 0, 0, 1), moved(far_out, 0, 0, 1))
+    gain = norm_gain.reshape(1, -1)
     hidden_state, packed = finish(
-        near_stats, near_out, *arrived, out_weight, residual_in, norm_gain.reshape(1, -1), extra
+        near_stats, near_out, *arrived, out_weight, residual_in, gain, extra
     )
 
     rows = {(0, 0): packed}
@@ -536,21 +594,32 @@
         for dx in range(1, across):
             rows[dz, dx] = moved(rows[dz, 0], 0, dx)
 
-    mixture = hidden_state
-    for dz in order:
+    wide = range(1, across)
+    column, *on_chip = run_experts(parties, who, [packed], weights, [jnp.float32], True)
+    mixture = hidden_state + column
+    beside = [(0, dx) for dx in wide]
+    for dz in [d for d in order if 1 < d < deep - 1] + [1, deep - 1]:
+        direct = dz == deep - 1
+        spots_now = [(dz, dx) for dx in range(across)] + beside
         results = run_experts(
             parties,
             who,
-            [rows[dz, dx] for dx in range(across)],
-            weights,
-            [jnp.float32] + [jnp.bfloat16] * (across - 1),
-        )
+            [rows[spot] for spot in spots_now],
+            on_chip,
+            [jnp.bfloat16 if direct else jnp.float32]
+            + [jnp.bfloat16] * (len(spots_now) - 1),
+        )
+        for n, (_, dx) in enumerate(beside):
+            mixture = mixture + moved(results[across + n], 0, -dx).astype(jnp.float32)
+        beside = []
+        if direct:
+            for dx in range(across):
+                mixture = mixture + moved(results[dx], -dz, -dx).astype(jnp.float32)
+            continue
         column = results[0]
-        for dx in range(1, across):
+        for dx in wide:
             column = column + moved(results[dx], 0, -dx).astype(jnp.float32)
-        if dz:
-            column = moved(column.astype(jnp.bfloat16), -dz, 0).astype(jnp.float32)
-        mixture = mixture + column
+        mixture = mixture + moved(column.astype(jnp.bfloat16), -dz, 0).astype(jnp.float32)
     return mixture.astype(jnp.bfloat16)
 
 

time: 131 us -> 138 us (1.053)
  waiting for transfers between devices: 46.2 us -> 38.5 us
  Pallas kernels: 37.5 us -> 43.8 us
  starting transfers between devices: 37.5 us -> 43.7 us
    ppermute x35, waiting for transfers between devices: 46.2 us -> 38.5 us  [moved(): lax.ppermute(array, 'blk', shift_pairs(deep, across, step_deep, step_acro...]
    pallas_call x13, Pallas kernels: 37.5 us -> 43.8 us  [the longest x8 24.1 us: attend(): pl.pallas_call(lambda *refs: attention_kernel(columns, state is None, *re...]
    ppermute x35, starting transfers between devices: 37.5 us -> 43.7 us  [moved(): lax.ppermute(array, 'blk', shift_pairs(deep, across, step_deep, step_acro...]
    unnamed x31 -> x23, local copies, waits for them, and re-layouts: 2.13 us -> 5.8 us
    concatenate x3 -> x0, other arithmetic: 2.2 us -> none  [paired(): return jnp.concatenate([keys[:, of], values[:, of]], axis=1)]
    slice x3 -> x0, local copies, waits for them, and re-layouts: 1.87 us -> none  [paired(): return jnp.concatenate([keys[:, of], values[:, of]], axis=1)]
  transfers between devices with their start and end apart: 35 -> 35, of which waited for: 14 -> 11; matrix products, arithmetic and copies ran while one was open for 3% -> 3% of each run, Pallas kernels for 29% -> 32%
where the time goes in v4:
time: 138 us; the launch traced here: 137 us
  Pallas kernels  43.8 us (32%)
  starting transfers between devices  43.7 us (32%)
  waiting for transfers between devices  38.5 us (28%)
  local copies, waits for them, and re-layouts  6.24 us (5%)
  other arithmetic  3.9 us (3%)
    ppermute x35, starting transfers between devices, moved(): lax.ppermute(array, 'blk', shift_pairs(deep, across, step_deep, step_acro...  43.7 us
    ppermute x35, waiting for transfers between devices, moved(): lax.ppermute(array, 'blk', shift_pairs(deep, across, step_deep, step_acro...  38.5 us
    pallas_call x8, Pallas kernels, attend(): pl.pallas_call(lambda *refs: attention_kernel(columns, state is None, *re...  24.1 us
    pallas_call x4, Pallas kernels, run_experts(): pl.pallas_call(lambda *refs: expert_kernel(parties, len(rows), load, *ref...  18 us
    unnamed x23, local copies, waits for them, and re-layouts  5.8 us
  transfers between devices with their start and end apart: 35, of which 11 were waited for; matrix products, arithmetic and copies ran while one was open for 3% of the time, Pallas kernels for 32%

profile of v4, /device:TPU:0, one launch (start us, length us, event | category | flops | bytes accessed | tf_op | source)
XLA Modules:
  0.0 136.5 jit_solution(13639707211563466583)
XLA Ops:
  0.0 0.5 collective-permute-start
  0.5 2.5 %collective-permute-start.3 = (bf16[512,256]{1,0:T(8,128)(2,1)}, bf16[512,256]{1,0:T(8,128)(2,1)S(1)}, u32[]{:S(2)}, u32[]{:S(2)}) collective-permute-start(bf16[512,256]{1,0:T(8,128)(2,1)} %refs_6_.1), channel_id=1, source_target_pairs={{0,2},{1,3},{2,0},{3,1},{4,6},{5,7},{6,4},{7,5},{8,10},{9,11},{10,... | collective-permute-start | bytes 786440 | tf_op jit(solution)/shard_map/ppermute | solution.py:509
  3.0 1.6 %collective-permute-start.4 = (bf16[512,256]{1,0:T(8,128)(2,1)}, bf16[512,256]{1,0:T(8,128)(2,1)S(1)}, u32[]{:S(2)}, u32[]{:S(2)}) collective-permute-start(bf16[512,256]{1,0:T(8,128)(2,1)} %refs_5_.1), channel_id=1, source_target_pairs={{0,4},{1,5},{2,6},{3,7},{4,8},{5,9},{6,10},{7,11},{8,12},{9,13},{1... | collective-permute-start | bytes 786440 | tf_op jit(solution)/shard_map/ppermute | solution.py:509
  4.5 1.6 %collective-permute-start.5 = (bf16[512,256]{1,0:T(8,128)(2,1)}, bf16[512,256]{1,0:T(8,128)(2,1)S(1)}, u32[]{:S(2)}, u32[]{:S(2)}) collective-permute-start(bf16[512,256]{1,0:T(8,128)(2,1)} %refs_6_.1), channel_id=1, source_target_pairs={{0,4},{1,5},{2,6},{3,7},{4,8},{5,9},{6,10},{7,11},{8,12},{9,13},{1... | collective-permute-start | bytes 786440 | tf_op jit(solution)/shard_map/ppermute | solution.py:509
  6.1 1.4 %collective-permute-done.1 = s32[64,8]{0,1:T(8,128)S(1)} collective-permute-done((s32[64,8]{0,1:T(8,128)}, s32[64,8]{0,1:T(8,128)S(1)}, u32[]{:S(2)}, u32[]{:S(2)}) %collective-permute-start.1) | collective-permute-done | bytes 2080 | tf_op jit(solution)/shard_map/ppermute | solution.py:509
  7.5 0.5 collective-permute-start.2
  8.0 2.2 %collective-permute-start.10 = (bf16[512,256]{1,0:T(8,128)(2,1)}, bf16[512,256]{1,0:T(8,128)(2,1)S(1)}, u32[]{:S(2)}, u32[]{:S(2)}) collective-permute-start(bf16[512,256]{1,0:T(8,128)(2,1)} %refs_5_.1), channel_id=1, source_target_pairs={{0,12},{1,13},{2,14},{3,15},{4,0},{5,1},{6,2},{7,3},{8,4},{9,5},{1... | collective-permute-start | bytes 786440 | tf_op jit(solution)/shard_map/ppermute | solution.py:509
  10.3 4.2 %collective-permute-start.11 = (bf16[512,256]{1,0:T(8,128)(2,1)}, bf16[512,256]{1,0:T(8,128)(2,1)S(1)}, u32[]{:S(2)}, u32[]{:S(2)}) collective-permute-start(bf16[512,256]{1,0:T(8,128)(2,1)} %refs_6_.1), channel_id=1, source_target_pairs={{0,12},{1,13},{2,14},{3,15},{4,0},{5,1},{6,2},{7,3},{8,4},{9,5},{1... | collective-permute-start | bytes 786440 | tf_op jit(solution)/shard_map/ppermute | solution.py:509
  14.5 1.5 %collective-permute-start.6 = (bf16[512,256]{1,0:T(8,128)(2,1)S(1)}, bf16[512,256]{1,0:T(8,128)(2,1)S(1)}, u32[]{:S(2)}, u32[]{:S(2)}) collective-permute-start(bf16[512,256]{1,0:T(8,128)(2,1)S(1)} %collective-permute-done.4.refs_7_), channel_id=1, source_target_pairs={{0,2},{1,3},{2,0},{3,1},{4,6},{5,7},{6,4},{7,5},{8,10},{9,11},{10,... | collective-permute-start | bytes 786440 | tf_op jit(solution)/shard_map/ppermute | solution.py:509
  16.0 3.9 %collective-permute-done.5.refs_8_ = bf16[512,256]{1,0:T(8,128)(2,1)S(1)} collective-permute-done((bf16[512,256]{1,0:T(8,128)(2,1)}, bf16[512,256]{1,0:T(8,128)(2,1)S(1)}, u32[]{:S(2)}, u32[]{:S(2)}) %collective-permute-start.5) | collective-permute-done | bytes 262176 | tf_op jit(solution)/shard_map/ppermute | solution.py:509
  19.8 0.3 collective-permute-start.7
  20.1 0.7 reduce_sum.18
  20.9 3.9 %collective-permute-done.10.refs_7_ = bf16[512,256]{1,0:T(8,128)(2,1)S(1)} collective-permute-done((bf16[512,256]{1,0:T(8,128)(2,1)}, bf16[512,256]{1,0:T(8,128)(2,1)S(1)}, u32[]{:S(2)}, u32[]{:S(2)}) %collective-permute-start.10) | collective-permute-done | bytes 262176 | tf_op jit(solution)/shard_map/ppermute | solution.py:509
  24.8 7.5 %collective-permute-start.9 = (bf16[512,256]{1,0:T(8,128)(2,1)S(1)}, bf16[512,256]{1,0:T(8,128)(2,1)S(1)}, u32[]{:S(2)}, u32[]{:S(2)}) collective-permute-start(bf16[512,256]{1,0:T(8,128)(2,1)S(1)} %collective-permute-done.5.refs_8_), channel_id=1, source_target_pairs={{0,4},{1,5},{2,6},{3,7},{4,8},{5,9},{6,10},{7,11},{8,12},{9,13},{1... | collective-permute-start | bytes 786440 | tf_op jit(solution)/shard_map/ppermute | solution.py:509
  32.3 0.7 broadcast_divide_fusion
  33.0 0.5 collective-permute-start.19
  33.6 0.7 select_reduce_fusion
  34.4 0.1 copy.48
  34.5 0.8 compare_reduce_fusion
  35.5 3.3 %collective-permute-done.8.refs_7_ = bf16[512,256]{1,0:T(8,128)(2,1)S(1)} collective-permute-done((bf16[512,256]{1,0:T(8,128)(2,1)S(1)}, bf16[512,256]{1,0:T(8,128)(2,1)S(1)}, u32[]{:S(2)}, u32[]{:S(2)}) %collective-permute-start.8) | collective-permute-done | bytes 262176 | tf_op jit(solution)/shard_map/ppermute | solution.py:509
  38.8 0.5 collective-permute-start.12
  39.3 2.3 %collective-permute-done.9.refs_8_ = bf16[512,256]{1,0:T(8,128)(2,1)S(1)} collective-permute-done((bf16[512,256]{1,0:T(8,128)(2,1)S(1)}, bf16[512,256]{1,0:T(8,128)(2,1)S(1)}, u32[]{:S(2)}, u32[]{:S(2)}) %collective-permute-start.9) | collective-permute-done | bytes 262176 | tf_op jit(solution)/shard_map/ppermute | solution.py:509
  41.6 0.5 collective-permute-start.13
  42.2 0.9 copy-done
  43.1 0.9 copy-done.7
  44.1 0.9 copy-done.8
  45.0 0.8 copy-done.9
  45.8 0.8 copy-done.10
  46.5 3.5 %attend_blocks.8 = (f32[8,1024]{1,0:T(8,128)S(1)}, f32[8,1024]{1,0:T(8,128)S(1)}, f32[128,1024]{1,0:T(8,128)S(1)}, f32[128,1024]{1,0:T(8,128)S(1)}) custom-call(bf16[64,2048]{1,0:T(8,128)(2,1)S(1)} %copy-done, bf16[64,2048]{1,0:T(8,128)(2,1)S(1)} %collective-permute-done.refs_1_, f32[8,512]{1,0:T(8,128)S(1)} %constant_dynamic-update-slice_fusion.refs_2_, ...), custom_call_target="tpu_custom_call" | custom-call | flops 603979776 | bytes 2686976 | tf_op jit(solution)/shard_map/attend_blocks/pallas_call | solution.py:363
  50.0 1.6 %collective-permute-start.14 = (bf16[512,256]{1,0:T(8,128)(2,1)S(1)}, bf16[512,256]{1,0:T(8,128)(2,1)S(1)}, u32[]{:S(2)}, u32[]{:S(2)}) collective-permute-start(bf16[512,256]{1,0:T(8,128)(2,1)S(1)} %collective-permute-done.10.refs_7_), channel_id=1, source_target_pairs={{0,2},{1,3},{2,0},{3,1},{4,6},{5,7},{6,4},{7,5},{8,10},{9,11},{10,... | collective-permute-start | bytes 786440 | tf_op jit(solution)/shard_map/ppermute | solution.py:509
  51.6 3.7 %collective-permute-start.15 = (bf16[512,256]{1,0:T(8,128)(2,1)S(1)}, bf16[512,256]{1,0:T(8,128)(2,1)S(1)}, u32[]{:S(2)}, u32[]{:S(2)}) collective-permute-start(bf16[512,256]{1,0:T(8,128)(2,1)S(1)} %collective-permute-done.3.refs_8_), channel_id=1, source_target_pairs={{0,12},{1,13},{2,14},{3,15},{4,0},{5,1},{6,2},{7,3},{8,4},{9,5},{1... | collective-permute-start | bytes 786440 | tf_op jit(solution)/shard_map/ppermute | solution.py:509
  55.3 2.9 %attend_blocks.9 = (f32[8,1024]{1,0:T(8,128)S(1)}, f32[8,1024]{1,0:T(8,128)S(1)}, f32[128,1024]{1,0:T(8,128)S(1)}, f32[128,1024]{1,0:T(8,128)S(1)}) custom-call(bf16[64,2048]{1,0:T(8,128)(2,1)S(1)} %copy-done, bf16[64,2048]{1,0:T(8,128)(2,1)S(1)} %collective-permute-done.refs_1_, ...), custom_call_target="tpu_custom_call", output_to_operand_aliasing={{0}: (3, {}), {1}: (4, {}), {2}: (5, {}), {3}: (6, {})} | custom-call | flops 536870912 | bytes 2621440 | tf_op jit(solution)/shard_map/attend_blocks/pallas_call | solution.py:363
  58.2 2.9 %attend_blocks.10 = (f32[8,1024]{1,0:T(8,128)S(1)}, f32[8,1024]{1,0:T(8,128)S(1)}, f32[128,1024]{1,0:T(8,128)S(1)}, f32[128,1024]{1,0:T(8,128)S(1)}) custom-call(bf16[64,2048]{1,0:T(8,128)(2,1)S(1)} %copy-done, bf16[64,2048]{1,0:T(8,128)(2,1)S(1)} %collective-permute-done.refs_1_, ...), custom_call_target="tpu_custom_call", output_to_operand_aliasing={{0}: (3, {}), {1}: (4, {}), {2}: (5, {}), {3}: (6, {})} | custom-call | flops 536870912 | bytes 2621440 | tf_op jit(solution)/shard_map/attend_blocks/pallas_call | solution.py:363
  61.1 2.9 %attend_blocks.11 = (f32[8,1024]{1,0:T(8,128)S(1)}, f32[8,1024]{1,0:T(8,128)S(1)}, f32[128,1024]{1,0:T(8,128)S(1)}, f32[128,1024]{1,0:T(8,128)S(1)}) custom-call(bf16[64,2048]{1,0:T(8,128)(2,1)S(1)} %copy-done, bf16[64,2048]{1,0:T(8,128)(2,1)S(1)} %collective-permute-done.refs_1_, ...), custom_call_target="tpu_custom_call", output_to_operand_aliasing={{0}: (3, {}), {1}: (4, {}), {2}: (5, {}), {3}: (6, {})} | custom-call | flops 536870912 | bytes 2621440 | tf_op jit(solution)/shard_map/attend_blocks/pallas_call | solution.py:363
  64.1 2.9 %attend_blocks.12 = (f32[8,1024]{1,0:T(8,128)S(1)}, f32[8,1024]{1,0:T(8,128)S(1)}, f32[128,1024]{1,0:T(8,128)S(1)}, f32[128,1024]{1,0:T(8,128)S(1)}) custom-call(bf16[64,2048]{1,0:T(8,128)(2,1)S(1)} %copy-done, bf16[64,2048]{1,0:T(8,128)(2,1)S(1)} %collective-permute-done.refs_1_, ...), custom_call_target="tpu_custom_call", output_to_operand_aliasing={{0}: (3, {}), {1}: (4, {}), {2}: (5, {}), {3}: (6, {})} | custom-call | flops 536870912 | bytes 2621440 | tf_op jit(solution)/shard_map/attend_blocks/pallas_call | solution.py:363
  67.0 2.9 %attend_blocks.13 = (f32[8,1024]{1,0:T(8,128)S(1)}, f32[8,1024]{1,0:T(8,128)S(1)}, f32[128,1024]{1,0:T(8,128)S(1)}, f32[128,1024]{1,0:T(8,128)S(1)}) custom-call(bf16[64,2048]{1,0:T(8,128)(2,1)S(1)} %copy-done, bf16[64,2048]{1,0:T(8,128)(2,1)S(1)} %collective-permute-done.refs_1_, ...), custom_call_target="tpu_custom_call", output_to_operand_aliasing={{0}: (3, {}), {1}: (4, {}), {2}: (5, {}), {3}: (6, {})} | custom-call | flops 536870912 | bytes 2621440 | tf_op jit(solution)/shard_map/attend_blocks/pallas_call | solution.py:363
  70.0 2.9 %attend_blocks.14 = (f32[8,1024]{1,0:T(8,128)S(1)}, f32[8,1024]{1,0:T(8,128)S(1)}, f32[128,1024]{1,0:T(8,128)S(1)}, f32[128,1024]{1,0:T(8,128)S(1)}) custom-call(bf16[64,2048]{1,0:T(8,128)(2,1)S(1)} %copy-done, bf16[64,2048]{1,0:T(8,128)(2,1)S(1)} %collective-permute-done.refs_1_, ...), custom_call_target="tpu_custom_call", output_to_operand_aliasing={{0}: (3, {}), {1}: (4, {}), {2}: (5, {}), {3}: (6, {})} | custom-call | flops 536870912 | bytes 2621440 | tf_op jit(solution)/shard_map/attend_blocks/pallas_call | solution.py:363
  72.9 3.1 %attend_blocks.15 = (f32[8,1024]{1,0:T(8,128)S(1)}, f32[8,1024]{1,0:T(8,128)S(1)}, f32[128,1024]{1,0:T(8,128)S(1)}, bf16[128,1024]{1,0:T(8,128)(2,1)S(1)}) custom-call(bf16[64,2048]{1,0:T(8,128)(2,1)S(1)} %copy-done, bf16[64,2048]{1,0:T(8,128)(2,1)S(1)} %collective-permute-done.refs_1_, ...), custom_call_target="tpu_custom_call", output_to_operand_aliasing={{0}: (3, {}), {1}: (4, {}), {2}: (5, {})} | custom-call | flops 536870912 | bytes 2621440 | tf_op jit(solution)/shard_map/attend_blocks/pallas_call | solution.py:363
  76.1 0.5 collective-permute-start.16
  76.7 1.0 collective-permute-done.16.far_stats
  77.7 1.7 %finish_attention.1 = (f32[64,1024]{1,0:T(8,128)S(1)}, bf16[64,1152]{1,0:T(8,128)(2,1)}) custom-call(f32[8,1024]{1,0:T(8,128)S(1)} %get-tuple-element.81.near_stats, f32[128,1024]{1,0:T(8,128)S(1)} %get-tuple-element.82.near_out, f32[8,1024]{1,0:T(8,128)S(1)} %collective-permute-done.16.far_stats, bf16[128,1024]{1,0:T(8,128)(2,1)S(1)} %collective-permute-done.17.far_out, ...), custom_call_target="tpu_custom_call" | custom-call | tf_op jit(solution)/shard_map/finish_attention/pallas_call | solution.py:586
  79.4 1.0 collective-permute-start.27
  80.4 10.2 %collective-permute-done.21.refs_1_ = bf16[64,1152]{1,0:T(8,128)(2,1)} collective-permute-done((bf16[64,1152]{1,0:T(8,128)(2,1)}, bf16[64,1152]{1,0:T(8,128)(2,1)}, u32[]{:S(2)}, u32[]{:S(2)}) %collective-permute-start.21) | collective-permute-done | bytes 147488 | tf_op jit(solution)/shard_map/ppermute | solution.py:509
  90.6 0.3 collective-permute-start.31
  91.0 0.6 collective-permute-start.23
  91.6 5.1 %collective-permute-done.31.refs_1_ = bf16[64,1152]{1,0:T(8,128)(2,1)S(1)} collective-permute-done((bf16[64,1152]{1,0:T(8,128)(2,1)}, bf16[64,1152]{1,0:T(8,128)(2,1)S(1)}, u32[]{:S(2)}, u32[]{:S(2)}) %collective-permute-start.31) | collective-permute-done | bytes 147488 | tf_op jit(solution)/shard_map/ppermute | solution.py:509
  96.6 0.6 collective-permute-start.22
  97.3 1.5 %collective-permute-start.28 = (bf16[64,1152]{1,0:T(8,128)(2,1)}, bf16[64,1152]{1,0:T(8,128)(2,1)S(1)}, u32[]{:S(2)}, u32[]{:S(2)}) collective-permute-start(bf16[64,1152]{1,0:T(8,128)(2,1)} %collective-permute-done.27.refs_1_), channel_id=1, source_target_pairs={{0,2},{1,3},{2,0},{3,1},{4,6},{5,7},{6,4},{7,5},{8,10},{9,11},{10,... | collective-permute-start | bytes 442376 | tf_op jit(solution)/shard_map/ppermute | solution.py:509
  98.7 0.6 collective-permute-start.32
  99.3 1.4 %copy-done.4 = bf16[1,768,1024]{2,1,0:T(8,128)(2,1)S(1)} copy-done((bf16[1,768,1024]{2,1,0:T(8,128)(2,1)S(1)}, bf16[1,768,1024]{2,1,0:T(8,128)(2,1)}, u32[]{:S(2)}) %copy-start.4) | copy-done | bytes 1572888
  100.7 10.5 %run_experts.4 = (f32[64,1024]{1,0:T(8,128)S(1)}, bf16[1,1024,768]{2,1,0:T(8,128)(2,1)S(1)}, bf16[1,1024,768]{2,1,0:T(8,128)(2,1)S(1)}, bf16[1,768,1024]{2,1,0:T...) custom-call(s32[2]{0:T(128)S(1)} %pad_add_fusion.refs_0_, ...), custom_call_target="tpu_custom_call" | custom-call | flops 603979776 | bytes 9437184 | tf_op jit(solution)/shard_map/run_experts/pallas_call | solution.py:467
  111.2 3.0 %run_experts.5 = (f32[64,1024]{1,0:T(8,128)S(1)}, bf16[64,1024]{1,0:T(8,128)(2,1)S(1)}, bf16[64,1024]{1,0:T(8,128)(2,1)S(1)}) custom-call(s32[2]{0:T(128)S(1)} %pad_add_fusion.refs_0_, bf16[64,1152]{1,0:T(8,128)(2,1)} %collective-permute-done.21.refs_1_, bf16[64,1152]{1,0:T(8,128)(2,1)S(1)} %collective-permute-done.22.refs_2_, ...), custom_call_target="tpu_custom_call" | custom-call | flops 1811939328 | bytes 9437184 | tf_op jit(solution)/shard_map/run_experts/pallas_call | solution.py:467
  114.2 1.5 %collective-permute-start.25 = (bf16[64,1024]{1,0:T(8,128)(2,1)S(1)}, bf16[64,1024]{1,0:T(8,128)(2,1)S(1)}, u32[]{:S(2)}, u32[]{:S(2)}) collective-permute-start(bf16[64,1024]{1,0:T(8,128)(2,1)S(1)} %get-tuple-element.96), channel_id=1, source_target_pairs={{0,2},{1,3},{2,0},{3,1},{4,6},{5,7},{6,4},{7,5},{8,10},{9,11},{10,... | collective-permute-start | bytes 393224 | tf_op jit(solution)/shard_map/ppermute | solution.py:509
  115.7 0.6 collective-permute-start.24
  116.3 2.5 %run_experts.6 = (f32[64,1024]{1,0:T(8,128)S(1)}, bf16[64,1024]{1,0:T(8,128)(2,1)S(1)}) custom-call(s32[2]{0:T(128)S(1)} %pad_add_fusion.refs_0_, bf16[64,1152]{1,0:T(8,128)(2,1)} %collective-permute-done.27.refs_1_, bf16[64,1152]{1,0:T(8,128)(2,1)S(1)} %collective-permute-done.28.refs_2_, bf16[1,1024,768]{2,1,0:T(8,128)(2,1)S(1)} %get-tuple-element.88.refs_4_.refs_3_, ...), custom_call_target="tpu_custom_call" | custom-call | flops 1207959552 | bytes 9437184 | tf_op jit(solution)/shard_map/run_experts/pallas_call | solution.py:467
  118.8 1.5 %collective-permute-start.29 = (bf16[64,1024]{1,0:T(8,128)(2,1)S(1)}, bf16[64,1024]{1,0:T(8,128)(2,1)S(1)}, u32[]{:S(2)}, u32[]{:S(2)}) collective-permute-start(bf16[64,1024]{1,0:T(8,128)(2,1)S(1)} %get-tuple-element.98), channel_id=1, source_target_pairs={{0,2},{1,3},{2,0},{3,1},{4,6},{5,7},{6,4},{7,5},{8,10},{9,11},{10,... | collective-permute-start | bytes 393224 | tf_op jit(solution)/shard_map/ppermute | solution.py:509
  120.3 2.1 %run_experts.7 = (bf16[64,1024]{1,0:T(8,128)(2,1)S(1)}, bf16[64,1024]{1,0:T(8,128)(2,1)S(1)}) custom-call(s32[2]{0:T(128)S(1)} %pad_add_fusion.refs_0_, bf16[64,1152]{1,0:T(8,128)(2,1)S(1)} %collective-permute-done.31.refs_1_, bf16[64,1152]{1,0:T(8,128)(2,1)S(1)} %collective-permute-done.32.refs_2_, ...), custom_call_target="tpu_custom_call" | custom-call | flops 1207959552 | bytes 9437184 | tf_op jit(solution)/shard_map/run_experts/pallas_call | solution.py:467
  122.5 0.1 collective-permute-start.34
  122.6 4.3 %collective-permute-start.26 = (bf16[64,1024]{1,0:T(8,128)(2,1)S(1)}, bf16[64,1024]{1,0:T(8,128)(2,1)S(1)}, u32[]{:S(2)}, u32[]{:S(2)}) collective-permute-start(bf16[64,1024]{1,0:T(8,128)(2,1)S(1)} %add_convert_fusion.2), channel_id=1, source_target_pairs={{0,8},{1,9},{2,10},{3,11},{4,12},{5,13},{6,14},{7,15},{8,0},{9,1},... | collective-permute-start | bytes 393224 | tf_op jit(solution)/shard_map/ppermute | solution.py:509
  127.0 1.2 collective-permute-start.30
  128.2 2.4 %collective-permute-done.33 = bf16[64,1024]{1,0:T(8,128)(2,1)S(1)} collective-permute-done((bf16[64,1024]{1,0:T(8,128)(2,1)S(1)}, bf16[64,1024]{1,0:T(8,128)(2,1)S(1)}, u32[]{:S(2)}, u32[]{:S(2)}) %collective-permute-start.33) | collective-permute-done | bytes 131104 | tf_op jit(solution)/shard_map/ppermute | solution.py:509
  130.7 2.3 %collective-permute-done.34 = bf16[64,1024]{1,0:T(8,128)(2,1)S(1)} collective-permute-done((bf16[64,1024]{1,0:T(8,128)(2,1)S(1)}, bf16[64,1024]{1,0:T(8,128)(2,1)S(1)}, u32[]{:S(2)}, u32[]{:S(2)}) %collective-permute-start.34) | collective-permute-done | bytes 131104 | tf_op jit(solution)/shard_map/ppermute | solution.py:509
  133.0 2.8 %collective-permute-done.26 = bf16[64,1024]{1,0:T(8,128)(2,1)S(1)} collective-permute-done((bf16[64,1024]{1,0:T(8,128)(2,1)S(1)}, bf16[64,1024]{1,0:T(8,128)(2,1)S(1)}, u32[]{:S(2)}, u32[]{:S(2)}) %collective-permute-start.26) | collective-permute-done | bytes 131104 | tf_op jit(solution)/shard_map/ppermute | solution.py:509
  135.8 0.8 add_convert_fusion
  (63 shorter events, 0.9 us)
Async XLA Ops:
  0.0 8.0 %collective-permute-start = (bf16[64,2048]{1,0:T(8,128)(2,1)}, bf16[64,2048]{1,0:T(8,128)(2,1)S(1)}, u32[]{:S(2)}, u32[]{:S(2)}) collective-permute-start(bf16[64,2048]{1,0:T(8,128)(2,1)} %refs_0_.15), channel_id=1, source_target_pairs={{0,1},{1,0},{2,3},{3,2},{4,5},{5,4},{6,7},{7,6},{8,9},{9,8},{10,11... | collective-permute-start | bytes 786440 | tf_op jit(solution)/shard_map/ppermute | solution.py:509
  0.5 9.8 %collective-permute-start.3 = (bf16[512,256]{1,0:T(8,128)(2,1)}, bf16[512,256]{1,0:T(8,128)(2,1)S(1)}, u32[]{:S(2)}, u32[]{:S(2)}) collective-permute-start(bf16[512,256]{1,0:T(8,128)(2,1)} %refs_6_.1), channel_id=1, source_target_pairs={{0,2},{1,3},{2,0},{3,1},{4,6},{5,7},{6,4},{7,5},{8,10},{9,11},{10,... | collective-permute-start | bytes 786440 | tf_op jit(solution)/shard_map/ppermute | solution.py:509
  3.0 11.5 %collective-permute-start.4 = (bf16[512,256]{1,0:T(8,128)(2,1)}, bf16[512,256]{1,0:T(8,128)(2,1)S(1)}, u32[]{:S(2)}, u32[]{:S(2)}) collective-permute-start(bf16[512,256]{1,0:T(8,128)(2,1)} %refs_5_.1), channel_id=1, source_target_pairs={{0,4},{1,5},{2,6},{3,7},{4,8},{5,9},{6,10},{7,11},{8,12},{9,13},{1... | collective-permute-start | bytes 786440 | tf_op jit(solution)/shard_map/ppermute | solution.py:509
  4.5 15.3 %collective-permute-start.5 = (bf16[512,256]{1,0:T(8,128)(2,1)}, bf16[512,256]{1,0:T(8,128)(2,1)S(1)}, u32[]{:S(2)}, u32[]{:S(2)}) collective-permute-start(bf16[512,256]{1,0:T(8,128)(2,1)} %refs_6_.1), channel_id=1, source_target_pairs={{0,4},{1,5},{2,6},{3,7},{4,8},{5,9},{6,10},{7,11},{8,12},{9,13},{1... | collective-permute-start | bytes 786440 | tf_op jit(solution)/shard_map/ppermute | solution.py:509
  6.1 1.4 %collective-permute-start.1 = (s32[64,8]{0,1:T(8,128)}, s32[64,8]{0,1:T(8,128)S(1)}, u32[]{:S(2)}, u32[]{:S(2)}) collective-permute-start(s32[64,8]{0,1:T(8,128)} %param.19), channel_id=1, source_target_pairs={{0,1},{1,0},{2,3},{3,2},{4,5},{5,4},{6,7},{7,6},{8,9},{9,8},{10,11... | collective-permute-start | bytes 6152 | tf_op jit(solution)/shard_map/ppermute | solution.py:509
  7.5 13.3 %collective-permute-start.2 = (bf16[512,256]{1,0:T(8,128)(2,1)}, bf16[512,256]{1,0:T(8,128)(2,1)S(1)}, u32[]{:S(2)}, u32[]{:S(2)}) collective-permute-start(bf16[512,256]{1,0:T(8,128)(2,1)} %refs_5_.1), channel_id=1, source_target_pairs={{0,2},{1,3},{2,0},{3,1},{4,6},{5,7},{6,4},{7,5},{8,10},{9,11},{10,... | collective-permute-start | bytes 786440 | tf_op jit(solution)/shard_map/ppermute | solution.py:509
  8.0 16.8 %collective-permute-start.10 = (bf16[512,256]{1,0:T(8,128)(2,1)}, bf16[512,256]{1,0:T(8,128)(2,1)S(1)}, u32[]{:S(2)}, u32[]{:S(2)}) collective-permute-start(bf16[512,256]{1,0:T(8,128)(2,1)} %refs_5_.1), channel_id=1, source_target_pairs={{0,12},{1,13},{2,14},{3,15},{4,0},{5,1},{6,2},{7,3},{8,4},{9,5},{1... | collective-permute-start | bytes 786440 | tf_op jit(solution)/shard_map/ppermute | solution.py:509
  10.3 22.7 %collective-permute-start.11 = (bf16[512,256]{1,0:T(8,128)(2,1)}, bf16[512,256]{1,0:T(8,128)(2,1)S(1)}, u32[]{:S(2)}, u32[]{:S(2)}) collective-permute-start(bf16[512,256]{1,0:T(8,128)(2,1)} %refs_6_.1), channel_id=1, source_target_pairs={{0,12},{1,13},{2,14},{3,15},{4,0},{5,1},{6,2},{7,3},{8,4},{9,5},{1... | collective-permute-start | bytes 786440 | tf_op jit(solution)/shard_map/ppermute | solution.py:509
  14.5 18.5 %collective-permute-start.6 = (bf16[512,256]{1,0:T(8,128)(2,1)S(1)}, bf16[512,256]{1,0:T(8,128)(2,1)S(1)}, u32[]{:S(2)}, u32[]{:S(2)}) collective-permute-start(bf16[512,256]{1,0:T(8,128)(2,1)S(1)} %collective-permute-done.4.refs_7_), channel_id=1, source_target_pairs={{0,2},{1,3},{2,0},{3,1},{4,6},{5,7},{6,4},{7,5},{8,10},{9,11},{10,... | collective-permute-start | bytes 786440 | tf_op jit(solution)/shard_map/ppermute | solution.py:509
  19.8 13.7 %collective-permute-start.7 = (bf16[512,256]{1,0:T(8,128)(2,1)S(1)}, bf16[512,256]{1,0:T(8,128)(2,1)S(1)}, u32[]{:S(2)}, u32[]{:S(2)}) collective-permute-start(bf16[512,256]{1,0:T(8,128)(2,1)S(1)} %collective-permute-done.5.refs_8_), channel_id=1, source_target_pairs={{0,2},{1,3},{2,0},{3,1},{4,6},{5,7},{6,4},{7,5},{8,10},{9,11},{10,... | collective-permute-start | bytes 786440 | tf_op jit(solution)/shard_map/ppermute | solution.py:509
  20.8 18.0 %collective-permute-start.8 = (bf16[512,256]{1,0:T(8,128)(2,1)S(1)}, bf16[512,256]{1,0:T(8,128)(2,1)S(1)}, u32[]{:S(2)}, u32[]{:S(2)}) collective-permute-start(bf16[512,256]{1,0:T(8,128)(2,1)S(1)} %collective-permute-done.4.refs_7_), channel_id=1, source_target_pairs={{0,4},{1,5},{2,6},{3,7},{4,8},{5,9},{6,10},{7,11},{8,12},{9,13},{1... | collective-permute-start | bytes 786440 | tf_op jit(solution)/shard_map/ppermute | solution.py:509
  24.8 16.8 %collective-permute-start.9 = (bf16[512,256]{1,0:T(8,128)(2,1)S(1)}, bf16[512,256]{1,0:T(8,128)(2,1)S(1)}, u32[]{:S(2)}, u32[]{:S(2)}) collective-permute-start(bf16[512,256]{1,0:T(8,128)(2,1)S(1)} %collective-permute-done.5.refs_8_), channel_id=1, source_target_pairs={{0,4},{1,5},{2,6},{3,7},{4,8},{5,9},{6,10},{7,11},{8,12},{9,13},{1... | collective-permute-start | bytes 786440 | tf_op jit(solution)/shard_map/ppermute | solution.py:509
  33.0 64.3 %collective-permute-start.18 = (bf16[1,1024,768]{2,1,0:T(8,128)(2,1)}, bf16[1,1024,768]{2,1,0:T(8,128)(2,1)}, u32[]{:S(2)}, u32[]{:S(2)}) collective-permute-start(bf16[1,1024,768]{2,1,0:T(8,128)(2,1)} %refs_2_.1), channel_id=1, source_target_pairs={{0,1},{1,0},{2,3},{3,2},{4,5},{5,4},{6,7},{7,6},{8,9},{9,8},{10,11... | collective-permute-start | bytes 4718600 | tf_op jit(solution)/shard_map/ppermute | solution.py:509
  33.0 65.8 %collective-permute-start.19 = (bf16[1,1024,768]{2,1,0:T(8,128)(2,1)}, bf16[1,1024,768]{2,1,0:T(8,128)(2,1)}, u32[]{:S(2)}, u32[]{:S(2)}) collective-permute-start(bf16[1,1024,768]{2,1,0:T(8,128)(2,1)} %refs_3_.3), channel_id=1, source_target_pairs={{0,1},{1,0},{2,3},{3,2},{4,5},{5,4},{6,7},{7,6},{8,9},{9,8},{10,11... | collective-permute-start | bytes 4718600 | tf_op jit(solution)/shard_map/ppermute | solution.py:509
  33.5 65.8 %collective-permute-start.20 = (bf16[1,768,1024]{2,1,0:T(8,128)(2,1)}, bf16[1,768,1024]{2,1,0:T(8,128)(2,1)}, u32[]{:S(2)}, u32[]{:S(2)}) collective-permute-start(bf16[1,768,1024]{2,1,0:T(8,128)(2,1)} %refs_4_.3), channel_id=1, source_target_pairs={{0,1},{1,0},{2,3},{3,2},{4,5},{5,4},{6,7},{7,6},{8,9},{9,8},{10,11... | collective-permute-start | bytes 4718600 | tf_op jit(solution)/shard_map/ppermute | solution.py:509
  38.8 11.2 %collective-permute-start.12 = (bf16[512,256]{1,0:T(8,128)(2,1)S(1)}, bf16[512,256]{1,0:T(8,128)(2,1)S(1)}, u32[]{:S(2)}, u32[]{:S(2)}) collective-permute-start(bf16[512,256]{1,0:T(8,128)(2,1)S(1)} %collective-permute-done.8.refs_7_), channel_id=1, source_target_pairs={{0,2},{1,3},{2,0},{3,1},{4,6},{5,7},{6,4},{7,5},{8,10},{9,11},{10,... | collective-permute-start | bytes 786440 | tf_op jit(solution)/shard_map/ppermute | solution.py:509
  41.6 10.0 %collective-permute-start.13 = (bf16[512,256]{1,0:T(8,128)(2,1)S(1)}, bf16[512,256]{1,0:T(8,128)(2,1)S(1)}, u32[]{:S(2)}, u32[]{:S(2)}) collective-permute-start(bf16[512,256]{1,0:T(8,128)(2,1)S(1)} %collective-permute-done.9.refs_8_), channel_id=1, source_target_pairs={{0,2},{1,3},{2,0},{3,1},{4,6},{5,7},{6,4},{7,5},{8,10},{9,11},{10,... | collective-permute-start | bytes 786440 | tf_op jit(solution)/shard_map/ppermute | solution.py:509
  42.1 0.9 copy-start
  43.1 0.9 copy-start.7
  44.1 0.9 copy-start.8
  45.0 0.8 copy-start.9
  45.8 0.8 copy-start.10
  50.0 22.9 %collective-permute-start.14 = (bf16[512,256]{1,0:T(8,128)(2,1)S(1)}, bf16[512,256]{1,0:T(8,128)(2,1)S(1)}, u32[]{:S(2)}, u32[]{:S(2)}) collective-permute-start(bf16[512,256]{1,0:T(8,128)(2,1)S(1)} %collective-permute-done.10.refs_7_), channel_id=1, source_target_pairs={{0,2},{1,3},{2,0},{3,1},{4,6},{5,7},{6,4},{7,5},{8,10},{9,11},{10,... | collective-permute-start | bytes 786440 | tf_op jit(solution)/shard_map/ppermute | solution.py:509
  51.6 21.4 %collective-permute-start.15 = (bf16[512,256]{1,0:T(8,128)(2,1)S(1)}, bf16[512,256]{1,0:T(8,128)(2,1)S(1)}, u32[]{:S(2)}, u32[]{:S(2)}) collective-permute-start(bf16[512,256]{1,0:T(8,128)(2,1)S(1)} %collective-permute-done.3.refs_8_), channel_id=1, source_target_pairs={{0,12},{1,13},{2,14},{3,15},{4,0},{5,1},{6,2},{7,3},{8,4},{9,5},{1... | collective-permute-start | bytes 786440 | tf_op jit(solution)/shard_map/ppermute | solution.py:509
  70.0 7.7 %copy-start.1 = (bf16[2048,1024]{1,0:T(8,128)(2,1)S(1)}, bf16[2048,1024]{1,0:T(8,128)(2,1)}, u32[]{:S(2)}) copy-start(bf16[2048,1024]{1,0:T(8,128)(2,1)} %weight_ref.1) | copy-start | bytes 12582916
  72.9 4.8 %copy-start.5 = (bf16[64,1024]{1,0:T(8,128)(2,1)S(1)}, bf16[64,1024]{1,0:T(8,128)(2,1)}, u32[]{:S(2)}) copy-start(bf16[64,1024]{1,0:T(8,128)(2,1)} %residual_ref.1) | copy-start | bytes 393220
  72.9 4.8 %copy-start.6 = (f32[1024]{0:T(1024)S(1)}, f32[1024]{0:T(1024)}, u32[]{:S(2)}) copy-start(f32[1024]{0:T(1024)} %param.22) | copy-start | bytes 12292
  76.0 1.7 %collective-permute-start.17 = (bf16[128,1024]{1,0:T(8,128)(2,1)S(1)}, bf16[128,1024]{1,0:T(8,128)(2,1)S(1)}, u32[]{:S(2)}, u32[]{:S(2)}) collective-permute-start(bf16[128,1024]{1,0:T(8,128)(2,1)S(1)} %get-tuple-element.84), channel_id=1, source_target_pairs={{0,1},{1,0},{2,3},{3,2},{4,5},{5,4},{6,7},{7,6},{8,9},{9,8},{10,11... | collective-permute-start | bytes 786440 | tf_op jit(solution)/shard_map/ppermute | solution.py:509
  76.1 1.6 %collective-permute-start.16 = (f32[8,1024]{1,0:T(8,128)S(1)}, f32[8,1024]{1,0:T(8,128)S(1)}, u32[]{:S(2)}, u32[]{:S(2)}) collective-permute-start(f32[8,1024]{1,0:T(8,128)S(1)} %get-tuple-element.83), channel_id=1, source_target_pairs={{0,1},{1,0},{2,3},{3,2},{4,5},{5,4},{6,7},{7,6},{8,9},{9,8},{10,11... | collective-permute-start | bytes 98312 | tf_op jit(solution)/shard_map/ppermute | solution.py:509
  77.7 21.6 %copy-start.2 = (bf16[1,1024,768]{2,1,0:T(8,128)(2,1)S(1)}, bf16[1,1024,768]{2,1,0:T(8,128)(2,1)}, u32[]{:S(2)}) copy-start(bf16[1,1024,768]{2,1,0:T(8,128)(2,1)} %refs_2_.1) | copy-start | bytes 4718596
  77.7 21.6 %copy-start.3 = (bf16[1,1024,768]{2,1,0:T(8,128)(2,1)S(1)}, bf16[1,1024,768]{2,1,0:T(8,128)(2,1)}, u32[]{:S(2)}) copy-start(bf16[1,1024,768]{2,1,0:T(8,128)(2,1)} %refs_3_.3) | copy-start | bytes 4718596
  79.4 11.2 %collective-permute-start.21 = (bf16[64,1152]{1,0:T(8,128)(2,1)}, bf16[64,1152]{1,0:T(8,128)(2,1)}, u32[]{:S(2)}, u32[]{:S(2)}) collective-permute-start(bf16[64,1152]{1,0:T(8,128)(2,1)} %get-tuple-element.86.refs_1_), channel_id=1, source_target_pairs={{0,8},{1,9},{2,10},{3,11},{4,12},{5,13},{6,14},{7,15},{8,0},{9,1},... | collective-permute-start | bytes 442376 | tf_op jit(solution)/shard_map/ppermute | solution.py:509
  79.4 11.6 %collective-permute-start.27 = (bf16[64,1152]{1,0:T(8,128)(2,1)}, bf16[64,1152]{1,0:T(8,128)(2,1)}, u32[]{:S(2)}, u32[]{:S(2)}) collective-permute-start(bf16[64,1152]{1,0:T(8,128)(2,1)} %get-tuple-element.86.refs_1_), channel_id=1, source_target_pairs={{0,4},{1,5},{2,6},{3,7},{4,8},{5,9},{6,10},{7,11},{8,12},{9,13},{1... | collective-permute-start | bytes 442376 | tf_op jit(solution)/shard_map/ppermute | solution.py:509
  90.6 6.0 %collective-permute-start.31 = (bf16[64,1152]{1,0:T(8,128)(2,1)}, bf16[64,1152]{1,0:T(8,128)(2,1)S(1)}, u32[]{:S(2)}, u32[]{:S(2)}) collective-permute-start(bf16[64,1152]{1,0:T(8,128)(2,1)} %get-tuple-element.86.refs_1_), channel_id=1, source_target_pairs={{0,12},{1,13},{2,14},{3,15},{4,0},{5,1},{6,2},{7,3},{8,4},{9,5},{1... | collective-permute-start | bytes 442376 | tf_op jit(solution)/shard_map/ppermute | solution.py:509
  91.0 20.2 %collective-permute-start.23 = (bf16[64,1152]{1,0:T(8,128)(2,1)}, bf16[64,1152]{1,0:T(8,128)(2,1)S(1)}, u32[]{:S(2)}, u32[]{:S(2)}) collective-permute-start(bf16[64,1152]{1,0:T(8,128)(2,1)} %get-tuple-element.86.refs_1_), channel_id=1, source_target_pairs={{0,2},{1,3},{2,0},{3,1},{4,6},{5,7},{6,4},{7,5},{8,10},{9,11},{10,... | collective-permute-start | bytes 442376 | tf_op jit(solution)/shard_map/ppermute | solution.py:509
  96.6 14.6 %collective-permute-start.22 = (bf16[64,1152]{1,0:T(8,128)(2,1)}, bf16[64,1152]{1,0:T(8,128)(2,1)S(1)}, u32[]{:S(2)}, u32[]{:S(2)}) collective-permute-start(bf16[64,1152]{1,0:T(8,128)(2,1)} %collective-permute-done.21.refs_1_), channel_id=1, source_target_pairs={{0,2},{1,3},{2,0},{3,1},{4,6},{5,7},{6,4},{7,5},{8,10},{9,11},{10,... | collective-permute-start | bytes 442376 | tf_op jit(solution)/shard_map/ppermute | solution.py:509
  97.3 19.0 %collective-permute-start.28 = (bf16[64,1152]{1,0:T(8,128)(2,1)}, bf16[64,1152]{1,0:T(8,128)(2,1)S(1)}, u32[]{:S(2)}, u32[]{:S(2)}) collective-permute-start(bf16[64,1152]{1,0:T(8,128)(2,1)} %collective-permute-done.27.refs_1_), channel_id=1, source_target_pairs={{0,2},{1,3},{2,0},{3,1},{4,6},{5,7},{6,4},{7,5},{8,10},{9,11},{10,... | collective-permute-start | bytes 442376 | tf_op jit(solution)/shard_map/ppermute | solution.py:509
  98.7 21.6 %collective-permute-start.32 = (bf16[64,1152]{1,0:T(8,128)(2,1)S(1)}, bf16[64,1152]{1,0:T(8,128)(2,1)S(1)}, u32[]{:S(2)}, u32[]{:S(2)}) collective-permute-start(bf16[64,1152]{1,0:T(8,128)(2,1)S(1)} %collective-permute-done.31.refs_1_), channel_id=1, source_target_pairs={{0,2},{1,3},{2,0},{3,1},{4,6},{5,7},{6,4},{7,5},{8,10},{9,11},{10,... | collective-permute-start | bytes 442376 | tf_op jit(solution)/shard_map/ppermute | solution.py:509
  99.3 1.4 %copy-start.4 = (bf16[1,768,1024]{2,1,0:T(8,128)(2,1)S(1)}, bf16[1,768,1024]{2,1,0:T(8,128)(2,1)}, u32[]{:S(2)}) copy-start(bf16[1,768,1024]{2,1,0:T(8,128)(2,1)} %refs_4_.3) | copy-start | bytes 4718596
  114.2 8.4 %collective-permute-start.25 = (bf16[64,1024]{1,0:T(8,128)(2,1)S(1)}, bf16[64,1024]{1,0:T(8,128)(2,1)S(1)}, u32[]{:S(2)}, u32[]{:S(2)}) collective-permute-start(bf16[64,1024]{1,0:T(8,128)(2,1)S(1)} %get-tuple-element.96), channel_id=1, source_target_pairs={{0,2},{1,3},{2,0},{3,1},{4,6},{5,7},{6,4},{7,5},{8,10},{9,11},{10,... | collective-permute-start | bytes 393224 | tf_op jit(solution)/shard_map/ppermute | solution.py:509
  115.7 12.5 %collective-permute-start.24 = (bf16[64,1024]{1,0:T(8,128)(2,1)S(1)}, bf16[64,1024]{1,0:T(8,128)(2,1)S(1)}, u32[]{:S(2)}, u32[]{:S(2)}) collective-permute-start(bf16[64,1024]{1,0:T(8,128)(2,1)S(1)} %get-tuple-element.94), channel_id=1, source_target_pairs={{0,2},{1,3},{2,0},{3,1},{4,6},{5,7},{6,4},{7,5},{8,10},{9,11},{10,... | collective-permute-start | bytes 393224 | tf_op jit(solution)/shard_map/ppermute | solution.py:509
  118.8 8.2 %collective-permute-start.29 = (bf16[64,1024]{1,0:T(8,128)(2,1)S(1)}, bf16[64,1024]{1,0:T(8,128)(2,1)S(1)}, u32[]{:S(2)}, u32[]{:S(2)}) collective-permute-start(bf16[64,1024]{1,0:T(8,128)(2,1)S(1)} %get-tuple-element.98), channel_id=1, source_target_pairs={{0,2},{1,3},{2,0},{3,1},{4,6},{5,7},{6,4},{7,5},{8,10},{9,11},{10,... | collective-permute-start | bytes 393224 | tf_op jit(solution)/shard_map/ppermute | solution.py:509
  122.4 8.2 %collective-permute-start.33 = (bf16[64,1024]{1,0:T(8,128)(2,1)S(1)}, bf16[64,1024]{1,0:T(8,128)(2,1)S(1)}, u32[]{:S(2)}, u32[]{:S(2)}) collective-permute-start(bf16[64,1024]{1,0:T(8,128)(2,1)S(1)} %get-tuple-element.99), channel_id=1, source_target_pairs={{0,4},{1,5},{2,6},{3,7},{4,8},{5,9},{6,10},{7,11},{8,12},{9,13},{1... | collective-permute-start | bytes 393224 | tf_op jit(solution)/shard_map/ppermute | solution.py:509
  122.5 10.5 %collective-permute-start.34 = (bf16[64,1024]{1,0:T(8,128)(2,1)S(1)}, bf16[64,1024]{1,0:T(8,128)(2,1)S(1)}, u32[]{:S(2)}, u32[]{:S(2)}) collective-permute-start(bf16[64,1024]{1,0:T(8,128)(2,1)S(1)} %get-tuple-element.100), channel_id=1, source_target_pairs={{0,6},{1,7},{2,4},{3,5},{4,10},{5,11},{6,8},{7,9},{8,14},{9,15},{1... | collective-permute-start | bytes 393224 | tf_op jit(solution)/shard_map/ppermute | solution.py:509
  122.6 13.1 %collective-permute-start.26 = (bf16[64,1024]{1,0:T(8,128)(2,1)S(1)}, bf16[64,1024]{1,0:T(8,128)(2,1)S(1)}, u32[]{:S(2)}, u32[]{:S(2)}) collective-permute-start(bf16[64,1024]{1,0:T(8,128)(2,1)S(1)} %add_convert_fusion.2), channel_id=1, source_target_pairs={{0,8},{1,9},{2,10},{3,11},{4,12},{5,13},{6,14},{7,15},{8,0},{9,1},... | collective-permute-start | bytes 393224 | tf_op jit(solution)/shard_map/ppermute | solution.py:509
  127.0 8.7 %collective-permute-start.30 = (bf16[64,1024]{1,0:T(8,128)(2,1)S(1)}, bf16[64,1024]{1,0:T(8,128)(2,1)S(1)}, u32[]{:S(2)}, u32[]{:S(2)}) collective-permute-start(bf16[64,1024]{1,0:T(8,128)(2,1)S(1)} %add_convert_fusion.1), channel_id=1, source_target_pairs={{0,12},{1,13},{2,14},{3,15},{4,0},{5,1},{6,2},{7,3},{8,4},{9,5},{1... | collective-permute-start | bytes 393224 | tf_op jit(solution)/shard_map/ppermute | solution.py:509

commit v5 on v4

--- a/solution.py
+++ b/solution.py
@@ -208,8 +208,8 @@
     wide = range(1, across)
     later = [dz for dz in visiting_order(deep) if 1 < dz < deep - 1]
     stages = [[(0, 0)]] + [[(0, dx)] for dx in wide] + [[(1, 0)]] + [[(1, dx)] for dx in wide]
-    stages += [[(dz, 0)] for dz in later] + [[(deep - 1, 0)]]
-    stages += [[(dz, dx)] for dz in later + [deep - 1] for dx in wide]
+    stages += [[(dz, 0) for dz in later + [deep - 1]]]
+    stages += [[(dz, dx) for dz in later + [deep - 1] for dx in wide]]
     return [stage for stage in stages if stage]
 
 
@@ -253,7 +253,7 @@
     stats_refs = results[0:2]
     out_refs = results[2:4]
     score_refs = results[4:6]
-    held_ref, arrived = results[6:]
+    spare_ref, held_ref, arrived = results[6:]
     copies = []
     held = []
     for number, source in enumerate(sources):
@@ -306,13 +306,16 @@
             high = part if high is None else jnp.maximum(high, part)
         return high * factor
 
+    final = {task[:2]: index for index, task in enumerate(tasks)}
     seen = set()
     high = score(0)
     for index, (owner, head, group, number) in enumerate(tasks):
         following = score(index + 1) if index + 1 < len(tasks) else None
         at = slice(head * tokens, head * tokens + TILE)
+        out_ref = out_refs[owner]
+        narrow = out_ref.dtype != jnp.float32
         if (owner, head) in seen:
-            source = (stats_refs[owner], out_refs[owner])
+            source = (stats_refs[owner], spare_ref if narrow else out_ref)
         elif first:
             source = None
         else:
@@ -345,7 +348,9 @@
             total = source[0][1:2, at] * fade + total
         stats_refs[owner][0:1, at] = high
         stats_refs[owner][1:2, at] = total
-        out_refs[owner][:, at] = out.astype(out_refs[owner].dtype)
+        if narrow and index < final[owner, head]:
+            out_ref = spare_ref
+        out_ref[:, at] = out.astype(out_ref.dtype)
         high = following
 
 
@@ -368,6 +373,7 @@
         + [here] * count,
         scratch_shapes=[pltpu.VMEM((longest, TILE), jnp.float32)] * 2
         + [
+            pltpu.VMEM((HEAD_SIZE, span if last else LANES), jnp.float32),
             pltpu.VMEM((count, longest, blocks[0].shape[1]), jnp.bfloat16),
             pltpu.SemaphoreType.DMA((count * PARTS,)),
         ],

time: 138 us -> 141 us (1.022)
  waiting for transfers between devices: 38.5 us -> 42.2 us
    ppermute x35, waiting for transfers between devices: 38.5 us -> 42.2 us  [moved(): lax.ppermute(array, 'blk', shift_pairs(deep, across, step_deep, step_acro...]
    pallas_call x8 -> x6, Pallas kernels: 24.1 us -> 23.5 us  [attend(): pl.pallas_call(lambda *refs: attention_kernel(columns, state is None, *re...]
  transfers between devices with their start and end apart: 35 -> 35, of which waited for: 11 -> 13; matrix products, arithmetic and copies ran while one was open for 3% -> 3% of each run, Pallas kernels for 32% -> 31%
where the time goes in v5:
time: 141 us; the launch traced here: 140 us
  starting transfers between devices  43.9 us (31%)
  Pallas kernels  43.2 us (31%)
  waiting for transfers between devices  42.2 us (30%)
  local copies, waits for them, and re-layouts  6.25 us (4%)
  other arithmetic  3.89 us (3%)
    ppermute x35, starting transfers between devices, moved(): lax.ppermute(array, 'blk', shift_pairs(deep, across, step_deep, step_acro...  43.9 us
    ppermute x35, waiting for transfers between devices, moved(): lax.ppermute(array, 'blk', shift_pairs(deep, across, step_deep, step_acro...  42.2 us
    pallas_call x6, Pallas kernels, attend(): pl.pallas_call(lambda *refs: attention_kernel(columns, state is None, *re...  23.5 us
    pallas_call x4, Pallas kernels, run_experts(): pl.pallas_call(lambda *refs: expert_kernel(parties, len(rows), load, *ref...  18 us
    unnamed x23, local copies, waits for them, and re-layouts  5.8 us
  transfers between devices with their start and end apart: 35, of which 13 were waited for; matrix products, arithmetic and copies ran while one was open for 3% of the time, Pallas kernels for 31%

profile of v5, /device:TPU:0, one launch (start us, length us, event | category | flops | bytes accessed | tf_op | source)
XLA Modules:
  0.0 139.7 jit_solution(12406701155582980929)
XLA Ops:
  0.0 0.5 collective-permute-start
  0.5 2.5 %collective-permute-start.3 = (bf16[512,256]{1,0:T(8,128)(2,1)}, bf16[512,256]{1,0:T(8,128)(2,1)S(1)}, u32[]{:S(2)}, u32[]{:S(2)}) collective-permute-start(bf16[512,256]{1,0:T(8,128)(2,1)} %refs_6_.1), channel_id=1, source_target_pairs={{0,2},{1,3},{2,0},{3,1},{4,6},{5,7},{6,4},{7,5},{8,10},{9,11},{10,... | collective-permute-start | bytes 786440 | tf_op jit(solution)/shard_map/ppermute | solution.py:515
  3.0 1.6 %collective-permute-start.4 = (bf16[512,256]{1,0:T(8,128)(2,1)}, bf16[512,256]{1,0:T(8,128)(2,1)S(1)}, u32[]{:S(2)}, u32[]{:S(2)}) collective-permute-start(bf16[512,256]{1,0:T(8,128)(2,1)} %refs_5_.1), channel_id=1, source_target_pairs={{0,4},{1,5},{2,6},{3,7},{4,8},{5,9},{6,10},{7,11},{8,12},{9,13},{1... | collective-permute-start | bytes 786440 | tf_op jit(solution)/shard_map/ppermute | solution.py:515
  4.5 1.6 %collective-permute-start.5 = (bf16[512,256]{1,0:T(8,128)(2,1)}, bf16[512,256]{1,0:T(8,128)(2,1)S(1)}, u32[]{:S(2)}, u32[]{:S(2)}) collective-permute-start(bf16[512,256]{1,0:T(8,128)(2,1)} %refs_6_.1), channel_id=1, source_target_pairs={{0,4},{1,5},{2,6},{3,7},{4,8},{5,9},{6,10},{7,11},{8,12},{9,13},{1... | collective-permute-start | bytes 786440 | tf_op jit(solution)/shard_map/ppermute | solution.py:515
  6.1 1.4 collective-permute-done.1
  7.5 0.5 collective-permute-start.2
  8.0 2.2 %collective-permute-start.10 = (bf16[512,256]{1,0:T(8,128)(2,1)}, bf16[512,256]{1,0:T(8,128)(2,1)S(1)}, u32[]{:S(2)}, u32[]{:S(2)}) collective-permute-start(bf16[512,256]{1,0:T(8,128)(2,1)} %refs_5_.1), channel_id=1, source_target_pairs={{0,12},{1,13},{2,14},{3,15},{4,0},{5,1},{6,2},{7,3},{8,4},{9,5},{1... | collective-permute-start | bytes 786440 | tf_op jit(solution)/shard_map/ppermute | solution.py:515
  10.3 4.2 %collective-permute-start.11 = (bf16[512,256]{1,0:T(8,128)(2,1)}, bf16[512,256]{1,0:T(8,128)(2,1)S(1)}, u32[]{:S(2)}, u32[]{:S(2)}) collective-permute-start(bf16[512,256]{1,0:T(8,128)(2,1)} %refs_6_.1), channel_id=1, source_target_pairs={{0,12},{1,13},{2,14},{3,15},{4,0},{5,1},{6,2},{7,3},{8,4},{9,5},{1... | collective-permute-start | bytes 786440 | tf_op jit(solution)/shard_map/ppermute | solution.py:515
  14.5 1.5 %collective-permute-start.6 = (bf16[512,256]{1,0:T(8,128)(2,1)S(1)}, bf16[512,256]{1,0:T(8,128)(2,1)S(1)}, u32[]{:S(2)}, u32[]{:S(2)}) collective-permute-start(bf16[512,256]{1,0:T(8,128)(2,1)S(1)} %collective-permute-done.4.refs_7_), channel_id=1, source_target_pairs={{0,2},{1,3},{2,0},{3,1},{4,6},{5,7},{6,4},{7,5},{8,10},{9,11},{10,... | collective-permute-start | bytes 786440 | tf_op jit(solution)/shard_map/ppermute | solution.py:515
  16.0 3.9 %collective-permute-done.5.refs_8_ = bf16[512,256]{1,0:T(8,128)(2,1)S(1)} collective-permute-done((bf16[512,256]{1,0:T(8,128)(2,1)}, bf16[512,256]{1,0:T(8,128)(2,1)S(1)}, u32[]{:S(2)}, u32[]{:S(2)}) %collective-permute-start.5) | collective-permute-done | bytes 262176 | tf_op jit(solution)/shard_map/ppermute | solution.py:515
  19.8 0.3 collective-permute-start.7
  20.1 0.7 reduce_sum.18
  20.9 3.9 %collective-permute-done.10.refs_9_ = bf16[512,256]{1,0:T(8,128)(2,1)S(1)} collective-permute-done((bf16[512,256]{1,0:T(8,128)(2,1)}, bf16[512,256]{1,0:T(8,128)(2,1)S(1)}, u32[]{:S(2)}, u32[]{:S(2)}) %collective-permute-start.10) | collective-permute-done | bytes 262176 | tf_op jit(solution)/shard_map/ppermute | solution.py:515
  24.8 7.5 %collective-permute-start.9 = (bf16[512,256]{1,0:T(8,128)(2,1)S(1)}, bf16[512,256]{1,0:T(8,128)(2,1)S(1)}, u32[]{:S(2)}, u32[]{:S(2)}) collective-permute-start(bf16[512,256]{1,0:T(8,128)(2,1)S(1)} %collective-permute-done.5.refs_8_), channel_id=1, source_target_pairs={{0,4},{1,5},{2,6},{3,7},{4,8},{5,9},{6,10},{7,11},{8,12},{9,13},{1... | collective-permute-start | bytes 786440 | tf_op jit(solution)/shard_map/ppermute | solution.py:515
  32.3 0.7 broadcast_divide_fusion
  33.0 0.5 collective-permute-start.19
  33.6 0.7 select_reduce_fusion
  34.4 0.1 copy.40
  34.5 0.1 stack.44
  34.5 4.3 %collective-permute-done.8.refs_7_ = bf16[512,256]{1,0:T(8,128)(2,1)S(1)} collective-permute-done((bf16[512,256]{1,0:T(8,128)(2,1)S(1)}, bf16[512,256]{1,0:T(8,128)(2,1)S(1)}, u32[]{:S(2)}, u32[]{:S(2)}) %collective-permute-start.8) | collective-permute-done | bytes 262176 | tf_op jit(solution)/shard_map/ppermute | solution.py:515
  38.8 0.5 collective-permute-start.14
  39.3 3.1 %collective-permute-done.9.refs_8_ = bf16[512,256]{1,0:T(8,128)(2,1)S(1)} collective-permute-done((bf16[512,256]{1,0:T(8,128)(2,1)S(1)}, bf16[512,256]{1,0:T(8,128)(2,1)S(1)}, u32[]{:S(2)}, u32[]{:S(2)}) %collective-permute-start.9) | collective-permute-done | bytes 262176 | tf_op jit(solution)/shard_map/ppermute | solution.py:515
  42.4 0.9 collective-permute-start.15
  43.3 0.8 compare_reduce_fusion
  44.2 0.1 tile.21
  44.3 2.7 %collective-permute-done.14.refs_9_ = bf16[512,256]{1,0:T(8,128)(2,1)S(1)} collective-permute-done((bf16[512,256]{1,0:T(8,128)(2,1)S(1)}, bf16[512,256]{1,0:T(8,128)(2,1)S(1)}, u32[]{:S(2)}, u32[]{:S(2)}) %collective-permute-start.14) | collective-permute-done | bytes 262176 | tf_op jit(solution)/shard_map/ppermute | solution.py:515
  47.0 1.8 %collective-permute-done.15.refs_10_ = bf16[512,256]{1,0:T(8,128)(2,1)S(1)} collective-permute-done((bf16[512,256]{1,0:T(8,128)(2,1)S(1)}, bf16[512,256]{1,0:T(8,128)(2,1)S(1)}, u32[]{:S(2)}, u32[]{:S(2)}) %collective-permute-start.15) | collective-permute-done | bytes 262176 | tf_op jit(solution)/shard_map/ppermute | solution.py:515
  48.8 0.3 collective-permute-start.13
  49.1 0.9 copy-done.1
  50.0 0.9 copy-done.7
  51.0 0.9 copy-done.8
  51.9 0.8 copy-done.9
  52.7 0.8 copy-done.10
  53.4 3.5 %attend_blocks.6 = (f32[8,1024]{1,0:T(8,128)S(1)}, f32[8,1024]{1,0:T(8,128)S(1)}, f32[128,1024]{1,0:T(8,128)S(1)}, f32[128,1024]{1,0:T(8,128)S(1)}) custom-call(bf16[64,2048]{1,0:T(8,128)(2,1)S(1)} %copy-done.1, bf16[64,2048]{1,0:T(8,128)(2,1)S(1)} %collective-permute-done.refs_1_, f32[8,512]{1,0:T(8,128)S(1)} %constant_dynamic-update-slice_fusion.refs_2_, ...), custom_call_target="tpu_custom_call" | custom-call | flops 603979776 | bytes 2686976 | tf_op jit(solution)/shard_map/attend_blocks/pallas_call | solution.py:368
  56.9 2.9 %attend_blocks.7 = (f32[8,1024]{1,0:T(8,128)S(1)}, f32[8,1024]{1,0:T(8,128)S(1)}, f32[128,1024]{1,0:T(8,128)S(1)}, f32[128,1024]{1,0:T(8,128)S(1)}) custom-call(bf16[64,2048]{1,0:T(8,128)(2,1)S(1)} %copy-done.1, bf16[64,2048]{1,0:T(8,128)(2,1)S(1)} %collective-permute-done.refs_1_, ...), custom_call_target="tpu_custom_call", output_to_operand_aliasing={{0}: (3, {}), {1}: (4, {}), {2}: (5, {}), {3}: (6, {})} | custom-call | flops 536870912 | bytes 2621440 | tf_op jit(solution)/shard_map/attend_blocks/pallas_call | solution.py:368
  59.9 2.9 %attend_blocks.8 = (f32[8,1024]{1,0:T(8,128)S(1)}, f32[8,1024]{1,0:T(8,128)S(1)}, f32[128,1024]{1,0:T(8,128)S(1)}, f32[128,1024]{1,0:T(8,128)S(1)}) custom-call(bf16[64,2048]{1,0:T(8,128)(2,1)S(1)} %copy-done.1, bf16[64,2048]{1,0:T(8,128)(2,1)S(1)} %collective-permute-done.refs_1_, ...), custom_call_target="tpu_custom_call", output_to_operand_aliasing={{0}: (3, {}), {1}: (4, {}), {2}: (5, {}), {3}: (6, {})} | custom-call | flops 536870912 | bytes 2621440 | tf_op jit(solution)/shard_map/attend_blocks/pallas_call | solution.py:368
  62.8 2.9 %attend_blocks.9 = (f32[8,1024]{1,0:T(8,128)S(1)}, f32[8,1024]{1,0:T(8,128)S(1)}, f32[128,1024]{1,0:T(8,128)S(1)}, f32[128,1024]{1,0:T(8,128)S(1)}) custom-call(bf16[64,2048]{1,0:T(8,128)(2,1)S(1)} %copy-done.1, bf16[64,2048]{1,0:T(8,128)(2,1)S(1)} %collective-permute-done.refs_1_, ...), custom_call_target="tpu_custom_call", output_to_operand_aliasing={{0}: (3, {}), {1}: (4, {}), {2}: (5, {}), {3}: (6, {})} | custom-call | flops 536870912 | bytes 2621440 | tf_op jit(solution)/shard_map/attend_blocks/pallas_call | solution.py:368
  65.7 5.5 %attend_blocks.10 = (f32[8,1024]{1,0:T(8,128)S(1)}, f32[8,1024]{1,0:T(8,128)S(1)}, f32[128,1024]{1,0:T(8,128)S(1)}, f32[128,1024]{1,0:T(8,128)S(1)}) custom-call(bf16[64,2048]{1,0:T(8,128)(2,1)S(1)} %copy-done.1, bf16[64,2048]{1,0:T(8,128)(2,1)S(1)} %collective-permute-done.refs_1_, ...), custom_call_target="tpu_custom_call", output_to_operand_aliasing={{0}: (3, {}), {1}: (4, {}), {2}: (5, {}), {3}: (6, {})} | custom-call | flops 1073741824 | bytes 3145728 | tf_op jit(solution)/shard_map/attend_blocks/pallas_call | solution.py:368
  71.3 5.7 %attend_blocks.11 = (f32[8,1024]{1,0:T(8,128)S(1)}, f32[8,1024]{1,0:T(8,128)S(1)}, f32[128,1024]{1,0:T(8,128)S(1)}, bf16[128,1024]{1,0:T(8,128)(2,1)S(1)}) custom-call(bf16[64,2048]{1,0:T(8,128)(2,1)S(1)} %copy-done.1, bf16[64,2048]{1,0:T(8,128)(2,1)S(1)} %collective-permute-done.refs_1_, ...), custom_call_target="tpu_custom_call", output_to_operand_aliasing={{0}: (3, {}), {1}: (4, {}), {2}: (5, {})} | custom-call | flops 1073741824 | bytes 3145728 | tf_op jit(solution)/shard_map/attend_blocks/pallas_call | solution.py:368
  77.1 0.5 collective-permute-start.16
  77.7 1.0 collective-permute-done.16.far_stats
  78.7 1.7 %finish_attention.1 = (f32[64,1024]{1,0:T(8,128)S(1)}, bf16[64,1152]{1,0:T(8,128)(2,1)}) custom-call(f32[8,1024]{1,0:T(8,128)S(1)} %get-tuple-element.65.near_stats, f32[128,1024]{1,0:T(8,128)S(1)} %get-tuple-element.66.near_out, f32[8,1024]{1,0:T(8,128)S(1)} %collective-permute-done.16.far_stats, bf16[128,1024]{1,0:T(8,128)(2,1)S(1)} %collective-permute-done.17.far_out, ...), custom_call_target="tpu_custom_call" | custom-call | tf_op jit(solution)/shard_map/finish_attention/pallas_call | solution.py:592
  80.4 0.1 collective-permute-start.21
  80.6 3.4 %collective-permute-start.27 = (bf16[64,1152]{1,0:T(8,128)(2,1)}, bf16[64,1152]{1,0:T(8,128)(2,1)}, u32[]{:S(2)}, u32[]{:S(2)}) collective-permute-start(bf16[64,1152]{1,0:T(8,128)(2,1)} %get-tuple-element.70.refs_1_), channel_id=1, source_target_pairs={{0,4},{1,5},{2,6},{3,7},{4,8},{5,9},{6,10},{7,11},{8,12},{9,13},{1... | collective-permute-start | bytes 442376 | tf_op jit(solution)/shard_map/ppermute | solution.py:515
  83.9 9.9 %collective-permute-done.21.refs_1_ = bf16[64,1152]{1,0:T(8,128)(2,1)} collective-permute-done((bf16[64,1152]{1,0:T(8,128)(2,1)}, bf16[64,1152]{1,0:T(8,128)(2,1)}, u32[]{:S(2)}, u32[]{:S(2)}) %collective-permute-start.21) | collective-permute-done | bytes 147488 | tf_op jit(solution)/shard_map/ppermute | solution.py:515
  93.9 1.8 %collective-permute-start.23 = (bf16[64,1152]{1,0:T(8,128)(2,1)}, bf16[64,1152]{1,0:T(8,128)(2,1)S(1)}, u32[]{:S(2)}, u32[]{:S(2)}) collective-permute-start(bf16[64,1152]{1,0:T(8,128)(2,1)} %get-tuple-element.70.refs_1_), channel_id=1, source_target_pairs={{0,2},{1,3},{2,0},{3,1},{4,6},{5,7},{6,4},{7,5},{8,10},{9,11},{10,... | collective-permute-start | bytes 442376 | tf_op jit(solution)/shard_map/ppermute | solution.py:515
  95.6 3.9 %collective-permute-done.31.refs_1_ = bf16[64,1152]{1,0:T(8,128)(2,1)S(1)} collective-permute-done((bf16[64,1152]{1,0:T(8,128)(2,1)}, bf16[64,1152]{1,0:T(8,128)(2,1)S(1)}, u32[]{:S(2)}, u32[]{:S(2)}) %collective-permute-start.31) | collective-permute-done | bytes 147488 | tf_op jit(solution)/shard_map/ppermute | solution.py:515
  99.5 2.0 %collective-permute-start.22 = (bf16[64,1152]{1,0:T(8,128)(2,1)}, bf16[64,1152]{1,0:T(8,128)(2,1)S(1)}, u32[]{:S(2)}, u32[]{:S(2)}) collective-permute-start(bf16[64,1152]{1,0:T(8,128)(2,1)} %collective-permute-done.21.refs_1_), channel_id=1, source_target_pairs={{0,2},{1,3},{2,0},{3,1},{4,6},{5,7},{6,4},{7,5},{8,10},{9,11},{10,... | collective-permute-start | bytes 442376 | tf_op jit(solution)/shard_map/ppermute | solution.py:515
  101.6 2.0 %collective-permute-start.32 = (bf16[64,1152]{1,0:T(8,128)(2,1)S(1)}, bf16[64,1152]{1,0:T(8,128)(2,1)S(1)}, u32[]{:S(2)}, u32[]{:S(2)}) collective-permute-start(bf16[64,1152]{1,0:T(8,128)(2,1)S(1)} %collective-permute-done.31.refs_1_), channel_id=1, source_target_pairs={{0,2},{1,3},{2,0},{3,1},{4,6},{5,7},{6,4},{7,5},{8,10},{9,11},{10,... | collective-permute-start | bytes 442376 | tf_op jit(solution)/shard_map/ppermute | solution.py:515
  103.7 1.4 %copy-done.4 = bf16[1,768,1024]{2,1,0:T(8,128)(2,1)S(1)} copy-done((bf16[1,768,1024]{2,1,0:T(8,128)(2,1)S(1)}, bf16[1,768,1024]{2,1,0:T(8,128)(2,1)}, u32[]{:S(2)}) %copy-start.4) | copy-done | bytes 1572888
  105.1 10.5 %run_experts.4 = (f32[64,1024]{1,0:T(8,128)S(1)}, bf16[1,1024,768]{2,1,0:T(8,128)(2,1)S(1)}, bf16[1,1024,768]{2,1,0:T(8,128)(2,1)S(1)}, bf16[1,768,1024]{2,1,0:T...) custom-call(s32[2]{0:T(128)S(1)} %pad_add_fusion.refs_0_, ...), custom_call_target="tpu_custom_call" | custom-call | flops 603979776 | bytes 9437184 | tf_op jit(solution)/shard_map/run_experts/pallas_call | solution.py:473
  115.6 3.0 %run_experts.5 = (f32[64,1024]{1,0:T(8,128)S(1)}, bf16[64,1024]{1,0:T(8,128)(2,1)S(1)}, bf16[64,1024]{1,0:T(8,128)(2,1)S(1)}) custom-call(s32[2]{0:T(128)S(1)} %pad_add_fusion.refs_0_, bf16[64,1152]{1,0:T(8,128)(2,1)} %collective-permute-done.21.refs_1_, bf16[64,1152]{1,0:T(8,128)(2,1)S(1)} %collective-permute-done.22.refs_2_, ...), custom_call_target="tpu_custom_call" | custom-call | flops 1811939328 | bytes 9437184 | tf_op jit(solution)/shard_map/run_experts/pallas_call | solution.py:473
  118.6 0.1 collective-permute-start.25
  118.7 1.9 %collective-permute-start.24 = (bf16[64,1024]{1,0:T(8,128)(2,1)S(1)}, bf16[64,1024]{1,0:T(8,128)(2,1)S(1)}, u32[]{:S(2)}, u32[]{:S(2)}) collective-permute-start(bf16[64,1024]{1,0:T(8,128)(2,1)S(1)} %get-tuple-element.78), channel_id=1, source_target_pairs={{0,2},{1,3},{2,0},{3,1},{4,6},{5,7},{6,4},{7,5},{8,10},{9,11},{10,... | collective-permute-start | bytes 393224 | tf_op jit(solution)/shard_map/ppermute | solution.py:515
  120.7 2.5 %run_experts.6 = (f32[64,1024]{1,0:T(8,128)S(1)}, bf16[64,1024]{1,0:T(8,128)(2,1)S(1)}) custom-call(s32[2]{0:T(128)S(1)} %pad_add_fusion.refs_0_, bf16[64,1152]{1,0:T(8,128)(2,1)} %collective-permute-done.27.refs_1_, bf16[64,1152]{1,0:T(8,128)(2,1)S(1)} %collective-permute-done.28.refs_2_, bf16[1,1024,768]{2,1,0:T(8,128)(2,1)S(1)} %get-tuple-element.72.refs_4_.refs_3_, ...), custom_call_target="tpu_custom_call" | custom-call | flops 1207959552 | bytes 9437184 | tf_op jit(solution)/shard_map/run_experts/pallas_call | solution.py:473
  123.1 0.1 collective-permute-start.29
  123.3 2.1 %run_experts.7 = (bf16[64,1024]{1,0:T(8,128)(2,1)S(1)}, bf16[64,1024]{1,0:T(8,128)(2,1)S(1)}) custom-call(s32[2]{0:T(128)S(1)} %pad_add_fusion.refs_0_, bf16[64,1152]{1,0:T(8,128)(2,1)S(1)} %collective-permute-done.31.refs_1_, bf16[64,1152]{1,0:T(8,128)(2,1)S(1)} %collective-permute-done.32.refs_2_, ...), custom_call_target="tpu_custom_call" | custom-call | flops 1207959552 | bytes 9437184 | tf_op jit(solution)/shard_map/run_experts/pallas_call | solution.py:473
  125.5 1.5 %collective-permute-start.34 = (bf16[64,1024]{1,0:T(8,128)(2,1)S(1)}, bf16[64,1024]{1,0:T(8,128)(2,1)S(1)}, u32[]{:S(2)}, u32[]{:S(2)}) collective-permute-start(bf16[64,1024]{1,0:T(8,128)(2,1)S(1)} %get-tuple-element.84), channel_id=1, source_target_pairs={{0,6},{1,7},{2,4},{3,5},{4,10},{5,11},{6,8},{7,9},{8,14},{9,15},{1... | collective-permute-start | bytes 393224 | tf_op jit(solution)/shard_map/ppermute | solution.py:515
  127.0 4.3 %collective-permute-start.26 = (bf16[64,1024]{1,0:T(8,128)(2,1)S(1)}, bf16[64,1024]{1,0:T(8,128)(2,1)S(1)}, u32[]{:S(2)}, u32[]{:S(2)}) collective-permute-start(bf16[64,1024]{1,0:T(8,128)(2,1)S(1)} %add_convert_fusion.2), channel_id=1, source_target_pairs={{0,8},{1,9},{2,10},{3,11},{4,12},{5,13},{6,14},{7,15},{8,0},{9,1},... | collective-permute-start | bytes 393224 | tf_op jit(solution)/shard_map/ppermute | solution.py:515
  131.4 1.2 collective-permute-start.30
  132.6 1.1 collective-permute-done.33
  133.7 3.4 %collective-permute-done.34 = bf16[64,1024]{1,0:T(8,128)(2,1)S(1)} collective-permute-done((bf16[64,1024]{1,0:T(8,128)(2,1)S(1)}, bf16[64,1024]{1,0:T(8,128)(2,1)S(1)}, u32[]{:S(2)}, u32[]{:S(2)}) %collective-permute-start.34) | collective-permute-done | bytes 131104 | tf_op jit(solution)/shard_map/ppermute | solution.py:515
  137.2 1.8 %collective-permute-done.26 = bf16[64,1024]{1,0:T(8,128)(2,1)S(1)} collective-permute-done((bf16[64,1024]{1,0:T(8,128)(2,1)S(1)}, bf16[64,1024]{1,0:T(8,128)(2,1)S(1)}, u32[]{:S(2)}, u32[]{:S(2)}) %collective-permute-start.26) | collective-permute-done | bytes 131104 | tf_op jit(solution)/shard_map/ppermute | solution.py:515
  139.0 0.8 add_convert_fusion
  (61 shorter events, 0.8 us)
Async XLA Ops:
  0.0 8.0 %collective-permute-start = (bf16[64,2048]{1,0:T(8,128)(2,1)}, bf16[64,2048]{1,0:T(8,128)(2,1)S(1)}, u32[]{:S(2)}, u32[]{:S(2)}) collective-permute-start(bf16[64,2048]{1,0:T(8,128)(2,1)} %refs_0_.11), channel_id=1, source_target_pairs={{0,1},{1,0},{2,3},{3,2},{4,5},{5,4},{6,7},{7,6},{8,9},{9,8},{10,11... | collective-permute-start | bytes 786440 | tf_op jit(solution)/shard_map/ppermute | solution.py:515
  0.5 9.8 %collective-permute-start.3 = (bf16[512,256]{1,0:T(8,128)(2,1)}, bf16[512,256]{1,0:T(8,128)(2,1)S(1)}, u32[]{:S(2)}, u32[]{:S(2)}) collective-permute-start(bf16[512,256]{1,0:T(8,128)(2,1)} %refs_6_.1), channel_id=1, source_target_pairs={{0,2},{1,3},{2,0},{3,1},{4,6},{5,7},{6,4},{7,5},{8,10},{9,11},{10,... | collective-permute-start | bytes 786440 | tf_op jit(solution)/shard_map/ppermute | solution.py:515
  3.0 11.5 %collective-permute-start.4 = (bf16[512,256]{1,0:T(8,128)(2,1)}, bf16[512,256]{1,0:T(8,128)(2,1)S(1)}, u32[]{:S(2)}, u32[]{:S(2)}) collective-permute-start(bf16[512,256]{1,0:T(8,128)(2,1)} %refs_5_.1), channel_id=1, source_target_pairs={{0,4},{1,5},{2,6},{3,7},{4,8},{5,9},{6,10},{7,11},{8,12},{9,13},{1... | collective-permute-start | bytes 786440 | tf_op jit(solution)/shard_map/ppermute | solution.py:515
  4.5 15.3 %collective-permute-start.5 = (bf16[512,256]{1,0:T(8,128)(2,1)}, bf16[512,256]{1,0:T(8,128)(2,1)S(1)}, u32[]{:S(2)}, u32[]{:S(2)}) collective-permute-start(bf16[512,256]{1,0:T(8,128)(2,1)} %refs_6_.1), channel_id=1, source_target_pairs={{0,4},{1,5},{2,6},{3,7},{4,8},{5,9},{6,10},{7,11},{8,12},{9,13},{1... | collective-permute-start | bytes 786440 | tf_op jit(solution)/shard_map/ppermute | solution.py:515
  6.1 1.4 collective-permute-start.1
  7.5 13.3 %collective-permute-start.2 = (bf16[512,256]{1,0:T(8,128)(2,1)}, bf16[512,256]{1,0:T(8,128)(2,1)S(1)}, u32[]{:S(2)}, u32[]{:S(2)}) collective-permute-start(bf16[512,256]{1,0:T(8,128)(2,1)} %refs_5_.1), channel_id=1, source_target_pairs={{0,2},{1,3},{2,0},{3,1},{4,6},{5,7},{6,4},{7,5},{8,10},{9,11},{10,... | collective-permute-start | bytes 786440 | tf_op jit(solution)/shard_map/ppermute | solution.py:515
  8.0 16.8 %collective-permute-start.10 = (bf16[512,256]{1,0:T(8,128)(2,1)}, bf16[512,256]{1,0:T(8,128)(2,1)S(1)}, u32[]{:S(2)}, u32[]{:S(2)}) collective-permute-start(bf16[512,256]{1,0:T(8,128)(2,1)} %refs_5_.1), channel_id=1, source_target_pairs={{0,12},{1,13},{2,14},{3,15},{4,0},{5,1},{6,2},{7,3},{8,4},{9,5},{1... | collective-permute-start | bytes 786440 | tf_op jit(solution)/shard_map/ppermute | solution.py:515
  10.3 22.7 %collective-permute-start.11 = (bf16[512,256]{1,0:T(8,128)(2,1)}, bf16[512,256]{1,0:T(8,128)(2,1)S(1)}, u32[]{:S(2)}, u32[]{:S(2)}) collective-permute-start(bf16[512,256]{1,0:T(8,128)(2,1)} %refs_6_.1), channel_id=1, source_target_pairs={{0,12},{1,13},{2,14},{3,15},{4,0},{5,1},{6,2},{7,3},{8,4},{9,5},{1... | collective-permute-start | bytes 786440 | tf_op jit(solution)/shard_map/ppermute | solution.py:515
  14.5 18.5 %collective-permute-start.6 = (bf16[512,256]{1,0:T(8,128)(2,1)S(1)}, bf16[512,256]{1,0:T(8,128)(2,1)S(1)}, u32[]{:S(2)}, u32[]{:S(2)}) collective-permute-start(bf16[512,256]{1,0:T(8,128)(2,1)S(1)} %collective-permute-done.4.refs_7_), channel_id=1, source_target_pairs={{0,2},{1,3},{2,0},{3,1},{4,6},{5,7},{6,4},{7,5},{8,10},{9,11},{10,... | collective-permute-start | bytes 786440 | tf_op jit(solution)/shard_map/ppermute | solution.py:515
  19.8 13.7 %collective-permute-start.7 = (bf16[512,256]{1,0:T(8,128)(2,1)S(1)}, bf16[512,256]{1,0:T(8,128)(2,1)S(1)}, u32[]{:S(2)}, u32[]{:S(2)}) collective-permute-start(bf16[512,256]{1,0:T(8,128)(2,1)S(1)} %collective-permute-done.5.refs_8_), channel_id=1, source_target_pairs={{0,2},{1,3},{2,0},{3,1},{4,6},{5,7},{6,4},{7,5},{8,10},{9,11},{10,... | collective-permute-start | bytes 786440 | tf_op jit(solution)/shard_map/ppermute | solution.py:515
  20.8 18.0 %collective-permute-start.8 = (bf16[512,256]{1,0:T(8,128)(2,1)S(1)}, bf16[512,256]{1,0:T(8,128)(2,1)S(1)}, u32[]{:S(2)}, u32[]{:S(2)}) collective-permute-start(bf16[512,256]{1,0:T(8,128)(2,1)S(1)} %collective-permute-done.4.refs_7_), channel_id=1, source_target_pairs={{0,4},{1,5},{2,6},{3,7},{4,8},{5,9},{6,10},{7,11},{8,12},{9,13},{1... | collective-permute-start | bytes 786440 | tf_op jit(solution)/shard_map/ppermute | solution.py:515
  24.8 17.6 %collective-permute-start.9 = (bf16[512,256]{1,0:T(8,128)(2,1)S(1)}, bf16[512,256]{1,0:T(8,128)(2,1)S(1)}, u32[]{:S(2)}, u32[]{:S(2)}) collective-permute-start(bf16[512,256]{1,0:T(8,128)(2,1)S(1)} %collective-permute-done.5.refs_8_), channel_id=1, source_target_pairs={{0,4},{1,5},{2,6},{3,7},{4,8},{5,9},{6,10},{7,11},{8,12},{9,13},{1... | collective-permute-start | bytes 786440 | tf_op jit(solution)/shard_map/ppermute | solution.py:515
  33.0 68.7 %collective-permute-start.18 = (bf16[1,1024,768]{2,1,0:T(8,128)(2,1)}, bf16[1,1024,768]{2,1,0:T(8,128)(2,1)}, u32[]{:S(2)}, u32[]{:S(2)}) collective-permute-start(bf16[1,1024,768]{2,1,0:T(8,128)(2,1)} %refs_2_.1), channel_id=1, source_target_pairs={{0,1},{1,0},{2,3},{3,2},{4,5},{5,4},{6,7},{7,6},{8,9},{9,8},{10,11... | collective-permute-start | bytes 4718600 | tf_op jit(solution)/shard_map/ppermute | solution.py:515
  33.0 68.7 %collective-permute-start.19 = (bf16[1,1024,768]{2,1,0:T(8,128)(2,1)}, bf16[1,1024,768]{2,1,0:T(8,128)(2,1)}, u32[]{:S(2)}, u32[]{:S(2)}) collective-permute-start(bf16[1,1024,768]{2,1,0:T(8,128)(2,1)} %refs_3_.3), channel_id=1, source_target_pairs={{0,1},{1,0},{2,3},{3,2},{4,5},{5,4},{6,7},{7,6},{8,9},{9,8},{10,11... | collective-permute-start | bytes 4718600 | tf_op jit(solution)/shard_map/ppermute | solution.py:515
  33.5 70.2 %collective-permute-start.20 = (bf16[1,768,1024]{2,1,0:T(8,128)(2,1)}, bf16[1,768,1024]{2,1,0:T(8,128)(2,1)}, u32[]{:S(2)}, u32[]{:S(2)}) collective-permute-start(bf16[1,768,1024]{2,1,0:T(8,128)(2,1)} %refs_4_.3), channel_id=1, source_target_pairs={{0,1},{1,0},{2,3},{3,2},{4,5},{5,4},{6,7},{7,6},{8,9},{9,8},{10,11... | collective-permute-start | bytes 4718600 | tf_op jit(solution)/shard_map/ppermute | solution.py:515
  38.8 8.2 %collective-permute-start.14 = (bf16[512,256]{1,0:T(8,128)(2,1)S(1)}, bf16[512,256]{1,0:T(8,128)(2,1)S(1)}, u32[]{:S(2)}, u32[]{:S(2)}) collective-permute-start(bf16[512,256]{1,0:T(8,128)(2,1)S(1)} %collective-permute-done.10.refs_9_), channel_id=1, source_target_pairs={{0,2},{1,3},{2,0},{3,1},{4,6},{5,7},{6,4},{7,5},{8,10},{9,11},{10,... | collective-permute-start | bytes 786440 | tf_op jit(solution)/shard_map/ppermute | solution.py:515
  42.4 6.4 %collective-permute-start.15 = (bf16[512,256]{1,0:T(8,128)(2,1)S(1)}, bf16[512,256]{1,0:T(8,128)(2,1)S(1)}, u32[]{:S(2)}, u32[]{:S(2)}) collective-permute-start(bf16[512,256]{1,0:T(8,128)(2,1)S(1)} %collective-permute-done.3.refs_8_), channel_id=1, source_target_pairs={{0,12},{1,13},{2,14},{3,15},{4,0},{5,1},{6,2},{7,3},{8,4},{9,5},{1... | collective-permute-start | bytes 786440 | tf_op jit(solution)/shard_map/ppermute | solution.py:515
  47.0 24.3 %collective-permute-start.12 = (bf16[512,256]{1,0:T(8,128)(2,1)S(1)}, bf16[512,256]{1,0:T(8,128)(2,1)S(1)}, u32[]{:S(2)}, u32[]{:S(2)}) collective-permute-start(bf16[512,256]{1,0:T(8,128)(2,1)S(1)} %collective-permute-done.8.refs_7_), channel_id=1, source_target_pairs={{0,2},{1,3},{2,0},{3,1},{4,6},{5,7},{6,4},{7,5},{8,10},{9,11},{10,... | collective-permute-start | bytes 786440 | tf_op jit(solution)/shard_map/ppermute | solution.py:515
  48.8 22.5 %collective-permute-start.13 = (bf16[512,256]{1,0:T(8,128)(2,1)S(1)}, bf16[512,256]{1,0:T(8,128)(2,1)S(1)}, u32[]{:S(2)}, u32[]{:S(2)}) collective-permute-start(bf16[512,256]{1,0:T(8,128)(2,1)S(1)} %collective-permute-done.9.refs_8_), channel_id=1, source_target_pairs={{0,2},{1,3},{2,0},{3,1},{4,6},{5,7},{6,4},{7,5},{8,10},{9,11},{10,... | collective-permute-start | bytes 786440 | tf_op jit(solution)/shard_map/ppermute | solution.py:515
  49.1 0.9 copy-start.1
  50.0 0.9 copy-start.7
  51.0 0.9 copy-start.8
  51.9 0.8 copy-start.9
  52.7 0.8 copy-start.10
  65.7 12.9 %copy-start = (bf16[2048,1024]{1,0:T(8,128)(2,1)S(1)}, bf16[2048,1024]{1,0:T(8,128)(2,1)}, u32[]{:S(2)}) copy-start(bf16[2048,1024]{1,0:T(8,128)(2,1)} %weight_ref.1) | copy-start | bytes 12582916
  71.3 7.4 %copy-start.5 = (bf16[64,1024]{1,0:T(8,128)(2,1)S(1)}, bf16[64,1024]{1,0:T(8,128)(2,1)}, u32[]{:S(2)}) copy-start(bf16[64,1024]{1,0:T(8,128)(2,1)} %residual_ref.1) | copy-start | bytes 393220
  71.3 7.3 %copy-start.6 = (f32[1024]{0:T(1024)S(1)}, f32[1024]{0:T(1024)}, u32[]{:S(2)}) copy-start(f32[1024]{0:T(1024)} %param.22) | copy-start | bytes 12292
  77.0 1.7 %collective-permute-start.17 = (bf16[128,1024]{1,0:T(8,128)(2,1)S(1)}, bf16[128,1024]{1,0:T(8,128)(2,1)S(1)}, u32[]{:S(2)}, u32[]{:S(2)}) collective-permute-start(bf16[128,1024]{1,0:T(8,128)(2,1)S(1)} %get-tuple-element.68), channel_id=1, source_target_pairs={{0,1},{1,0},{2,3},{3,2},{4,5},{5,4},{6,7},{7,6},{8,9},{9,8},{10,11... | collective-permute-start | bytes 786440 | tf_op jit(solution)/shard_map/ppermute | solution.py:515
  77.1 1.6 %collective-permute-start.16 = (f32[8,1024]{1,0:T(8,128)S(1)}, f32[8,1024]{1,0:T(8,128)S(1)}, u32[]{:S(2)}, u32[]{:S(2)}) collective-permute-start(f32[8,1024]{1,0:T(8,128)S(1)} %get-tuple-element.67), channel_id=1, source_target_pairs={{0,1},{1,0},{2,3},{3,2},{4,5},{5,4},{6,7},{7,6},{8,9},{9,8},{10,11... | collective-permute-start | bytes 98312 | tf_op jit(solution)/shard_map/ppermute | solution.py:515
  78.7 25.0 %copy-start.2 = (bf16[1,1024,768]{2,1,0:T(8,128)(2,1)S(1)}, bf16[1,1024,768]{2,1,0:T(8,128)(2,1)}, u32[]{:S(2)}) copy-start(bf16[1,1024,768]{2,1,0:T(8,128)(2,1)} %refs_2_.1) | copy-start | bytes 4718596
  78.7 25.0 %copy-start.3 = (bf16[1,1024,768]{2,1,0:T(8,128)(2,1)S(1)}, bf16[1,1024,768]{2,1,0:T(8,128)(2,1)}, u32[]{:S(2)}) copy-start(bf16[1,1024,768]{2,1,0:T(8,128)(2,1)} %refs_3_.3) | copy-start | bytes 4718596
  80.4 13.4 %collective-permute-start.21 = (bf16[64,1152]{1,0:T(8,128)(2,1)}, bf16[64,1152]{1,0:T(8,128)(2,1)}, u32[]{:S(2)}, u32[]{:S(2)}) collective-permute-start(bf16[64,1152]{1,0:T(8,128)(2,1)} %get-tuple-element.70.refs_1_), channel_id=1, source_target_pairs={{0,8},{1,9},{2,10},{3,11},{4,12},{5,13},{6,14},{7,15},{8,0},{9,1},... | collective-permute-start | bytes 442376 | tf_op jit(solution)/shard_map/ppermute | solution.py:515
  80.6 13.3 %collective-permute-start.27 = (bf16[64,1152]{1,0:T(8,128)(2,1)}, bf16[64,1152]{1,0:T(8,128)(2,1)}, u32[]{:S(2)}, u32[]{:S(2)}) collective-permute-start(bf16[64,1152]{1,0:T(8,128)(2,1)} %get-tuple-element.70.refs_1_), channel_id=1, source_target_pairs={{0,4},{1,5},{2,6},{3,7},{4,8},{5,9},{6,10},{7,11},{8,12},{9,13},{1... | collective-permute-start | bytes 442376 | tf_op jit(solution)/shard_map/ppermute | solution.py:515
  93.8 5.7 %collective-permute-start.31 = (bf16[64,1152]{1,0:T(8,128)(2,1)}, bf16[64,1152]{1,0:T(8,128)(2,1)S(1)}, u32[]{:S(2)}, u32[]{:S(2)}) collective-permute-start(bf16[64,1152]{1,0:T(8,128)(2,1)} %get-tuple-element.70.refs_1_), channel_id=1, source_target_pairs={{0,12},{1,13},{2,14},{3,15},{4,0},{5,1},{6,2},{7,3},{8,4},{9,5},{1... | collective-permute-start | bytes 442376 | tf_op jit(solution)/shard_map/ppermute | solution.py:515
  93.9 21.7 %collective-permute-start.23 = (bf16[64,1152]{1,0:T(8,128)(2,1)}, bf16[64,1152]{1,0:T(8,128)(2,1)S(1)}, u32[]{:S(2)}, u32[]{:S(2)}) collective-permute-start(bf16[64,1152]{1,0:T(8,128)(2,1)} %get-tuple-element.70.refs_1_), channel_id=1, source_target_pairs={{0,2},{1,3},{2,0},{3,1},{4,6},{5,7},{6,4},{7,5},{8,10},{9,11},{10,... | collective-permute-start | bytes 442376 | tf_op jit(solution)/shard_map/ppermute | solution.py:515
  99.5 16.0 %collective-permute-start.22 = (bf16[64,1152]{1,0:T(8,128)(2,1)}, bf16[64,1152]{1,0:T(8,128)(2,1)S(1)}, u32[]{:S(2)}, u32[]{:S(2)}) collective-permute-start(bf16[64,1152]{1,0:T(8,128)(2,1)} %collective-permute-done.21.refs_1_), channel_id=1, source_target_pairs={{0,2},{1,3},{2,0},{3,1},{4,6},{5,7},{6,4},{7,5},{8,10},{9,11},{10,... | collective-permute-start | bytes 442376 | tf_op jit(solution)/shard_map/ppermute | solution.py:515
  101.6 19.0 %collective-permute-start.28 = (bf16[64,1152]{1,0:T(8,128)(2,1)}, bf16[64,1152]{1,0:T(8,128)(2,1)S(1)}, u32[]{:S(2)}, u32[]{:S(2)}) collective-permute-start(bf16[64,1152]{1,0:T(8,128)(2,1)} %collective-permute-done.27.refs_1_), channel_id=1, source_target_pairs={{0,2},{1,3},{2,0},{3,1},{4,6},{5,7},{6,4},{7,5},{8,10},{9,11},{10,... | collective-permute-start | bytes 442376 | tf_op jit(solution)/shard_map/ppermute | solution.py:515
  101.6 21.6 %collective-permute-start.32 = (bf16[64,1152]{1,0:T(8,128)(2,1)S(1)}, bf16[64,1152]{1,0:T(8,128)(2,1)S(1)}, u32[]{:S(2)}, u32[]{:S(2)}) collective-permute-start(bf16[64,1152]{1,0:T(8,128)(2,1)S(1)} %collective-permute-done.31.refs_1_), channel_id=1, source_target_pairs={{0,2},{1,3},{2,0},{3,1},{4,6},{5,7},{6,4},{7,5},{8,10},{9,11},{10,... | collective-permute-start | bytes 442376 | tf_op jit(solution)/shard_map/ppermute | solution.py:515
  103.7 1.4 %copy-start.4 = (bf16[1,768,1024]{2,1,0:T(8,128)(2,1)S(1)}, bf16[1,768,1024]{2,1,0:T(8,128)(2,1)}, u32[]{:S(2)}) copy-start(bf16[1,768,1024]{2,1,0:T(8,128)(2,1)} %refs_4_.3) | copy-start | bytes 4718596
  118.6 8.4 %collective-permute-start.25 = (bf16[64,1024]{1,0:T(8,128)(2,1)S(1)}, bf16[64,1024]{1,0:T(8,128)(2,1)S(1)}, u32[]{:S(2)}, u32[]{:S(2)}) collective-permute-start(bf16[64,1024]{1,0:T(8,128)(2,1)S(1)} %get-tuple-element.80), channel_id=1, source_target_pairs={{0,2},{1,3},{2,0},{3,1},{4,6},{5,7},{6,4},{7,5},{8,10},{9,11},{10,... | collective-permute-start | bytes 393224 | tf_op jit(solution)/shard_map/ppermute | solution.py:515
  118.7 13.9 %collective-permute-start.24 = (bf16[64,1024]{1,0:T(8,128)(2,1)S(1)}, bf16[64,1024]{1,0:T(8,128)(2,1)S(1)}, u32[]{:S(2)}, u32[]{:S(2)}) collective-permute-start(bf16[64,1024]{1,0:T(8,128)(2,1)S(1)} %get-tuple-element.78), channel_id=1, source_target_pairs={{0,2},{1,3},{2,0},{3,1},{4,6},{5,7},{6,4},{7,5},{8,10},{9,11},{10,... | collective-permute-start | bytes 393224 | tf_op jit(solution)/shard_map/ppermute | solution.py:515
  123.1 8.2 %collective-permute-start.29 = (bf16[64,1024]{1,0:T(8,128)(2,1)S(1)}, bf16[64,1024]{1,0:T(8,128)(2,1)S(1)}, u32[]{:S(2)}, u32[]{:S(2)}) collective-permute-start(bf16[64,1024]{1,0:T(8,128)(2,1)S(1)} %get-tuple-element.82), channel_id=1, source_target_pairs={{0,2},{1,3},{2,0},{3,1},{4,6},{5,7},{6,4},{7,5},{8,10},{9,11},{10,... | collective-permute-start | bytes 393224 | tf_op jit(solution)/shard_map/ppermute | solution.py:515
  125.4 8.3 %collective-permute-start.33 = (bf16[64,1024]{1,0:T(8,128)(2,1)S(1)}, bf16[64,1024]{1,0:T(8,128)(2,1)S(1)}, u32[]{:S(2)}, u32[]{:S(2)}) collective-permute-start(bf16[64,1024]{1,0:T(8,128)(2,1)S(1)} %get-tuple-element.83), channel_id=1, source_target_pairs={{0,4},{1,5},{2,6},{3,7},{4,8},{5,9},{6,10},{7,11},{8,12},{9,13},{1... | collective-permute-start | bytes 393224 | tf_op jit(solution)/shard_map/ppermute | solution.py:515
  125.5 11.7 %collective-permute-start.34 = (bf16[64,1024]{1,0:T(8,128)(2,1)S(1)}, bf16[64,1024]{1,0:T(8,128)(2,1)S(1)}, u32[]{:S(2)}, u32[]{:S(2)}) collective-permute-start(bf16[64,1024]{1,0:T(8,128)(2,1)S(1)} %get-tuple-element.84), channel_id=1, source_target_pairs={{0,6},{1,7},{2,4},{3,5},{4,10},{5,11},{6,8},{7,9},{8,14},{9,15},{1... | collective-permute-start | bytes 393224 | tf_op jit(solution)/shard_map/ppermute | solution.py:515
  127.0 12.0 %collective-permute-start.26 = (bf16[64,1024]{1,0:T(8,128)(2,1)S(1)}, bf16[64,1024]{1,0:T(8,128)(2,1)S(1)}, u32[]{:S(2)}, u32[]{:S(2)}) collective-permute-start(bf16[64,1024]{1,0:T(8,128)(2,1)S(1)} %add_convert_fusion.2), channel_id=1, source_target_pairs={{0,8},{1,9},{2,10},{3,11},{4,12},{5,13},{6,14},{7,15},{8,0},{9,1},... | collective-permute-start | bytes 393224 | tf_op jit(solution)/shard_map/ppermute | solution.py:515
  131.4 7.6 %collective-permute-start.30 = (bf16[64,1024]{1,0:T(8,128)(2,1)S(1)}, bf16[64,1024]{1,0:T(8,128)(2,1)S(1)}, u32[]{:S(2)}, u32[]{:S(2)}) collective-permute-start(bf16[64,1024]{1,0:T(8,128)(2,1)S(1)} %add_convert_fusion.1), channel_id=1, source_target_pairs={{0,12},{1,13},{2,14},{3,15},{4,0},{5,1},{6,2},{7,3},{8,4},{9,5},{1... | collective-permute-start | bytes 393224 | tf_op jit(solution)/shard_map/ppermute | solution.py:515
